TPU v7x, 32 devices: a whole 2x2x4 slice. The times are simulated.
32 devices in a mesh: dom: 8 (over z, y), edge: 4 (over x, core).
Axes of the slice: x: 2, y: 2, z: 4, core: 2. Of those that a mesh axis runs over, the one named last changes fastest.
Arguments:
- fine_nodes: bfloat16 [65536, 128], P('dom'), may hold values from -6 to 6
- fine_edges: bfloat16 [131072, 128], P(('dom', 'edge')), may hold values from -6 to 6
- fine_senders: int32 [131072], P(('dom', 'edge')), may hold values from 0 to 8703, as said below
- fine_receivers: int32 [131072], P(('dom', 'edge')), may hold values from 0 to 8191
- fine_halo: int32 [8, 8, 64], P('dom'), may hold values from 0 to 8191
- coarse_edges: bfloat16 [32768, 128], P(('dom', 'edge')), may hold values from -6 to 6
- coarse_senders: int32 [32768], P(('dom', 'edge')), may hold values from 0 to 2303, as said below
- coarse_receivers: int32 [32768], P(('dom', 'edge')), may hold values from 0 to 2047
- coarse_halo: int32 [8, 8, 32], P('dom'), may hold values from 0 to 2047
- pool_send: int32 [8, 8, 1536], P('dom'), may hold values from 0 to 8191, as said below
- pool_dest: int32 [8, 8, 1536], P('dom'), may hold values from 0 to 2048, as said below
- unpool_slot: int32 [65536], P('dom'), may hold values from 0 to 12287, as said below
- edge_in_weight: bfloat16 [2, 384, 128], replicated, may hold values from -0.3125 to 0.3125
- edge_out_weight: bfloat16 [2, 128, 128], replicated, may hold values from -0.5 to 0.5
- node_in_weight: bfloat16 [2, 256, 128], replicated, may hold values from -0.375 to 0.375
- node_out_weight: bfloat16 [2, 128, 128], replicated, may hold values from -0.5 to 0.5
- edge_gain: float32 [2, 128], replicated, may hold values from 0.5 to 1.5
- node_gain: float32 [2, 128], replicated, may hold values from 0.5 to 1.5
Outputs:
- fine_out: bfloat16 [65536, 128], P('dom')
- coarse_out: bfloat16 [16384, 128], P('dom')
Inputs may be any that keep to these rules, and one draw needn't show every extreme that they name: `fine_senders`: an entry below 8192 is a row of the edge's own partition; an entry 8192 + d * 64 + s names slot s of fine_halo[d, p] for the edge's partition p. `coarse_senders`: an entry below 2048 is a row of the edge's own coarse partition; an entry 2048 + d * 32 + s names slot s of coarse_halo[d, p]. pool_send[d, p, s] is a row of partition d. For each pair (d, p) the slots that carry data come first and number at most 1536; in every draw some p receives 1536 from every d. Every row of partition d is carried exactly once over all p and s; empty slots hold 0. pool_dest[p, d, s] is 2048 exactly where slot s of pool_send[d, p] is empty, else a row of coarse partition p. `unpool_slot`: row r of partition d holds p * 1536 + s for the one carrying slot with pool_send[d, p, s] = r.
All inputs are finite; a program needn't handle non-finite values.
Results may differ from a plain program's by a relative error of at most 0.0068.
Values may be sent and summed in bfloat16 or wider, within the bound.
No kernel may reach another device: no remote copies, remote signals or barrier semaphores. Data moves between devices by JAX's collectives and lax.ppermute only.
A program may use at most 64 MiB of HBM per device.

v0:
```python
import jax
import jax.numpy as jnp
from jax import lax
from jax.sharding import PartitionSpec as P

COARSE = 2048


def layer_norm(values, gain):
    center = values - jnp.mean(values, axis=-1, keepdims=True)
    spread = jnp.mean(center * center, axis=-1, keepdims=True)
    return center * lax.rsqrt(spread + 1e-05) * gain


def node_update(rows, summed, w_first, w_second, gain):
    inputs = jnp.concatenate([rows, summed.astype(jnp.bfloat16)], axis=1)
    hidden = jax.nn.silu(jnp.dot(inputs, w_first, preferred_element_type=jnp.float32)).astype(
        jnp.bfloat16
    )
    result = layer_norm(jnp.dot(hidden, w_second, preferred_element_type=jnp.float32), gain)
    return (rows.astype(jnp.float32) + result).astype(jnp.bfloat16)


def graph_layer(nodes, edges, senders, receivers, border, level, weights):
    edge_in_weight, edge_out_weight, node_in_weight, node_out_weight, edge_gain, node_gain = weights
    width = nodes.shape[-1]
    outgoing = nodes[border[0]]
    ghosts = lax.all_to_all(outgoing, "dom", split_axis=0, concat_axis=0, tiled=True)
    table = jnp.concatenate([nodes, ghosts.reshape(-1, width)], axis=0)
    inputs = jnp.concatenate([table[senders], nodes[receivers], edges], axis=1)
    hidden = jax.nn.silu(
        jnp.dot(inputs, edge_in_weight[level], preferred_element_type=jnp.float32)
    ).astype(jnp.bfloat16)
    message = layer_norm(
        jnp.dot(hidden, edge_out_weight[level], preferred_element_type=jnp.float32),
        edge_gain[level],
    )
    partial_sum = jax.ops.segment_sum(message, receivers, num_segments=nodes.shape[0])
    summed = lax.psum(partial_sum, "edge")
    return node_update(
        nodes, summed, node_in_weight[level], node_out_weight[level], node_gain[level]
    )


def pooled_mean(arrived, places, width):
    sums = jax.ops.segment_sum(
        arrived.reshape(-1, width).astype(jnp.float32), places, num_segments=COARSE + 1
    )[:COARSE]
    counts = jax.ops.segment_sum(jnp.ones_like(places), places, num_segments=COARSE + 1)[:COARSE]
    return (sums / jnp.maximum(counts, 1).astype(jnp.float32)[:, None]).astype(jnp.bfloat16)


def shards(
    fine_nodes,
    fine_edges,
    fine_senders,
    fine_receivers,
    fine_halo,
    coarse_edges,
    coarse_senders,
    coarse_receivers,
    coarse_halo,
    pool_send,
    pool_dest,
    unpool_slot,
    edge_in_weight,
    edge_out_weight,
    node_in_weight,
    node_out_weight,
    edge_gain,
    node_gain,
):
    weights = (
        edge_in_weight,
        edge_out_weight,
        node_in_weight,
        node_out_weight,
        edge_gain,
        node_gain,
    )
    width = fine_nodes.shape[-1]
    fine_mid = graph_layer(
        fine_nodes, fine_edges, fine_senders, fine_receivers, fine_halo, 0, weights
    )
    places = pool_dest[0].reshape(-1)
    arrived = lax.all_to_all(fine_mid[pool_send[0]], "dom", split_axis=0, concat_axis=0, tiled=True)
    coarse_in = pooled_mean(arrived, places, width)
    coarse_out = graph_layer(
        coarse_in, coarse_edges, coarse_senders, coarse_receivers, coarse_halo, 1, weights
    )
    padded = jnp.concatenate([coarse_out, jnp.zeros((1, width), jnp.bfloat16)], axis=0)
    back = lax.all_to_all(padded[pool_dest[0]], "dom", split_axis=0, concat_axis=0, tiled=True)
    parents = back.reshape(-1, width)[unpool_slot]
    fine_out = (fine_mid.astype(jnp.float32) + parents.astype(jnp.float32)).astype(jnp.bfloat16)
    return (fine_out, coarse_out)


def solution(mesh):
    placed = (
        P("dom", None),
        P(("dom", "edge"), None),
        P(("dom", "edge")),
        P(("dom", "edge")),
        P("dom", None, None),
        P(("dom", "edge"), None),
        P(("dom", "edge")),
        P(("dom", "edge")),
        P("dom", None, None),
        P("dom", None, None),
        P("dom", None, None),
        P("dom"),
        P(),
        P(),
        P(),
        P(),
        P(),
        P(),
    )
    return jax.shard_map(
        shards,
        mesh=mesh,
        in_specs=placed,
        out_specs=(P("dom", None), P("dom", None)),
        check_vma=False,
    )
```

profile of v0, /device:TPU:0, one launch (start us, length us, event | category | flops | bytes accessed | tf_op | source)
XLA Modules:
  0.0 602.7 jit_solution(17450261135767377777)
XLA Ops:
  0.6 0.7 compare_select_fusion.8
  1.3 0.1 reshape.183
  1.4 3.5 gather_fusion
  4.9 7.3 %all-to-all-start = ((bf16[8,64,128]{2,1,0:T(8,128)(2,1)}), bf16[8,64,128]{2,1,0:T(8,128)(2,1)S(1)}, u32[]{:S(2)}, u32[]{:S(2)}) async-start(bf16[8,64,128]{2,1,0:T(8,128)(2,1)} %bitcast.1), calls=%async_computation | async-start | bytes 262144 | tf_op jit(solution)/shard_map/all_to_all | solution.py:28
  12.2 0.7 fusion.77
  13.0 0.8 slice_bitcast_fusion.1
  13.7 1.0 compare_select_fusion.1
  14.7 0.8 slice_bitcast_fusion
  15.5 4.1 copy.24
  19.5 0.0 copy-done
  19.5 12.1 %gather_fusion.2 = bf16[4096,128]{1,0:T(8,128)(2,1)S(1)} fusion(bf16[8192,128]{1,0:T(8,128)(2,1)S(1)} %copy-done, s32[4096]{0:T(1024)S(1)} %fusion.77), kind=kCustom, calls=%fused_computation.2 | custom fusion | bytes 2113536 | tf_op jit(solution)/shard_map/gather | solution.py:30
  31.7 0.0 copy-done.8
  31.7 0.0 all-to-all-done
  31.7 5.6 pad_maximum_fusion
  37.3 16.2 %gather_fusion.1 = bf16[4096,128]{1,0:T(8,128)(2,1)} fusion(bf16[8704,128]{1,0:T(8,128)(2,1)} %pad_maximum_fusion, s32[4096]{0:T(1024)S(1)} %fusion.76), kind=kCustom, calls=%fused_computation.1 | custom fusion | bytes 2113536 | tf_op jit(solution)/shard_map/gather | solution.py:30
  53.5 0.0 copy-done.15
  53.5 4.3 fusion.95
  57.8 2.0 multiply_reduce_fusion.1
  59.8 0.2 copy-done.4
  60.0 1.7 multiply_multiply_fusion
  61.7 2.9 copy.25
  64.6 24.8 %scatter_custom_fusion = f32[8192,128]{1,0:T(8,128)} fusion(s32[4096]{0:T(1024)} %param.21, f32[4096,128]{1,0:T(8,128)} %copy.25, f32[]{:T(128)} %constant.13.clone.1), kind=kCustom, calls=%fused_computation.33 | custom fusion | flops 524288 | bytes 4194816 | tf_op jit(solution)/shard_map/scatter-add | solution.py:38
  89.4 77.1 %all-reduce.3 = bf16[8192,128]{1,0:T(8,128)(2,1)} all-reduce(f32[8192,128]{1,0:T(8,128)} %scatter_custom_fusion), channel_id=1, replica_groups=mesh['dom'=8,'edge'=4] {'edge'}, use_global_device_ids=true, to_apply=%region_3.4 | all-reduce | flops 1048576 | bytes 6291456 | tf_op jit(solution)/shard_map/psum | solution.py:39
  166.5 5.8 fusion.100
  172.3 2.8 multiply_reduce_fusion
  175.1 0.6 copy-done.2
  175.7 3.8 add_convert_fusion.1
  179.5 3.2 copy.26
  182.7 43.3 %gather_fusion.3 = bf16[12288,128]{1,0:T(8,128)(2,1)} fusion(bf16[8192,128]{1,0:T(8,128)(2,1)S(1)} %copy.26, s32[12288]{0:T(1024)S(1)} %broadcast_clamp_fusion.1), kind=kCustom, calls=%fused_computation.3 | custom fusion | bytes 6340608 | tf_op jit(solution)/shard_map/gather | solution.py:86
  226.0 5.5 all-to-all-start.1
  231.6 0.1 reshape.215
  231.7 65.0 %scatter_custom_fusion.2 = s32[2049]{0:T(1024)S(1)} fusion(s32[12288]{0:T(1024)S(1)} %reshape.263, s32[12288]{0:T(1024)S(1)} %broadcast.163, s32[]{:T(128)} %constant.14.clone.1), kind=kCustom, calls=%fused_computation.101 | custom fusion | flops 12288 | bytes 8200 | tf_op jit(solution)/shard_map/scatter-add | solution.py:49
  296.7 0.0 copy-done.10
  296.8 6.4 %all-to-all-done.1 = bf16[8,1536,128]{2,1,0:T(8,128)(2,1)S(1)} async-done(((bf16[8,1536,128]{2,1,0:T(8,128)(2,1)}), bf16[8,1536,128]{2,1,0:T(8,128)(2,1)S(1)}, u32[]{:S(2)}, u32[]{:S(2)}) %all-to-all-start.1) | async-done | bytes 3145760 | tf_op jit(solution)/shard_map/all_to_all | solution.py:86
  303.2 67.0 %scatter_custom_fusion.1 = f32[2049,128]{1,0:T(8,128)} fusion(s32[12288]{0:T(1024)S(1)} %reshape.263, bf16[12288,128]{1,0:T(8,128)(2,1)S(1)} %bitcast.78, f32[]{:T(128)} %constant.13.clone.1), kind=kCustom, calls=%fused_computation.13 | custom fusion | flops 3145728 | bytes 4194820 | tf_op jit(solution)/shard_map/scatter-add | solution.py:46
  370.2 1.6 fusion.24
  371.7 1.5 gather_fusion.4
  373.2 23.5 %all-to-all-start.2 = ((bf16[8,32,128]{2,1,0:T(8,128)(2,1)}), bf16[8,32,128]{2,1,0:T(8,128)(2,1)S(1)}, u32[]{:S(2)}, u32[]{:S(2)}) async-start(bf16[8,32,128]{2,1,0:T(8,128)(2,1)} %bitcast.13), calls=%async_computation.2 | async-start | bytes 131072 | tf_op jit(solution)/shard_map/all_to_all | solution.py:28
  396.7 0.0 copy-done.11
  396.7 3.2 gather_fusion.6
  399.9 0.0 copy-start.12
  400.0 0.0 copy-start.13
  400.0 0.0 copy-start.16
  400.0 3.6 all-to-all-done.2
  403.7 3.2 gather_fusion.5
  406.9 0.6 fusion.105
  407.5 0.1 multiply_reduce_fusion.3
  407.6 0.1 multiply_multiply_fusion.1
  407.7 0.0 copy-start.18
  407.7 0.2 copy.27
  407.9 6.3 %scatter_custom_fusion.3 = f32[2048,128]{1,0:T(8,128)S(1)} fusion(s32[1024]{0:T(1024)S(1)} %copy-done.11, f32[1024,128]{1,0:T(8,128)S(1)} %copy.27, f32[]{:T(128)} %constant.13.clone.1), kind=kCustom, calls=%fused_computation.61 | custom fusion | flops 131072 | bytes 1048580 | tf_op jit(solution)/shard_map/scatter-add | solution.py:38
  414.2 25.8 %all-reduce.4 = bf16[2048,128]{1,0:T(8,128)(2,1)S(1)} all-reduce(f32[2048,128]{1,0:T(8,128)S(1)} %scatter_custom_fusion.3), channel_id=1, replica_groups=mesh['dom'=8,'edge'=4] {'edge'}, use_global_device_ids=true, to_apply=%region_11.12 | all-reduce | flops 262144 | bytes 1572864 | tf_op jit(solution)/shard_map/psum | solution.py:39
  440.0 0.9 fusion.110
  440.9 0.6 multiply_reduce_fusion.2
  441.5 1.0 add_convert_fusion.2
  442.5 0.0 copy-start.5
  442.6 0.8 copy-done.5
  443.4 43.3 %gather_fusion.7 = bf16[12288,128]{1,0:T(8,128)(2,1)} fusion(bf16[2049,128]{1,0:T(8,128)(2,1)S(1)} %concatenate.27, s32[12288]{0:T(1024)S(1)} %broadcast_clamp_fusion), kind=kCustom, calls=%fused_computation.7 | custom fusion | bytes 6340608 | tf_op jit(solution)/shard_map/gather | solution.py:92
  486.7 3.8 all-to-all-start.3
  490.5 71.3 %all-to-all-done.3 = bf16[8,1536,128]{2,1,0:T(8,128)(2,1)S(1)} async-done(((bf16[8,1536,128]{2,1,0:T(8,128)(2,1)}), bf16[8,1536,128]{2,1,0:T(8,128)(2,1)S(1)}, u32[]{:S(2)}, u32[]{:S(2)}) %all-to-all-start.3) | async-done | bytes 3145760 | tf_op jit(solution)/shard_map/all_to_all | solution.py:92
  561.8 29.2 %gather_fusion.8 = bf16[8192,128]{1,0:T(8,128)(2,1)} fusion(bf16[12288,128]{1,0:T(8,128)(2,1)S(1)} %bitcast.77, s32[8192]{0:T(1024)S(1)} %fusion.67), kind=kCustom, calls=%fused_computation.8 | custom fusion | bytes 4227072 | tf_op jit(solution)/shard_map/gather | solution.py:93
  591.0 4.2 copy.28
  595.3 3.4 add_convert_fusion
  598.7 4.1 copy.29
  (50 shorter events, 0.3 us)
Async XLA Ops:
  4.9 26.8 %all-to-all-start = ((bf16[8,64,128]{2,1,0:T(8,128)(2,1)}), bf16[8,64,128]{2,1,0:T(8,128)(2,1)S(1)}, u32[]{:S(2)}, u32[]{:S(2)}) async-start(bf16[8,64,128]{2,1,0:T(8,128)(2,1)} %bitcast.1), calls=%async_computation | async-start | bytes 262144 | tf_op jit(solution)/shard_map/all_to_all | solution.py:28
  13.7 5.8 copy-start
  19.5 12.1 %copy-start.8 = (s32[4096]{0:T(1024)S(1)}, s32[4096]{0:T(1024)}, u32[]{:S(2)}) copy-start(s32[4096]{0:T(1024)} %param.20) | copy-start | bytes 49156
  37.3 16.2 %copy-start.15 = (bf16[2,128,128]{2,1,0:T(8,128)(2,1)S(1)}, bf16[2,128,128]{2,1,0:T(8,128)(2,1)}, u32[]{:S(2)}) copy-start(bf16[2,128,128]{2,1,0:T(8,128)(2,1)} %param.31) | copy-start | bytes 196612
  57.8 2.2 copy-start.4
  89.4 77.1 %copy-start.14 = (bf16[2,256,128]{2,1,0:T(8,128)(2,1)S(1)}, bf16[2,256,128]{2,1,0:T(8,128)(2,1)}, u32[]{:S(2)}) copy-start(bf16[2,256,128]{2,1,0:T(8,128)(2,1)} %param.32) | copy-start | bytes 393220
  89.4 77.1 %copy-start.17 = (bf16[2,128,128]{2,1,0:T(8,128)(2,1)S(1)}, bf16[2,128,128]{2,1,0:T(8,128)(2,1)}, u32[]{:S(2)}) copy-start(bf16[2,128,128]{2,1,0:T(8,128)(2,1)} %param.33) | copy-start | bytes 196612
  172.3 3.4 copy-start.2
  226.0 5.5 copy-start.6
  226.0 5.6 copy-start.9
  226.0 70.7 %copy-start.10 = (s32[1024]{0:T(1024)S(1)}, s32[1024]{0:T(1024)}, u32[]{:S(2)}) copy-start(s32[1024]{0:T(1024)} %param.24) | copy-start | bytes 12292
  226.0 77.1 %all-to-all-start.1 = ((bf16[8,1536,128]{2,1,0:T(8,128)(2,1)}), bf16[8,1536,128]{2,1,0:T(8,128)(2,1)S(1)}, u32[]{:S(2)}, u32[]{:S(2)}) async-start(bf16[8,1536,128]{2,1,0:T(8,128)(2,1)} %bitcast.79), calls=%async_computation.1 | async-start | bytes 6291456 | tf_op jit(solution)/shard_map/all_to_all | solution.py:86
  303.2 93.5 %copy-start.11 = (s32[1024]{0:T(1024)S(1)}, s32[1024]{0:T(1024)}, u32[]{:S(2)}) copy-start(s32[1024]{0:T(1024)} %param.25) | copy-start | bytes 12292
  373.2 30.4 %all-to-all-start.2 = ((bf16[8,32,128]{2,1,0:T(8,128)(2,1)}), bf16[8,32,128]{2,1,0:T(8,128)(2,1)S(1)}, u32[]{:S(2)}, u32[]{:S(2)}) async-start(bf16[8,32,128]{2,1,0:T(8,128)(2,1)} %bitcast.13), calls=%async_computation.2 | async-start | bytes 131072 | tf_op jit(solution)/shard_map/all_to_all | solution.py:28
  399.9 6.9 %copy-start.12 = (bf16[1024,128]{1,0:T(8,128)(2,1)S(1)}, bf16[1024,128]{1,0:T(8,128)(2,1)}, u32[]{:S(2)}) copy-start(bf16[1024,128]{1,0:T(8,128)(2,1)} %param.23) | copy-start | bytes 786436
  400.0 6.9 %copy-start.13 = (bf16[2,384,128]{2,1,0:T(8,128)(2,1)S(1)}, bf16[2,384,128]{2,1,0:T(8,128)(2,1)}, u32[]{:S(2)}) copy-start(bf16[2,384,128]{2,1,0:T(8,128)(2,1)} %param.30) | copy-start | bytes 589828
  400.0 6.9 %copy-start.16 = (bf16[2,128,128]{2,1,0:T(8,128)(2,1)S(1)}, bf16[2,128,128]{2,1,0:T(8,128)(2,1)}, u32[]{:S(2)}) copy-start(bf16[2,128,128]{2,1,0:T(8,128)(2,1)} %param.31) | copy-start | bytes 196612
  407.7 32.3 %copy-start.18 = (bf16[2,128,128]{2,1,0:T(8,128)(2,1)S(1)}, bf16[2,128,128]{2,1,0:T(8,128)(2,1)}, u32[]{:S(2)}) copy-start(bf16[2,128,128]{2,1,0:T(8,128)(2,1)} %param.33) | copy-start | bytes 196612
  440.0 1.5 copy-start.3
  442.5 0.8 copy-start.5
  486.7 3.8 copy-start.7
  486.7 75.1 %all-to-all-start.3 = ((bf16[8,1536,128]{2,1,0:T(8,128)(2,1)}), bf16[8,1536,128]{2,1,0:T(8,128)(2,1)S(1)}, u32[]{:S(2)}, u32[]{:S(2)}) async-start(bf16[8,1536,128]{2,1,0:T(8,128)(2,1)} %bitcast.80), calls=%async_computation.3 | async-start | bytes 6291456 | tf_op jit(solution)/shard_map/all_to_all | solution.py:92
  591.0 4.2 copy-start.1
where the time goes:
time: 604 us; the launch traced here: 603 us
  other arithmetic  188 us (31%)
  local copies, waits for them, and re-layouts  178 us (29%)
  blocking collectives  103 us (17%)
  waiting for transfers between devices  81.4 us (13%)
  starting transfers between devices  40.1 us (7%)
  matrix products  11.6 us (2%)
    psum x2, blocking collectives, graph_layer(): summed = lax.psum(partial_sum, 'edge')  103 us
    all_to_all x1, waiting for transfers between devices, shards(): lax.all_to_all(padded[pool_dest[0]], 'dom', split_axis=0, concat_axis=0,...  71.3 us
    scatter-add x1, other arithmetic, pooled_mean(): jax.ops.segment_sum(arrived.reshape(-1, width).astype(jnp.float32), place...  67 us
    scatter-add x1, other arithmetic, pooled_mean(): jax.ops.segment_sum(jnp.ones_like(places), places, num_segments=COARSE + 1)  65 us
    gather x1, local copies, waits for them, and re-layouts, shards(): padded[pool_dest[0]]  43.3 us
    gather x1, local copies, waits for them, and re-layouts, shards(): fine_mid[pool_send[0]]  43.3 us
    gather x4, local copies, waits for them, and re-layouts, graph_layer(): inputs = jnp.concatenate([table[senders], nodes[receivers], edges], axis=1)  34.7 us
    gather x2, local copies, waits for them, and re-layouts, shards(): parents = back.reshape(-1, width)[unpool_slot]  33.5 us
  transfers between devices with their start and end apart: 4, of which 3 were waited for; matrix products, arithmetic and copies ran while one was open for 15% of the time, Pallas kernels for 0%

commit v1 on v0

v1 whole, which is shorter than its diff:
```python
import jax
import jax.numpy as jnp
from jax import lax
from jax.experimental import pallas as pl
from jax.experimental.pallas import tpu as pltpu
from jax.sharding import PartitionSpec as P

BF = jnp.bfloat16
F32 = jnp.float32
VMEM = pl.BlockSpec(memory_space=pltpu.VMEM)
SMEM = pl.BlockSpec(memory_space=pltpu.SMEM)
COARSE = 2048
UNROLL = 16
ACCS = 4


def call(kernel, out_shape, in_specs, scratch=(), name=None):
    outs = jax.tree.map(lambda _: VMEM, out_shape)
    return pl.pallas_call(
        kernel,
        out_shape=out_shape,
        in_specs=in_specs,
        out_specs=outs,
        scratch_shapes=list(scratch),
        name=name,
        compiler_params=pltpu.CompilerParams(vmem_limit_bytes=60 * 1024 * 1024),
    )


def shaped(rows, dtype, width=128):
    return jax.ShapeDtypeStruct((rows, width), dtype)


def dot(a, b):
    return jnp.dot(a, b, preferred_element_type=F32)


def silu(v):
    return v / (1.0 + jnp.exp(-v))


def norm(values, gain):
    center = values - jnp.mean(values, axis=-1, keepdims=True)
    spread = jnp.mean(center * center, axis=-1, keepdims=True)
    return center * lax.rsqrt(spread + 1e-05) * gain


def blocks(total, size, body):
    size = min(size, total)

    def step(i, carry):
        body(pl.multiple_of(i * size, size))
        return carry

    lax.fori_loop(0, total // size, step, 0)


def edge_gather(nodes, edges, near, receivers, w_in):
    rows, width = nodes.shape
    count = edges.shape[0]

    def kernel(near_ref, recv_ref, nodes_ref, edges_ref, w_ref, out_ref, send_tab, recv_tab):
        w_s = w_ref[0:width, :]
        w_r = w_ref[width : 2 * width, :]
        w_e = w_ref[2 * width : 3 * width, :]

        def project(at):
            block = nodes_ref[pl.ds(at, min(512, rows)), :]
            send_tab[pl.ds(at, min(512, rows)), :] = dot(block, w_s)
            recv_tab[pl.ds(at, min(512, rows)), :] = dot(block, w_r)

        blocks(rows, 512, project)
        send_tab[pl.ds(rows, 8), :] = jnp.zeros((8, width), F32)

        def gather(i, carry):
            base = i * UNROLL
            for j in range(UNROLL):
                s = near_ref[base + j]
                r = recv_ref[base + j]
                out_ref[pl.ds(base + j, 1), :] = send_tab[pl.ds(s, 1), :] + recv_tab[pl.ds(r, 1), :]
            return carry

        lax.fori_loop(0, count // UNROLL, gather, 0)

        def add_edges(at):
            n = min(512, count)
            out_ref[pl.ds(at, n), :] = out_ref[pl.ds(at, n), :] + dot(edges_ref[pl.ds(at, n), :], w_e)

        blocks(count, 512, add_edges)

    return call(
        kernel,
        shaped(count, F32),
        [SMEM, SMEM, VMEM, VMEM, VMEM],
        [pltpu.VMEM((rows + 8, width), F32), pltpu.VMEM((rows, width), F32)],
        "edge_gather",
    )(near, receivers, nodes, edges, w_in)


def edge_message(pre, ghosts, far, receivers, table, w_in, w_out, gain, slots, mapped):
    count, width = pre.shape
    ghost_rows = ghosts.shape[0]
    half = slots // 2
    n = min(256, count)

    def kernel(recv_ref, table_ref, far_ref, pre_ref, ghost_ref, w_ref, wo_ref, gain_ref, keep_ref, send_ref, msg, *accs):
        def clear(at):
            for acc in accs:
                acc[pl.ds(at, 512), :] = jnp.zeros((512, width), F32)

        blocks(slots, 512, clear)
        w_s = w_ref[0:width, :]
        w_o = wo_ref[...]

        def message(at):
            pick = (far_ref[pl.ds(at, n), :] == lax.broadcasted_iota(jnp.int32, (n, ghost_rows), 1)).astype(BF)
            picked = dot(pick, ghost_ref[...]).astype(BF)
            hidden = silu(pre_ref[pl.ds(at, n), :] + dot(picked, w_s)).astype(BF)
            msg[pl.ds(at, n), :] = norm(dot(hidden, w_o), gain_ref[...])

        blocks(count, n, message)

        def scatter(i, carry):
            base = i * UNROLL
            for j in range(UNROLL):
                acc = accs[j % ACCS]
                r = recv_ref[base + j]
                if mapped:
                    r = table_ref[r]
                acc[pl.ds(r, 1), :] = acc[pl.ds(r, 1), :] + msg[pl.ds(base + j, 1), :]
            return carry

        lax.fori_loop(0, count // UNROLL, scatter, 0)

        def finish(at):
            m = min(512, half)
            low = accs[0][pl.ds(at, m), :]
            high = accs[0][pl.ds(at + half, m), :]
            for acc in accs[1:]:
                low = low + acc[pl.ds(at, m), :]
                high = high + acc[pl.ds(at + half, m), :]
            keep_ref[pl.ds(at, m), :] = low
            send_ref[pl.ds(at, m), :] = high.astype(BF)

        blocks(half, 512, finish)

    return call(
        kernel,
        (shaped(half, F32), shaped(half, BF)),
        [SMEM, SMEM] + [VMEM] * 6,
        [pltpu.VMEM((count, width), F32)] + [pltpu.VMEM((slots, width), F32)] * ACCS,
        "edge_message",
    )(receivers, table, far.reshape(count, 1), pre, ghosts, w_in, w_out, gain)


def node_update(rows, kept, first, second, w_in, w_out, gain):
    count, width = rows.shape
    n = min(256, count)

    def kernel(rows_ref, kept_ref, first_ref, second_ref, w_ref, wo_ref, gain_ref, out_ref):
        def step(at):
            own = rows_ref[pl.ds(at, n), :]
            total = (
                kept_ref[pl.ds(at, n), :]
                + first_ref[pl.ds(at, n), :].astype(F32)
                + second_ref[pl.ds(at, n), :].astype(F32)
            ).astype(BF)
            hidden = silu(dot(own, w_ref[0:width, :]) + dot(total, w_ref[width : 2 * width, :])).astype(BF)
            result = norm(dot(hidden, wo_ref[...]), gain_ref[...])
            out_ref[pl.ds(at, n), :] = (own.astype(F32) + result).astype(BF)

        blocks(count, n, step)

    return call(kernel, shaped(count, BF), [VMEM] * 7, (), "node_update")(
        rows, kept, first, second, w_in, w_out, gain
    )


def take_rows(table, index):
    rows, width = table.shape
    count = index.shape[0]

    def kernel(index_ref, table_ref, out_ref, wide, picked):
        def widen(at):
            wide[pl.ds(at, 256), :] = table_ref[pl.ds(at, 256), :].astype(F32)

        blocks(rows, 256, widen)

        def gather(i, carry):
            base = i * UNROLL
            for j in range(UNROLL):
                picked[pl.ds(base + j, 1), :] = wide[pl.ds(index_ref[base + j], 1), :]
            return carry

        lax.fori_loop(0, count // UNROLL, gather, 0)

        def narrow(at):
            out_ref[pl.ds(at, 256), :] = picked[pl.ds(at, 256), :].astype(BF)

        blocks(count, 256, narrow)

    return call(
        kernel,
        shaped(count, BF),
        [SMEM, VMEM],
        [pltpu.VMEM((rows, width), F32), pltpu.VMEM((count, width), F32)],
        "take_rows",
    )(index, table)


def pool_sum(arrived, places):
    count, width = arrived.shape
    n = 256

    def kernel(arrived_ref, places_ref, out_ref):
        rows = arrived_ref[...]

        def step(at):
            pick = (places_ref[...] == at + lax.broadcasted_iota(jnp.int32, (n, count), 0)).astype(BF)
            out_ref[pl.ds(at, n), :] = dot(pick, rows)

        blocks(COARSE, n, step)

    return call(kernel, shaped(COARSE, F32), [VMEM, VMEM], (), "pool_sum")(arrived, places.reshape(1, count))


def child_count(places):
    count = places.shape[0]
    high = (places // 128)[None, :] == jnp.arange(COARSE // 128, dtype=jnp.int32)[:, None]
    low = (places % 128)[:, None] == jnp.arange(128, dtype=jnp.int32)[None, :]
    return dot(high.astype(BF), low.astype(BF)).reshape(COARSE)


def swap(x, bit):
    size = lax.axis_size("edge")
    return lax.ppermute(x, "edge", [(i, i ^ bit) for i in range(size)])


def layer_sums(nodes, edges, senders, receivers, border, level, w, slots, table):
    rows, width = nodes.shape
    outgoing = nodes[border[0].reshape(-1)].reshape(border.shape[1], border.shape[2], width)
    arrived = lax.all_to_all(outgoing, "dom", split_axis=0, concat_axis=0, tiled=True)
    pre = edge_gather(nodes, edges, jnp.minimum(senders, rows), receivers, w[0][level])
    ghosts = arrived.reshape(-1, width)
    mapped = table is not None
    if mapped:
        index = receivers
    else:
        me = lax.axis_index("edge")
        quarter = rows // 4
        index = order_of((receivers // quarter) ^ me) * quarter + receivers % quarter
        table = index
    keep, send = edge_message(
        pre, ghosts, senders - rows, index, table, w[0][level], w[1][level], w[4][level][None], slots, mapped
    )
    first = swap(send, 1)
    half = slots // 4
    second = swap((keep[half:] + first[half:].astype(F32)).astype(BF), 2)
    return keep[:half], first[:half], second


def order_of(rel):
    return (rel & 1) * 2 + (rel >> 1)


def shards(
    fine_nodes,
    fine_edges,
    fine_senders,
    fine_receivers,
    fine_halo,
    coarse_edges,
    coarse_senders,
    coarse_receivers,
    coarse_halo,
    pool_send,
    pool_dest,
    unpool_slot,
    edge_in_weight,
    edge_out_weight,
    node_in_weight,
    node_out_weight,
    edge_gain,
    node_gain,
):
    w = (edge_in_weight, edge_out_weight, node_in_weight, node_out_weight, edge_gain, node_gain)
    width = fine_nodes.shape[-1]
    n_dom = pool_send.shape[1]
    span = pool_send.shape[2]
    part = span // 4
    slots = n_dom * span
    quarter = n_dom * part
    me = lax.axis_index("edge")
    target = unpool_slot // span
    within = unpool_slot % span
    slot_place = order_of((within // part) ^ me) * quarter + target * part + within % part
    my_send = lax.dynamic_slice_in_dim(pool_send[0], me * part, part, 1).reshape(-1)
    my_dest = lax.dynamic_slice_in_dim(pool_dest[0], me * part, part, 1).reshape(-1)
    counts = child_count(pool_dest[0].reshape(-1))
    scale = jnp.maximum(counts, 1.0)[:, None]

    kept, first, second = layer_sums(
        fine_nodes, fine_edges, fine_senders, fine_receivers, fine_halo, 0, w, slots, slot_place
    )
    own = take_rows(fine_nodes, my_send)
    mid = node_update(own, kept, first, second, w[2][0], w[3][0], w[5][0][None])

    arrived = lax.all_to_all(mid.reshape(n_dom, part, width), "dom", split_axis=0, concat_axis=0, tiled=True)
    sums = pool_sum(arrived.reshape(-1, width), my_dest)
    bit = me & 1
    half = COARSE // 2
    mine = lax.dynamic_slice_in_dim(sums, bit * half, half, 0)
    theirs = lax.dynamic_slice_in_dim(sums, (1 - bit) * half, half, 0)
    mine = mine + swap(theirs, 1)
    mine = mine + swap(mine.astype(BF), 2).astype(F32)
    mine = (mine / lax.dynamic_slice_in_dim(scale, bit * half, half, 0)).astype(BF)
    theirs = swap(mine, 1)
    coarse_in = jnp.concatenate([jnp.where(bit == 0, mine, theirs), jnp.where(bit == 0, theirs, mine)], axis=0)

    kept, first, second = layer_sums(
        coarse_in, coarse_edges, coarse_senders, coarse_receivers, coarse_halo, 1, w, COARSE, None
    )
    fourth = COARSE // 4
    own = lax.dynamic_slice_in_dim(coarse_in, me * fourth, fourth, 0)
    top = node_update(own, kept, first, second, w[2][1], w[3][1], w[5][1][None])
    coarse_out = lax.all_gather(top, "edge", axis=0, tiled=True)

    parents = take_rows(coarse_out, jnp.minimum(my_dest, COARSE - 1))
    back = lax.all_to_all(parents.reshape(n_dom, part, width), "dom", split_axis=0, concat_axis=0, tiled=True)
    final = (mid.astype(F32) + back.reshape(-1, width).astype(F32)).astype(BF)
    pair = jnp.concatenate([final, swap(final, 2)], axis=0)
    table = jnp.concatenate([pair, swap(pair, 1)], axis=0)
    fine_out = take_rows(table, slot_place)
    return (fine_out, coarse_out)


def solution(mesh):
    placed = (
        P("dom", None),
        P(("dom", "edge"), None),
        P(("dom", "edge")),
        P(("dom", "edge")),
        P("dom", None, None),
        P(("dom", "edge"), None),
        P(("dom", "edge")),
        P(("dom", "edge")),
        P("dom", None, None),
        P("dom", None, None),
        P("dom", None, None),
        P("dom"),
        P(),
        P(),
        P(),
        P(),
        P(),
        P(),
    )
    return jax.shard_map(
        shards,
        mesh=mesh,
        in_specs=placed,
        out_specs=(P("dom", None), P("dom", None)),
        check_vma=False,
    )
```

time: 604 us -> 269 us (0.45)
  other arithmetic: 188 us -> 28.2 us
  local copies, waits for them, and re-layouts: 178 us -> 23.3 us
  Pallas kernels: 0 us -> 94.8 us
  blocking collectives: 103 us -> 33.3 us
  waiting for transfers between devices: 81.4 us -> 63.4 us
  starting transfers between devices: 40.1 us -> 22.2 us
  matrix products: 11.6 us -> 1.8 us
    scatter-add x4 -> x0, other arithmetic: 163 us -> none  [the longest x1 67 us: pooled_mean(): jax.ops.segment_sum(arrived.reshape(-1, width).astype(jnp.float32), place...]
    gather x10 -> x2, local copies, waits for them, and re-layouts: 160 us -> 4.99 us  [layer_sums(): nodes[border[0].reshape(-1)]]
    psum x2 -> x0, blocking collectives: 103 us -> none  [graph_layer(): summed = lax.psum(partial_sum, 'edge')]
    pallas_call x0 -> x10, Pallas kernels: none -> 94.8 us  [the longest x2 31.9 us: edge_message(): call(kernel, (shaped(half, F32), shaped(half, BF)), [SMEM, SMEM] + [VMEM]...]
    all_to_all x4 -> x3, waiting for transfers between devices: 81.4 us -> 20.6 us  [the longest x1 19.1 us: shards(): lax.all_to_all(mid.reshape(n_dom, part, width), 'dom', split_axis=0, conc...]
    ppermute x0 -> x9, waiting for transfers between devices: none -> 42.8 us  [swap(): return lax.ppermute(x, 'edge', [(i, i ^ bit) for i in range(size)])]
    all_to_all x0 -> x1, blocking collectives: none -> 25.1 us  [shards(): lax.all_to_all(parents.reshape(n_dom, part, width), 'dom', split_axis=0,...]
    all_to_all x4 -> x3, starting transfers between devices: 40.1 us -> 16.8 us  [the longest x2 10.8 us: layer_sums(): lax.all_to_all(outgoing, 'dom', split_axis=0, concat_axis=0, tiled=True)]
  transfers between devices with their start and end apart: 4 -> 12, of which waited for: 3 -> 11; matrix products, arithmetic and copies ran while one was open for 15% -> 7% of each run, Pallas kernels for 0% -> 10%
where the time goes in v1:
time: 269 us; the launch traced here: 268 us
  Pallas kernels  94.8 us (35%)
  waiting for transfers between devices  63.4 us (24%)
  blocking collectives  33.3 us (12%)
  other arithmetic  28.2 us (10%)
  local copies, waits for them, and re-layouts  23.3 us (9%)
  starting transfers between devices  22.2 us (8%)
    ppermute x9, waiting for transfers between devices, swap(): return lax.ppermute(x, 'edge', [(i, i ^ bit) for i in range(size)])  42.8 us
    pallas_call x2, Pallas kernels, edge_message(): call(kernel, (shaped(half, F32), shaped(half, BF)), [SMEM, SMEM] + [VMEM]...  31.9 us
    all_to_all x1, blocking collectives, shards(): lax.all_to_all(parents.reshape(n_dom, part, width), 'dom', split_axis=0,...  25.1 us
    pallas_call x3, Pallas kernels, take_rows(): call(kernel, shaped(count, BF), [SMEM, VMEM], [pltpu.VMEM((rows, width),...  25 us
    pallas_call x2, Pallas kernels, edge_gather(): call(kernel, shaped(count, F32), [SMEM, SMEM, VMEM, VMEM, VMEM], [pltpu.V...  19.5 us
    all_to_all x1, waiting for transfers between devices, shards(): lax.all_to_all(mid.reshape(n_dom, part, width), 'dom', split_axis=0, conc...  19.1 us
    concatenate x1, other arithmetic, shards(): table = jnp.concatenate([pair, swap(pair, 1)], axis=0)  15.5 us
    pallas_call x2, Pallas kernels, node_update(): call(kernel, shaped(count, BF), [VMEM] * 7, (), 'node_update')  11.8 us
  transfers between devices with their start and end apart: 12, of which 11 were waited for; matrix products, arithmetic and copies ran while one was open for 7% of the time, Pallas kernels for 10%

profile of v1, /device:TPU:0, one launch (start us, length us, event | category | flops | bytes accessed | tf_op | source)
XLA Modules:
  0.0 267.8 jit_solution(17903914968232074729)
XLA Ops:
  0.6 0.8 reshape_squeeze.9
  1.4 3.5 %gather_fusion = bf16[512,128]{1,0:T(8,128)(2,1)} fusion(bf16[8192,128]{1,0:T(8,128)(2,1)} %nodes_ref.1, s32[1024]{0:T(1024)S(1)} %pad_clamp_fusion.1), kind=kCustom, calls=%fused_computation | custom fusion | bytes 264192 | tf_op jit(solution)/shard_map/gather | solution.py:241
  4.9 7.3 %all-to-all-start = ((bf16[8,64,128]{2,1,0:T(8,128)(2,1)}), bf16[8,64,128]{2,1,0:T(8,128)(2,1)S(1)}, u32[]{:S(2)}, u32[]{:S(2)}) async-start(bf16[8,64,128]{2,1,0:T(8,128)(2,1)} %bitcast.3), calls=%async_computation | async-start | bytes 262144 | tf_op jit(solution)/shard_map/all_to_all | solution.py:242
  12.2 1.6 slice_bitcast_fusion
  13.9 1.3 broadcast_minimum_fusion
  15.2 1.4 fusion.12.table_ref.index_ref
  16.6 1.3 fusion.23
  17.9 2.0 copy.20.far_ref
  19.9 14.7 %edge_gather.2.pre_ref = f32[4096,128]{1,0:T(8,128)} custom-call(s32[4096]{0:T(1024)} %get-tuple-element.28.near_ref, s32[4096]{0:T(1024)} %recv_ref.4, bf16[8192,128]{1,0:T(8,128)(2,1)} %nodes_ref.1, bf16[4096,128]{1,0:T(8,128)(2,1)} %edges_ref.2, bf16[384,128]{1,0:T(8,128)(2,1)} %get-tuple-element.17.w_ref), custom_call_target="tpu_custom_call" | custom-call | tf_op jit(solution)/shard_map/edge_gather/pallas_call | solution.py:91
  34.6 0.6 slice_bitcast_fusion.5
  35.2 0.7 copy-done.6
  35.9 25.2 %edge_message.2 = (f32[6144,128]{1,0:T(8,128)}, bf16[6144,128]{1,0:T(8,128)(2,1)}) custom-call(s32[4096]{0:T(1024)} %recv_ref.4, s32[8192]{0:T(1024)} %fusion.12.table_ref.index_ref, s32[4096,1]{1,0:T(8,128)} %copy.20.far_ref, f32[4096,128]{1,0:T(8,128)} %edge_gather.2.pre_ref, bf16[512,128]{1,0:T(8,128)(2,1)} %bitcast.38, ...), custom_call_target="tpu_custom_call" | custom-call | tf_op jit(solution)/shard_map/edge_message/pallas_call | solution.py:147
  61.0 3.6 %collective-permute-done = bf16[6144,128]{1,0:T(8,128)(2,1)S(1)} collective-permute-done((bf16[6144,128]{1,0:T(8,128)(2,1)}, bf16[6144,128]{1,0:T(8,128)(2,1)S(1)}, u32[]{:S(2)}, u32[]{:S(2)}) %collective-permute-start) | collective-permute-done | bytes 1572896 | tf_op jit(solution)/shard_map/ppermute | solution.py:236
  64.6 3.3 %add_convert_fusion = (bf16[3072,128]{1,0:T(8,128)(2,1)S(1)}, f32[3072,128]{1,0:T(8,128)}) fusion(f32[6144,128]{1,0:T(8,128)} %get-tuple-element.6, bf16[6144,128]{1,0:T(8,128)(2,1)S(1)} %collective-permute-done), kind=kLoop, calls=%fused_computation.9 | loop fusion | flops 1179648 | bytes 6291456 | tf_op jit(solution)/shard_map/convert_element_type | solution.py:258
  67.9 1.5 collective-permute-start.1
  69.4 0.7 dynamic-slice_bitcast_fusion
  70.1 0.6 reshape.155.index_ref
  70.7 6.3 %take_rows.3.rows_ref = bf16[3072,128]{1,0:T(8,128)(2,1)} custom-call(s32[3072]{0:T(1024)} %reshape.155.index_ref, bf16[8192,128]{1,0:T(8,128)(2,1)} %nodes_ref.1), custom_call_target="tpu_custom_call" | custom-call | tf_op jit(solution)/shard_map/take_rows/pallas_call | solution.py:202
  77.1 0.5 fusion.22
  77.6 0.6 slice_bitcast_fusion.4
  78.3 0.7 slice_bitcast_fusion.2
  78.9 1.0 slice.86.first_ref
  79.9 7.6 %collective-permute-done.1.second_ref = bf16[3072,128]{1,0:T(8,128)(2,1)S(1)} collective-permute-done((bf16[3072,128]{1,0:T(8,128)(2,1)S(1)}, bf16[3072,128]{1,0:T(8,128)(2,1)S(1)}, u32[]{:S(2)}, u32[]{:S(2)}) %collective-permute-start.1) | collective-permute-done | bytes 786464 | tf_op jit(solution)/shard_map/ppermute | solution.py:236
  87.5 0.9 copy-done.5
  88.4 8.9 %node_update.2 = bf16[3072,128]{1,0:T(8,128)(2,1)} custom-call(bf16[3072,128]{1,0:T(8,128)(2,1)} %take_rows.3.rows_ref, f32[3072,128]{1,0:T(8,128)} %get-tuple-element.11.kept_ref, bf16[3072,128]{1,0:T(8,128)(2,1)} %slice.86.first_ref, bf16[3072,128]{1,0:T(8,128)(2,1)} %copy-done.5, bf16[256,128]{1,0:T(8,128)(2,1)} %get-tuple-element.19.w_ref, ...), custom_call_target="tpu_custom_call" | custom-call | tf_op jit(solution)/shard_map/node_update/pallas_call | solution.py:174
  97.3 6.0 %all-to-all-start.1 = ((bf16[8,384,128]{2,1,0:T(8,128)(2,1)}), bf16[8,384,128]{2,1,0:T(8,128)(2,1)S(1)}, u32[]{:S(2)}, u32[]{:S(2)}) async-start(bf16[8,384,128]{2,1,0:T(8,128)(2,1)} %bitcast.35), calls=%async_computation.1 | async-start | bytes 1572864 | tf_op jit(solution)/shard_map/all_to_all | solution.py:308
  103.3 0.6 copy.22
  103.9 19.1 %all-to-all-done.1 = bf16[8,384,128]{2,1,0:T(8,128)(2,1)S(1)} async-done(((bf16[8,384,128]{2,1,0:T(8,128)(2,1)}), bf16[8,384,128]{2,1,0:T(8,128)(2,1)S(1)}, u32[]{:S(2)}, u32[]{:S(2)}) %all-to-all-start.1) | async-done | bytes 786464 | tf_op jit(solution)/shard_map/all_to_all | solution.py:308
  123.0 0.9 copy-done.4
  123.9 6.7 %pool_sum.1 = f32[2048,128]{1,0:T(8,128)} custom-call(bf16[3072,128]{1,0:T(8,128)(2,1)} %bitcast.36, s32[1,3072]{1,0:T(1,128)} %bitcast.41), custom_call_target="tpu_custom_call" | custom-call | tf_op jit(solution)/shard_map/pool_sum/pallas_call | solution.py:224
  130.6 1.1 constant_dynamic-slice_fusion
  131.8 1.8 collective-permute-done.2
  133.7 1.1 fusion.6
  134.8 1.6 collective-permute-start.3
  136.3 1.8 fusion.4
  138.2 0.6 broadcast_minimum_fusion.1
  138.8 1.0 copy.21.far_ref
  139.8 3.3 %collective-permute-done.3 = bf16[1024,128]{1,0:T(8,128)(2,1)S(1)} collective-permute-done((bf16[1024,128]{1,0:T(8,128)(2,1)S(1)}, bf16[1024,128]{1,0:T(8,128)(2,1)S(1)}, u32[]{:S(2)}, u32[]{:S(2)}) %collective-permute-start.3) | collective-permute-done | bytes 262176 | tf_op jit(solution)/shard_map/ppermute | solution.py:236
  143.5 1.5 collective-permute-done.4
  145.1 1.5 gather_fusion.1
  146.6 3.5 %all-to-all-start.2 = ((bf16[8,32,128]{2,1,0:T(8,128)(2,1)}), bf16[8,32,128]{2,1,0:T(8,128)(2,1)S(1)}, u32[]{:S(2)}, u32[]{:S(2)}) async-start(bf16[8,32,128]{2,1,0:T(8,128)(2,1)} %bitcast.14), calls=%async_computation.2 | async-start | bytes 131072 | tf_op jit(solution)/shard_map/all_to_all | solution.py:242
  150.1 0.6 fusion.17.recv_ref.table_ref
  150.7 4.8 %edge_gather.3.pre_ref = f32[1024,128]{1,0:T(8,128)} custom-call(s32[1024]{0:T(1024)} %get-tuple-element.30.near_ref, s32[1024]{0:T(1024)} %recv_ref.5, bf16[2048,128]{1,0:T(8,128)(2,1)} %copy-done.3, bf16[1024,128]{1,0:T(8,128)(2,1)} %edges_ref.3, bf16[384,128]{1,0:T(8,128)(2,1)} %get-tuple-element.16.w_ref), custom_call_target="tpu_custom_call" | custom-call | tf_op jit(solution)/shard_map/edge_gather/pallas_call | solution.py:91
  155.5 1.5 all-to-all-done.2
  157.0 0.6 copy-done.7
  157.6 6.8 %edge_message.3 = (f32[1024,128]{1,0:T(8,128)}, bf16[1024,128]{1,0:T(8,128)(2,1)}) custom-call(s32[1024]{0:T(1024)} %fusion.17.recv_ref.table_ref, s32[1024]{0:T(1024)} %fusion.17.recv_ref.table_ref, s32[1024,1]{1,0:T(8,128)} %copy.21.far_ref, f32[1024,128]{1,0:T(8,128)} %edge_gather.3.pre_ref, bf16[256,128]{1,0:T(8,128)(2,1)} %bitcast.39, ...), custom_call_target="tpu_custom_call" | custom-call | tf_op jit(solution)/shard_map/edge_message/pallas_call | solution.py:147
  164.4 1.7 collective-permute-done.5
  166.1 1.8 add_convert_fusion.1
  167.9 1.5 collective-permute-start.6
  169.4 0.6 min.17.index_ref
  170.0 1.1 fusion.7.rows_ref
  171.1 0.7 slice.88.first_ref
  171.8 1.7 collective-permute-done.6.second_ref
  173.4 0.6 copy-done.9
  174.1 2.8 %node_update.3 = bf16[512,128]{1,0:T(8,128)(2,1)} custom-call(bf16[512,128]{1,0:T(8,128)(2,1)} %fusion.7.rows_ref, f32[512,128]{1,0:T(8,128)} %get-tuple-element.13.kept_ref, bf16[512,128]{1,0:T(8,128)(2,1)} %slice.88.first_ref, bf16[512,128]{1,0:T(8,128)(2,1)} %copy-done.9, bf16[256,128]{1,0:T(8,128)(2,1)} %get-tuple-element.18.w_ref, ...), custom_call_target="tpu_custom_call" | custom-call | tf_op jit(solution)/shard_map/node_update/pallas_call | solution.py:174
  176.9 8.2 %all_gather.3.table_ref = bf16[2048,128]{1,0:T(8,128)(2,1)} all-gather(bf16[512,128]{1,0:T(8,128)(2,1)} %node_update.3), channel_id=1, replica_groups=mesh['dom'=8,'edge'=4] {'edge'}, dimensions={0}, use_global_device_ids=true | all-gather | bytes 655360 | tf_op jit(solution)/shard_map/all_gather | solution.py:326
  185.1 5.5 %take_rows.4 = bf16[3072,128]{1,0:T(8,128)(2,1)} custom-call(s32[3072]{0:T(1024)} %min.17.index_ref, bf16[2048,128]{1,0:T(8,128)(2,1)} %all_gather.3.table_ref), custom_call_target="tpu_custom_call" | custom-call | tf_op jit(solution)/shard_map/take_rows/pallas_call | solution.py:202
  190.6 25.1 %all_to_all.20 = bf16[8,384,128]{2,1,0:T(8,128)(2,1)S(1)} all-to-all(bf16[8,384,128]{2,1,0:T(8,128)(2,1)} %bitcast.37), channel_id=1, replica_groups=mesh['dom'=8,'edge'=4] {'dom'}, dimensions={0} | all-to-all | bytes 1572864 | tf_op jit(solution)/shard_map/all_to_all | solution.py:329
  216.0 0.6 collective-permute-start.7
  216.6 18.1 %collective-permute-done.7 = bf16[3072,128]{1,0:T(8,128)(2,1)S(1)} collective-permute-done((bf16[3072,128]{1,0:T(8,128)(2,1)S(1)}, bf16[3072,128]{1,0:T(8,128)(2,1)S(1)}, u32[]{:S(2)}, u32[]{:S(2)}) %collective-permute-start.7) | collective-permute-done | bytes 786464 | tf_op jit(solution)/shard_map/ppermute | solution.py:236
  234.9 3.4 %collective-permute-done.8 = bf16[6144,128]{1,0:T(8,128)(2,1)S(1)} collective-permute-done((bf16[6144,128]{1,0:T(8,128)(2,1)S(1)}, bf16[6144,128]{1,0:T(8,128)(2,1)S(1)}, u32[]{:S(2)}, u32[]{:S(2)}) %collective-permute-start.8) | collective-permute-done | bytes 1572896 | tf_op jit(solution)/shard_map/ppermute | solution.py:236
  238.3 15.5 %pad_maximum_fusion.table_ref = bf16[12288,128]{1,0:T(8,128)(2,1)} fusion(bf16[6144,128]{1,0:T(8,128)(2,1)S(1)} %collective-permute-done.8, bf16[3072,128]{1,0:T(8,128)(2,1)S(1)} %collective-permute-done.7, bf16[3072,128]{1,0:T(8,128)(2,1)S(1)} %fusion.2), kind=kLoop, calls=%fused_computation.4 | loop fusion | flops 9437184 | bytes 6291456 | tf_op jit(solution)/shard_map/concatenate | solution.py:332
  253.8 13.1 %take_rows.5 = bf16[8192,128]{1,0:T(8,128)(2,1)} custom-call(s32[8192]{0:T(1024)} %fusion.12.table_ref.index_ref, bf16[12288,128]{1,0:T(8,128)(2,1)} %pad_maximum_fusion.table_ref), custom_call_target="tpu_custom_call" | custom-call | tf_op jit(solution)/shard_map/take_rows/pallas_call | solution.py:202
  267.0 0.8 copy.24
  (48 shorter events, 1.1 us)
Async XLA Ops:
  4.9 30.3 %all-to-all-start = ((bf16[8,64,128]{2,1,0:T(8,128)(2,1)}), bf16[8,64,128]{2,1,0:T(8,128)(2,1)S(1)}, u32[]{:S(2)}, u32[]{:S(2)}) async-start(bf16[8,64,128]{2,1,0:T(8,128)(2,1)} %bitcast.3), calls=%async_computation | async-start | bytes 262144 | tf_op jit(solution)/shard_map/all_to_all | solution.py:242
  19.9 14.7 %copy-start.11 = (bf16[2,128,128]{2,1,0:T(8,128)(2,1)S(1)}, bf16[2,128,128]{2,1,0:T(8,128)(2,1)}, u32[]{:S(2)}) copy-start(bf16[2,128,128]{2,1,0:T(8,128)(2,1)} %param.31) | copy-start | bytes 196612
  35.2 0.7 copy-start.6
  61.0 3.6 %collective-permute-start = (bf16[6144,128]{1,0:T(8,128)(2,1)}, bf16[6144,128]{1,0:T(8,128)(2,1)S(1)}, u32[]{:S(2)}, u32[]{:S(2)}) collective-permute-start(bf16[6144,128]{1,0:T(8,128)(2,1)} %get-tuple-element.7), channel_id=1, source_target_pairs={{0,1},{1,0},{2,3},{3,2},{4,5},{5,4},{6,7},{7,6},{8,9},{9,8},{10,11... | collective-permute-start | bytes 4718600 | tf_op jit(solution)/shard_map/ppermute | solution.py:236
  64.6 4.8 %copy-start.10 = (s32[1,8,1536]{2,1,0:T(8,128)S(1)}, s32[1,8,1536]{2,1,0:T(8,128)}, u32[]{:S(2)}) copy-start(s32[1,8,1536]{2,1,0:T(8,128)} %param.28) | copy-start | bytes 147460
  67.9 9.2 %copy-start.16 = (f32[2,128]{1,0:T(2,128)S(1)}, f32[2,128]{1,0:T(2,128)}, u32[]{:S(2)}) copy-start(f32[2,128]{1,0:T(2,128)} %param.35) | copy-start | bytes 3076
  67.9 9.7 %copy-start.12 = (bf16[2,128,128]{2,1,0:T(8,128)(2,1)S(1)}, bf16[2,128,128]{2,1,0:T(8,128)(2,1)}, u32[]{:S(2)}) copy-start(bf16[2,128,128]{2,1,0:T(8,128)(2,1)} %param.33) | copy-start | bytes 196612
  67.9 10.4 %copy-start.8 = (bf16[2,256,128]{2,1,0:T(8,128)(2,1)S(1)}, bf16[2,256,128]{2,1,0:T(8,128)(2,1)}, u32[]{:S(2)}) copy-start(bf16[2,256,128]{2,1,0:T(8,128)(2,1)} %param.32) | copy-start | bytes 393220
  67.9 19.6 %collective-permute-start.1 = (bf16[3072,128]{1,0:T(8,128)(2,1)S(1)}, bf16[3072,128]{1,0:T(8,128)(2,1)S(1)}, u32[]{:S(2)}, u32[]{:S(2)}) collective-permute-start(bf16[3072,128]{1,0:T(8,128)(2,1)S(1)} %get-tuple-element.10), channel_id=1, source_target_pairs={{0,2},{1,3},{2,0},{3,1},{4,6},{5,7},{6,4},{7,5},{8,10},{9,11},{10,... | collective-permute-start | bytes 2359304 | tf_op jit(solution)/shard_map/ppermute | solution.py:236
  87.5 0.9 copy-start.5
  97.3 25.7 %all-to-all-start.1 = ((bf16[8,384,128]{2,1,0:T(8,128)(2,1)}), bf16[8,384,128]{2,1,0:T(8,128)(2,1)S(1)}, u32[]{:S(2)}, u32[]{:S(2)}) async-start(bf16[8,384,128]{2,1,0:T(8,128)(2,1)} %bitcast.35), calls=%async_computation.1 | async-start | bytes 1572864 | tf_op jit(solution)/shard_map/all_to_all | solution.py:308
  123.0 0.9 copy-start.4
  130.6 7.6 %copy-start.15 = (s32[1,8,32]{2,1,0:T(8,128)S(1)}, s32[1,8,32]{2,1,0:T(8,128)}, u32[]{:S(2)}) copy-start(s32[1,8,32]{2,1,0:T(8,128)} %param.26) | copy-start | bytes 3076
  130.6 7.6 %copy-start.14 = (s32[1024]{0:T(1024)S(1)}, s32[1024]{0:T(1024)}, u32[]{:S(2)}) copy-start(s32[1024]{0:T(1024)} %param.24) | copy-start | bytes 12292
  131.7 11.5 %copy-start.1 = (f32[2048,128]{1,0:T(8,128)S(1)}, f32[2048,128]{1,0:T(8,128)}, u32[]{:S(2)}) copy-start(f32[2048,128]{1,0:T(8,128)} %pool_sum.1) | copy-start | bytes 3145732
  131.7 2.0 collective-permute-start.2
  134.8 8.4 %collective-permute-start.3 = (bf16[1024,128]{1,0:T(8,128)(2,1)S(1)}, bf16[1024,128]{1,0:T(8,128)(2,1)S(1)}, u32[]{:S(2)}, u32[]{:S(2)}) collective-permute-start(bf16[1024,128]{1,0:T(8,128)(2,1)S(1)} %fusion.6), channel_id=1, source_target_pairs={{0,2},{1,3},{2,0},{3,1},{4,6},{5,7},{6,4},{7,5},{8,10},{9,11},{10,... | collective-permute-start | bytes 786440 | tf_op jit(solution)/shard_map/ppermute | solution.py:236
  139.8 10.2 %copy-start.13 = (s32[1024]{0:T(1024)S(1)}, s32[1024]{0:T(1024)}, u32[]{:S(2)}) copy-start(s32[1024]{0:T(1024)} %recv_ref.5) | copy-start | bytes 12292
  143.4 1.6 collective-permute-start.4
  145.1 5.6 %copy-start.3 = (bf16[2048,128]{1,0:T(8,128)(2,1)}, bf16[2048,128]{1,0:T(8,128)(2,1)S(1)}, u32[]{:S(2)}) copy-start(bf16[2048,128]{1,0:T(8,128)(2,1)S(1)} %pad_maximum_fusion.2.nodes_ref) | copy-start | bytes 1572868
  146.6 10.4 %all-to-all-start.2 = ((bf16[8,32,128]{2,1,0:T(8,128)(2,1)}), bf16[8,32,128]{2,1,0:T(8,128)(2,1)S(1)}, u32[]{:S(2)}, u32[]{:S(2)}) async-start(bf16[8,32,128]{2,1,0:T(8,128)(2,1)} %bitcast.14), calls=%async_computation.2 | async-start | bytes 131072 | tf_op jit(solution)/shard_map/all_to_all | solution.py:242
  157.0 0.6 copy-start.7
  164.4 1.7 collective-permute-start.5
  167.9 5.5 %collective-permute-start.6 = (bf16[512,128]{1,0:T(8,128)(2,1)S(1)}, bf16[512,128]{1,0:T(8,128)(2,1)S(1)}, u32[]{:S(2)}, u32[]{:S(2)}) collective-permute-start(bf16[512,128]{1,0:T(8,128)(2,1)S(1)} %get-tuple-element.12), channel_id=1, source_target_pairs={{0,2},{1,3},{2,0},{3,1},{4,6},{5,7},{6,4},{7,5},{8,10},{9,11},{10,... | collective-permute-start | bytes 393224 | tf_op jit(solution)/shard_map/ppermute | solution.py:236
  173.4 0.6 copy-start.9
  174.1 41.6 %copy-start = (bf16[3072,128]{1,0:T(8,128)(2,1)S(1)}, bf16[3072,128]{1,0:T(8,128)(2,1)}, u32[]{:S(2)}) copy-start(bf16[3072,128]{1,0:T(8,128)(2,1)} %node_update.2) | copy-start | bytes 2359300
  216.0 18.7 %collective-permute-start.7 = (bf16[3072,128]{1,0:T(8,128)(2,1)S(1)}, bf16[3072,128]{1,0:T(8,128)(2,1)S(1)}, u32[]{:S(2)}, u32[]{:S(2)}) collective-permute-start(bf16[3072,128]{1,0:T(8,128)(2,1)S(1)} %fusion.2), channel_id=1, source_target_pairs={{0,2},{1,3},{2,0},{3,1},{4,6},{5,7},{6,4},{7,5},{8,10},{9,11},{10,... | collective-permute-start | bytes 2359304 | tf_op jit(solution)/shard_map/ppermute | solution.py:236
  234.8 3.5 %collective-permute-start.8 = (bf16[6144,128]{1,0:T(8,128)(2,1)S(1)}, bf16[6144,128]{1,0:T(8,128)(2,1)S(1)}, u32[]{:S(2)}, u32[]{:S(2)}) collective-permute-start(bf16[6144,128]{1,0:T(8,128)(2,1)S(1)} %pad_maximum_fusion.1), channel_id=1, source_target_pairs={{0,1},{1,0},{2,3},{3,2},{4,5},{5,4},{6,7},{7,6},{8,9},{9,8},{10,11... | collective-permute-start | bytes 4718600 | tf_op jit(solution)/shard_map/ppermute | solution.py:236
  253.8 13.1 %copy-start.2 = (bf16[2048,128]{1,0:T(8,128)(2,1)S(1)}, bf16[2048,128]{1,0:T(8,128)(2,1)}, u32[]{:S(2)}) copy-start(bf16[2048,128]{1,0:T(8,128)(2,1)} %all_gather.3.table_ref) | copy-start | bytes 1572868

commit v2 on v1

v2 whole, which is shorter than its diff:
```python
import jax
import jax.numpy as jnp
from jax import lax
from jax.experimental import pallas as pl
from jax.experimental.pallas import tpu as pltpu
from jax.sharding import PartitionSpec as P

BF = jnp.bfloat16
F32 = jnp.float32
VMEM = pl.BlockSpec(memory_space=pltpu.VMEM)
SMEM = pl.BlockSpec(memory_space=pltpu.SMEM)
HBM = pl.BlockSpec(memory_space=pltpu.HBM)
INDEX = "index"
WEIGHT = "weight"
COARSE = 2048
UNROLL = 32
ACCS = 4


def nbytes(x):
    width = -(-x.shape[-1] // 128) * 128
    return x.size // x.shape[-1] * width * x.dtype.itemsize


class Late:
    def __init__(self, ref, copy):
        self.ref = ref
        self.wait = copy.wait


def call(kernel, out_shape, in_specs, scratch=(), name=None):
    def run(*args):
        late = [k for k, spec in enumerate(in_specs) if spec in (INDEX, WEIGHT)]
        homes = [
            (pltpu.SMEM if in_specs[k] is INDEX else pltpu.VMEM)(args[k].shape, args[k].dtype) for k in late
        ]
        used = sum(nbytes(x) for x, spec in zip(args, in_specs) if spec is VMEM or spec is WEIGHT)
        used += sum(nbytes(x) for x in jax.tree.leaves(out_shape) if len(x.shape) > 1)
        used += sum(nbytes(x) for x in scratch)
        n_out = len(jax.tree.leaves(out_shape))

        def body(*refs):
            ins, outs = list(refs[: len(args)]), refs[len(args) : len(args) + n_out]
            mine = refs[len(args) + n_out : len(args) + n_out + len(scratch)]
            rest = refs[len(args) + n_out + len(scratch) :]
            for at, k in enumerate(late):
                copy = pltpu.make_async_copy(ins[k], rest[at], rest[len(late) + at])
                copy.start()
                ins[k] = Late(rest[at], copy)
            kernel(*ins, *outs, *mine)

        return pl.pallas_call(
            body,
            out_shape=out_shape,
            in_specs=[HBM if spec in (INDEX, WEIGHT) else spec for spec in in_specs],
            out_specs=jax.tree.map(lambda x: VMEM if len(x.shape) > 1 else SMEM, out_shape),
            scratch_shapes=[pltpu.VMEM(x.shape, x.dtype) for x in scratch]
            + homes
            + [pltpu.SemaphoreType.DMA(())] * len(late),
            name=name,
            compiler_params=pltpu.CompilerParams(vmem_limit_bytes=used + 2 * 1024 * 1024),
        )(*args)

    return run


def shaped(rows, dtype, width=128):
    return jax.ShapeDtypeStruct((rows, width), dtype)


def dot(a, b):
    return jnp.dot(a, b, preferred_element_type=F32)


def silu(v):
    return v / (1.0 + jnp.exp(-v))


def norm(values, gain):
    center = values - jnp.mean(values, axis=-1, keepdims=True)
    spread = jnp.mean(center * center, axis=-1, keepdims=True)
    return center * lax.rsqrt(spread + 1e-05) * gain


def blocks(total, size, body):
    size = min(size, total)

    def step(i, carry):
        body(pl.multiple_of(i * size, size))
        return carry

    lax.fori_loop(0, total // size, step, 0)


def edge_gather(nodes, senders, receivers, w_in, level, ghost_rows):
    rows, width = nodes.shape
    count = senders.shape[0]

    def kernel(send_idx, recv_idx, nodes_ref, w_late, out_ref, send_tab, recv_tab):
        send_tab[pl.ds(rows, ghost_rows), :] = jnp.zeros((ghost_rows, width), F32)
        w_late.wait()
        w_s = w_late.ref[level, 0:width, :]
        w_r = w_late.ref[level, width : 2 * width, :]

        def project(at):
            block = nodes_ref[pl.ds(at, 512), :]
            send_tab[pl.ds(at, 512), :] = dot(block, w_s)
            recv_tab[pl.ds(at, 512), :] = dot(block, w_r)

        blocks(rows, 512, project)
        send_idx.wait()
        recv_idx.wait()

        def gather(i, carry):
            base = i * UNROLL
            for j in range(UNROLL):
                s = send_idx.ref[base + j]
                r = recv_idx.ref[base + j]
                out_ref[pl.ds(base + j, 1), :] = send_tab[pl.ds(s, 1), :] + recv_tab[pl.ds(r, 1), :]
            return carry

        lax.fori_loop(0, count // UNROLL, gather, 0)

    return call(
        kernel,
        shaped(count, F32),
        [INDEX, INDEX, VMEM, WEIGHT],
        [shaped(rows + ghost_rows, F32), shaped(rows, F32)],
        "edge_gather",
    )(senders, receivers, nodes, w_in)


def edge_message(pre, edges, ghosts, senders, receivers, table, w_in, w_out, gain, level, rows, slots):
    count, width = pre.shape
    ghost_rows = ghosts.shape[0]
    fourth = slots // 4
    n = 256
    total = count // n
    mapped = table is not None

    def kernel(recv_idx, *refs):
        if mapped:
            table_idx, refs = refs[0], refs[1:]
        (send_late, pre_ref, edge_ref, ghost_ref, w_late, wo_late, gain_late,
         k0_ref, k2_ref, s1_ref, s3_ref, even, odd) = refs[:13]
        accs = refs[13:]

        def clear(at):
            for acc in accs:
                acc[pl.ds(at, 512), :] = jnp.zeros((512, width), F32)

        blocks(slots, 512, clear)
        send_late.wait()
        w_late.wait()
        wo_late.wait()
        gain_late.wait()
        w_s = w_late.ref[level, 0:width, :]
        w_e = w_late.ref[level, 2 * width : 3 * width, :]
        w_o = wo_late.ref[level]
        scale = gain_late.ref[level : level + 1, :]

        def message(b, msg):
            at = pl.multiple_of(b * n, n)
            columns = []
            for k in range(n // 128):
                far = (send_late.ref[pl.ds(b * (n // 128) + k, 1), :] - rows).astype(F32)
                columns.append(jnp.broadcast_to(far, (8, 128)).T[:, 0:1])
            column = jnp.concatenate(columns, axis=0)
            lane = lax.broadcasted_iota(jnp.int32, (n, ghost_rows), 1).astype(F32)
            pick = (column == lane).astype(BF)
            picked = dot(pick, ghost_ref[...]).astype(BF)
            first = pre_ref[pl.ds(at, n), :] + (dot(picked, w_s) + dot(edge_ref[pl.ds(at, n), :], w_e))
            msg[...] = norm(dot(silu(first).astype(BF), w_o), scale)

        def scatter(b, msg):
            base = b * n
            for j in range(n):
                acc = accs[j % ACCS]
                r = recv_idx.ref[base + j]
                if mapped:
                    r = table_idx.ref[r]
                acc[pl.ds(r, 1), :] = acc[pl.ds(r, 1), :] + msg[pl.ds(j, 1), :]

        message(0, even)
        recv_idx.wait()
        if mapped:
            table_idx.wait()

        def step(i, carry):
            b = 2 * i
            message(b + 1, odd)
            scatter(b, even)
            message(jnp.minimum(b + 2, total - 1), even)
            scatter(b + 1, odd)
            return carry

        lax.fori_loop(0, total // 2, step, 0)
        for place, out_ref in ((3, s3_ref), (1, k2_ref), (2, s1_ref), (0, k0_ref)):
            m = 256 if fourth % 256 == 0 else fourth

            def body(at, out_ref=out_ref, start=place * fourth, m=m):
                value = accs[0][pl.ds(at + start, m), :]
                for acc in accs[1:]:
                    value = value + acc[pl.ds(at + start, m), :]
                out_ref[pl.ds(at, m), :] = value.astype(out_ref.dtype)

            blocks(fourth, m, body)

    maps = [INDEX, INDEX] if mapped else [INDEX]
    index = (receivers, table) if mapped else (receivers,)
    return call(
        kernel,
        (shaped(fourth, F32), shaped(fourth, F32), shaped(fourth, BF), shaped(fourth, BF)),
        maps + [WEIGHT] + [VMEM] * 3 + [WEIGHT] * 3,
        [shaped(n, F32), shaped(n, F32)] + [shaped(slots, F32)] * ACCS,
        "edge_message",
    )(*index, senders.reshape(-1, 128), pre, edges, ghosts, w_in, w_out, gain)


def node_update(rows, kept, first, second, w_in, w_out, gain, level):
    count, width = rows.shape
    n = min(512, count)

    def kernel(rows_ref, kept_ref, first_ref, second_ref, w_late, wo_late, gain_late, out_ref):
        for late in (w_late, wo_late, gain_late):
            late.wait()
        w_n = w_late.ref[level, 0:width, :]
        w_a = w_late.ref[level, width : 2 * width, :]
        w_o = wo_late.ref[level]
        scale = gain_late.ref[level : level + 1, :]

        def step(at):
            own = rows_ref[pl.ds(at, n), :]
            total = (
                kept_ref[pl.ds(at, n), :]
                + first_ref[pl.ds(at, n), :].astype(F32)
                + second_ref[pl.ds(at, n), :].astype(F32)
            ).astype(BF)
            hidden = silu(dot(own, w_n) + dot(total, w_a)).astype(BF)
            result = norm(dot(hidden, w_o), scale)
            out_ref[pl.ds(at, n), :] = (own.astype(F32) + result).astype(BF)

        blocks(count, n, step)

    return call(kernel, shaped(count, BF), [VMEM] * 4 + [WEIGHT] * 3, (), "node_update")(
        rows, kept, first, second, w_in, w_out, gain
    )


def take_rows(tables, index):
    width = tables[0].shape[1]
    rows = sum(x.shape[0] for x in tables)
    count = index.shape[0]

    def kernel(index_late, *refs):
        refs, (out_ref, wide, picked) = refs[:-3], refs[-3:]
        start = 0
        for ref in refs:

            def widen(at, ref=ref, start=start):
                wide[pl.ds(start + at, 256), :] = ref[pl.ds(at, 256), :].astype(F32)

            blocks(ref.shape[0], 256, widen)
            start += ref.shape[0]
        index_late.wait()

        def gather(i, carry):
            base = i * UNROLL
            for j in range(UNROLL):
                picked[pl.ds(base + j, 1), :] = wide[pl.ds(index_late.ref[base + j], 1), :]
            return carry

        lax.fori_loop(0, count // UNROLL, gather, 0)

        def narrow(at):
            out_ref[pl.ds(at, 256), :] = picked[pl.ds(at, 256), :].astype(BF)

        blocks(count, 256, narrow)

    return call(
        kernel,
        shaped(count, BF),
        [INDEX] + [VMEM] * len(tables),
        [shaped(rows, F32), shaped(count, F32)],
        "take_rows",
    )(index, *tables)


def resolve(table, index):
    count = index.shape[0]

    def kernel(table_late, index_late, out_ref):
        table_late.wait()
        index_late.wait()

        def look(i, carry):
            base = i * UNROLL
            for j in range(UNROLL):
                out_ref[base + j] = table_late.ref[index_late.ref[base + j]]
            return carry

        lax.fori_loop(0, count // UNROLL, look, 0)

    return call(kernel, jax.ShapeDtypeStruct((count,), jnp.int32), [INDEX, INDEX], (), "resolve")(table, index)


def pool_sum(arrived, places):
    count, width = arrived.shape
    n = 256

    def kernel(arrived_ref, places_late, out_ref):
        places_late.wait()
        rows = arrived_ref[...]

        def step(at):
            pick = (places_late.ref[...] == at + lax.broadcasted_iota(jnp.int32, (n, count), 0)).astype(BF)
            out_ref[pl.ds(at, n), :] = dot(pick, rows)

        blocks(COARSE, n, step)

    return call(kernel, shaped(COARSE, F32), [VMEM, WEIGHT], (), "pool_sum")(arrived, places.reshape(1, count))


def child_count(places):
    count = places.shape[0]
    high = (places // 128)[None, :] == jnp.arange(COARSE // 128, dtype=jnp.int32)[:, None]
    low = (places % 128)[:, None] == jnp.arange(128, dtype=jnp.int32)[None, :]
    return dot(high.astype(BF), low.astype(BF)).reshape(COARSE)


def swap(x, bit):
    size = lax.axis_size("edge")
    return lax.ppermute(x, "edge", [(i, i ^ bit) for i in range(size)])


def layer_sums(nodes, edges, senders, receivers, border, level, w, slots, table):
    rows, width = nodes.shape
    outgoing = nodes[border[0].reshape(-1)].reshape(border.shape[1], border.shape[2], width)
    arrived = lax.all_to_all(outgoing, "dom", split_axis=0, concat_axis=0, tiled=True)
    ghosts = arrived.reshape(-1, width)
    pre = edge_gather(nodes, senders, receivers, w[0], level, ghosts.shape[0])
    if table is None:
        me = lax.axis_index("edge")
        quarter = rows // 4
        receivers = order_of((receivers // quarter) ^ me) * quarter + receivers % quarter
    k0, k2, s1, s3 = edge_message(
        pre, edges, ghosts, senders, receivers, table, w[0], w[1], w[4], level, rows, slots
    )
    second = swap((k2 + swap(s3, 1).astype(F32)).astype(BF), 2)
    return k0, swap(s1, 1), second


def order_of(rel):
    return (rel & 1) * 2 + (rel >> 1)


def shards(
    fine_nodes,
    fine_edges,
    fine_senders,
    fine_receivers,
    fine_halo,
    coarse_edges,
    coarse_senders,
    coarse_receivers,
    coarse_halo,
    pool_send,
    pool_dest,
    unpool_slot,
    edge_in_weight,
    edge_out_weight,
    node_in_weight,
    node_out_weight,
    edge_gain,
    node_gain,
):
    w = (edge_in_weight, edge_out_weight, node_in_weight, node_out_weight, edge_gain, node_gain)
    width = fine_nodes.shape[-1]
    n_dom = pool_send.shape[1]
    span = pool_send.shape[2]
    part = span // 4
    slots = n_dom * span
    quarter = n_dom * part
    me = lax.axis_index("edge")
    target = unpool_slot // span
    within = unpool_slot % span
    slot_place = order_of((within // part) ^ me) * quarter + target * part + within % part
    my_send = lax.dynamic_slice_in_dim(pool_send[0], me * part, part, 1).reshape(-1)
    my_dest = lax.dynamic_slice_in_dim(pool_dest[0], me * part, part, 1).reshape(-1)
    counts = child_count(pool_dest[0].reshape(-1))
    scale = jnp.maximum(counts, 1.0)[:, None]

    kept, first, second = layer_sums(
        fine_nodes, fine_edges, fine_senders, fine_receivers, fine_halo, 0, w, slots, slot_place
    )
    direct = n_dom == 8
    my_send, lists, kept = lax.optimization_barrier((my_send, pool_dest[0], kept))
    if direct:
        known = lax.all_to_all(lists, "dom", 0, 0, tiled=True)
        place = place_of(known)
    own = take_rows([fine_nodes], my_send)
    mid = node_update(own, kept, first, second, w[2], w[3], w[5], 0)

    arrived = lax.all_to_all(mid.reshape(n_dom, part, width), "dom", split_axis=0, concat_axis=0, tiled=True)
    if direct:
        mid_x = swap(mid, 2)
        place, slot_of, _ = lax.optimization_barrier((place, unpool_slot, mid))
        parent = resolve(place, slot_of)
        my_dest, parent, arrived, mid_x = lax.optimization_barrier((my_dest, parent, arrived, mid_x))
    sums = pool_sum(arrived.reshape(-1, width), my_dest)
    bit = me & 1
    half = COARSE // 2
    mine = lax.dynamic_slice_in_dim(sums, bit * half, half, 0)
    theirs = lax.dynamic_slice_in_dim(sums, (1 - bit) * half, half, 0)
    mine = mine + swap(theirs, 1)
    mine = mine + swap(mine.astype(BF), 2).astype(F32)
    mine = (mine / lax.dynamic_slice_in_dim(scale, bit * half, half, 0)).astype(BF)
    if direct:
        mine, mid, mid_1, mid_3 = lax.optimization_barrier((mine, mid, swap(mid, 1), swap(mid_x, 1)))
    theirs = swap(mine, 1)
    coarse_in = jnp.concatenate([jnp.where(bit == 0, mine, theirs), jnp.where(bit == 0, theirs, mine)], axis=0)

    kept, first, second = layer_sums(
        coarse_in, coarse_edges, coarse_senders, coarse_receivers, coarse_halo, 1, w, COARSE, None
    )
    fourth = COARSE // 4
    own = lax.dynamic_slice_in_dim(coarse_in, me * fourth, fourth, 0)
    top = node_update(own, kept, first, second, w[2], w[3], w[5], 1)
    if direct:
        return spread_out(top, [mid, mid_x, mid_1, mid_3], slot_place, parent)

    coarse_out = lax.all_gather(top, "edge", axis=0, tiled=True)
    parents = take_rows([coarse_out], jnp.minimum(my_dest, COARSE - 1))
    back = lax.all_to_all(parents.reshape(n_dom, part, width), "dom", split_axis=0, concat_axis=0, tiled=True)
    final = (mid.astype(F32) + back.reshape(-1, width).astype(F32)).astype(BF)
    final_x = swap(final, 2)
    fine_out = take_rows([final, final_x, swap(final, 1), swap(final_x, 1)], slot_place)
    return (fine_out, coarse_out)


def place_of(known):
    me = lax.axis_index("edge")
    here = lax.axis_index("dom")
    fourth = COARSE // 4
    owner = jnp.arange(known.shape[0], dtype=jnp.int32)[:, None]
    rel = (known // fourth) ^ me
    spot = (rel & 1) * 4 + (rel >> 1) * 2 + ((owner ^ here) & 1)
    return (spot * (4 * fourth) + (owner >> 1) * fourth + known % fourth).reshape(-1)


def spread_out(top, mids, slot_place, parent):
    fourth, width = top.shape
    me = lax.axis_index("edge")
    here = lax.axis_index("dom")
    lines = [[0, 2, 4, 6], [1, 3, 5, 7]]

    def cross(x):
        return lax.ppermute(x, "dom", [(i, i ^ 1) for i in range(8)])

    copies = jnp.broadcast_to(top[None], (4, fourth, width))
    line = lax.all_to_all(copies, "dom", 0, 0, tiled=True, axis_index_groups=lines).reshape(4 * fourth, width)
    slot_place, _ = lax.optimization_barrier((slot_place, top))
    mid_rows = take_rows(mids, slot_place)
    line, mid_rows = lax.optimization_barrier((line, mid_rows))
    line_y = cross(line)
    line_x = swap(line, 2)
    corner_x = swap(line_y[: 2 * fourth], 2)
    corner_y = cross(line_x[2 * fourth :])
    pieces = [line, line_y, line_x, corner_x, corner_y]
    pieces = pieces + [swap(x, 1) for x in pieces]

    rel = jnp.arange(4, dtype=jnp.int32) ^ me
    starts = ((rel & 1) * 4 + (rel >> 1) * 2) * (4 * fourth) + (here >> 1) * fourth
    return unpool(pieces, mid_rows, parent, starts)


def unpool(pieces, mid_rows, parent, starts):
    count, width = mid_rows.shape
    total = sum(x.shape[0] for x in pieces)
    fourth = COARSE // 4

    def kernel(parent_ref, starts_ref, mid_ref, *refs):
        refs, (out_ref, coarse_ref, wide, picked) = refs[:-4], refs[-4:]
        start = 0
        for ref in refs:

            def widen(at, ref=ref, start=start):
                wide[pl.ds(start + at, 256), :] = ref[pl.ds(at, 256), :].astype(F32)

            blocks(ref.shape[0], 256, widen)
            start += ref.shape[0]
        parent_ref.wait()

        def gather(i, carry):
            base = i * UNROLL
            for j in range(UNROLL):
                picked[pl.ds(base + j, 1), :] = wide[pl.ds(parent_ref.ref[base + j], 1), :]
            return carry

        lax.fori_loop(0, count // UNROLL, gather, 0)
        starts_ref.wait()
        for k in range(4):
            rows = wide[pl.ds(pl.multiple_of(starts_ref.ref[k], fourth), fourth), :]
            coarse_ref[k * fourth : (k + 1) * fourth, :] = rows.astype(BF)

        def narrow(at):
            out_ref[pl.ds(at, 256), :] = (picked[pl.ds(at, 256), :] + mid_ref[pl.ds(at, 256), :].astype(F32)).astype(BF)

        blocks(count, 256, narrow)

    return call(
        kernel,
        (shaped(count, BF), shaped(COARSE, BF)),
        [INDEX, INDEX, VMEM] + [VMEM] * len(pieces),
        [shaped(total, F32), shaped(count, F32)],
        "unpool",
    )(parent, starts, mid_rows, *pieces)


def solution(mesh):
    placed = (
        P("dom", None),
        P(("dom", "edge"), None),
        P(("dom", "edge")),
        P(("dom", "edge")),
        P("dom", None, None),
        P(("dom", "edge"), None),
        P(("dom", "edge")),
        P(("dom", "edge")),
        P("dom", None, None),
        P("dom", None, None),
        P("dom", None, None),
        P("dom"),
        P(),
        P(),
        P(),
        P(),
        P(),
        P(),
    )
    return jax.shard_map(
        shards,
        mesh=mesh,
        in_specs=placed,
        out_specs=(P("dom", None), P("dom", None)),
        check_vma=False,
    )
```

time: 269 us -> 205 us (0.76)
  blocking collectives: 33.3 us -> 0 us
  other arithmetic: 28.2 us -> 5.61 us
  starting transfers between devices: 22.2 us -> 38.5 us
  waiting for transfers between devices: 63.4 us -> 51 us
  Pallas kernels: 94.8 us -> 86.5 us
  local copies, waits for them, and re-layouts: 23.3 us -> 18.8 us
    all_to_all x1 -> x0, blocking collectives: 25.1 us -> none  [shards(): lax.all_to_all(parents.reshape(n_dom, part, width), 'dom', split_axis=0,...]
    all_to_all x1, waiting for transfers between devices: 19.1 us -> 0.01 us  [shards(): lax.all_to_all(mid.reshape(n_dom, part, width), 'dom', split_axis=0, conc...]
    concatenate x2 -> x0, other arithmetic: 15.6 us -> none  [the longest x1 15.5 us: shards(): table = jnp.concatenate([pair, swap(pair, 1)], axis=0)]
    all_to_all x0 -> x2, starting transfers between devices: none -> 9.47 us  [the longest x1 6 us: shards(): known = lax.all_to_all(lists, 'dom', 0, 0, tiled=True)]
    pallas_call x10 -> x11, Pallas kernels: 94.8 us -> 86.5 us  [run(): pl.pallas_call(body, out_shape=out_shape, in_specs=[HBM if spec in (INDEX...]
    all_gather x1 -> x0, blocking collectives: 8.16 us -> none  [shards(): coarse_out = lax.all_gather(top, 'edge', axis=0, tiled=True)]
    unnamed x36 -> x74, local copies, waits for them, and re-layouts: 5.14 us -> 9.43 us
    convert_element_type x3 -> x2, other arithmetic: 5.28 us -> 1.06 us  [layer_sums(): second = swap((k2 + swap(s3, 1).astype(F32)).astype(BF), 2)]
  transfers between devices with their start and end apart: 12 -> 26, of which waited for: 11 -> 13; matrix products, arithmetic and copies ran while one was open for 7% -> 4% of each run, Pallas kernels for 10% -> 24%
where the time goes in v2:
time: 205 us; the launch traced here: 204 us
  Pallas kernels  86.5 us (42%)
  waiting for transfers between devices  51 us (25%)
  starting transfers between devices  38.5 us (19%)
  local copies, waits for them, and re-layouts  18.8 us (9%)
  other arithmetic  5.61 us (3%)
    pallas_call x11, Pallas kernels, run(): pl.pallas_call(body, out_shape=out_shape, in_specs=[HBM if spec in (INDEX...  86.5 us
    ppermute x19, waiting for transfers between devices, swap(): return lax.ppermute(x, 'edge', [(i, i ^ bit) for i in range(size)])  40.7 us
    all_to_all x2, starting transfers between devices, layer_sums(): lax.all_to_all(outgoing, 'dom', split_axis=0, concat_axis=0, tiled=True)  13.3 us
    unnamed x74, local copies, waits for them, and re-layouts  9.43 us
    ppermute x19, starting transfers between devices, swap(): return lax.ppermute(x, 'edge', [(i, i ^ bit) for i in range(size)])  8.93 us
    all_to_all x1, starting transfers between devices, shards(): lax.all_to_all(mid.reshape(n_dom, part, width), 'dom', split_axis=0, conc...  6.01 us
    all_to_all x1, starting transfers between devices, shards(): known = lax.all_to_all(lists, 'dom', 0, 0, tiled=True)  6 us
    gather x2, local copies, waits for them, and re-layouts, layer_sums(): nodes[border[0].reshape(-1)]  4.99 us
  transfers between devices with their start and end apart: 26, of which 13 were waited for; matrix products, arithmetic and copies ran while one was open for 4% of the time, Pallas kernels for 24%

profile of v2, /device:TPU:0, one launch (start us, length us, event | category | flops | bytes accessed | tf_op | source)
XLA Modules:
  0.0 203.5 jit_solution(14936391897629458539)
XLA Ops:
  0.6 0.8 reshape_squeeze.9
  1.4 3.5 %gather_fusion = bf16[512,128]{1,0:T(8,128)(2,1)} fusion(bf16[8192,128]{1,0:T(8,128)(2,1)} %refs_1_.4, s32[1024]{0:T(1024)S(1)} %pad_clamp_fusion.1), kind=kCustom, calls=%fused_computation | custom fusion | bytes 264192 | tf_op jit(solution)/shard_map/gather | solution.py:338
  5.0 7.3 %all-to-all-start = ((bf16[8,64,128]{2,1,0:T(8,128)(2,1)}), bf16[8,64,128]{2,1,0:T(8,128)(2,1)S(1)}, u32[]{:S(2)}, u32[]{:S(2)}) async-start(bf16[8,64,128]{2,1,0:T(8,128)(2,1)} %bitcast.3), calls=%async_computation | async-start | bytes 262144 | tf_op jit(solution)/shard_map/all_to_all | solution.py:339
  12.3 1.6 copy-done.1
  13.9 0.9 copy-done.3
  14.8 0.7 copy-done.21
  15.5 0.7 copy-done.23
  16.2 9.7 %edge_gather.2.refs_3_ = f32[4096,128]{1,0:T(8,128)S(1)} custom-call(s32[4096]{0:T(1024)S(1)} %copy-done.23, s32[4096]{0:T(1024)S(1)} %copy-done.21, bf16[8192,128]{1,0:T(8,128)(2,1)S(1)} %copy-done.1, bf16[2,384,128]{2,1,0:T(8,128)(2,1)S(1)} %copy-done.3), custom_call_target="tpu_custom_call" | custom-call | tf_op jit(solution)/shard_map/edge_gather/pallas_call | solution.py:52
  26.1 0.8 copy-done.12
  26.9 0.7 copy-done.22
  27.6 0.7 copy-done.24
  28.3 0.7 copy-done.27
  29.0 15.2 %edge_message.2 = (f32[3072,128]{1,0:T(8,128)S(1)}, f32[3072,128]{1,0:T(8,128)S(1)}, bf16[3072,128]{1,0:T(8,128)(2,1)}, bf16[3072,128]{1,0:T(8,128)(2,1)S(1)}) custom-call(s32[4096]{0:T(1024)S(1)} %copy-done.22, s32[8192]{0:T(1024)S(1)} %fusion.17.refs_1_.refs_0_, s32[32,128]{1,0:T(8,128)S(1)} %bitcast.23, f32[4096,128]{1,0:T(8,128)S(1)} %edge_gather.2.refs_3_, ...), custom_call_target="tpu_custom_call" | custom-call | tf_op jit(solution)/shard_map/edge_message/pallas_call | solution.py:52
  44.3 0.5 collective-permute-start
  44.8 1.8 collective-permute-done.1
  46.6 1.0 add_convert_fusion
  47.6 1.6 collective-permute-start.2
  49.2 0.7 all_to_all.21
  49.9 6.0 %all-to-all-start.1 = ((s32[8,1,1536]{2,1,0:T(1,128)}), s32[8,1,1536]{2,1,0:T(1,128)S(1)}, u32[]{:S(2)}, u32[]{:S(2)}) async-start(s32[8,1,1536]{2,1,0:T(1,128)} %all_to_all.21), calls=%async_computation.1 | async-start | bytes 98304 | tf_op jit(solution)/shard_map/all_to_all | solution.py:399
  55.9 3.7 %take_rows.2.refs_0_ = bf16[3072,128]{1,0:T(8,128)(2,1)S(1)} custom-call(s32[3072]{0:T(1024)S(1)} %reshape.176.refs_0_, bf16[8192,128]{1,0:T(8,128)(2,1)S(1)} %copy-done.2), custom_call_target="tpu_custom_call" | custom-call | tf_op jit(solution)/shard_map/take_rows/pallas_call | solution.py:52
  59.7 8.0 %collective-permute-done.2.refs_3_ = bf16[3072,128]{1,0:T(8,128)(2,1)} collective-permute-done((bf16[3072,128]{1,0:T(8,128)(2,1)}, bf16[3072,128]{1,0:T(8,128)(2,1)}, u32[]{:S(2)}, u32[]{:S(2)}) %collective-permute-start.2) | collective-permute-done | bytes 786464 | tf_op jit(solution)/shard_map/ppermute | solution.py:333
  67.6 5.6 %node_update.2.refs_1_ = bf16[3072,128]{1,0:T(8,128)(2,1)} custom-call(bf16[3072,128]{1,0:T(8,128)(2,1)S(1)} %take_rows.2.refs_0_, f32[3072,128]{1,0:T(8,128)S(1)} %copy-done.6, bf16[3072,128]{1,0:T(8,128)(2,1)S(1)} %collective-permute-done.refs_2_, bf16[3072,128]{1,0:T(8,128)(2,1)} %collective-permute-done.2.refs_3_, bf16[2,256,128]{2,1,0:T(8,128)(2,1)S(1)} %copy-done.10, ...), custom_call_target="tpu_custom_call" | custom-call | tf_op jit(solution)/shard_map/node_update/pallas_call | solution.py:52
  73.3 6.0 %all-to-all-start.2 = ((bf16[8,384,128]{2,1,0:T(8,128)(2,1)}), bf16[8,384,128]{2,1,0:T(8,128)(2,1)S(1)}, u32[]{:S(2)}, u32[]{:S(2)}) async-start(bf16[8,384,128]{2,1,0:T(8,128)(2,1)} %bitcast.6), calls=%async_computation.2 | async-start | bytes 1572864 | tf_op jit(solution)/shard_map/all_to_all | solution.py:404
  79.3 1.6 collective-permute-start.3
  81.0 0.9 fusion.8.refs_0_
  81.9 16.8 %resolve.1.refs_0_ = s32[8192]{0:T(1024)S(1)} custom-call(s32[12288]{0:T(1024)S(1)} %fusion.8.refs_0_, s32[8192]{0:T(1024)S(1)} %copy-done.20), custom_call_target="tpu_custom_call" | custom-call | tf_op jit(solution)/shard_map/resolve/pallas_call | solution.py:52
  98.7 0.6 copy-done.17
  99.3 4.6 %pool_sum.1 = f32[2048,128]{1,0:T(8,128)S(1)} custom-call(bf16[3072,128]{1,0:T(8,128)(2,1)S(1)} %bitcast.16, s32[1,3072]{1,0:T(1,128)S(1)} %bitcast.24), custom_call_target="tpu_custom_call" | custom-call | tf_op jit(solution)/shard_map/pool_sum/pallas_call | solution.py:52
  104.0 0.8 constant_dynamic-slice_fusion
  104.8 0.5 collective-permute-start.6
  105.4 1.7 collective-permute-done.4
  107.0 1.1 fusion.5
  108.1 1.2 collective-permute-start.5
  109.5 1.8 fusion.3
  111.3 5.3 %collective-permute-done.5 = bf16[1024,128]{1,0:T(8,128)(2,1)} collective-permute-done((bf16[1024,128]{1,0:T(8,128)(2,1)S(1)}, bf16[1024,128]{1,0:T(8,128)(2,1)}, u32[]{:S(2)}, u32[]{:S(2)}) %collective-permute-start.5) | collective-permute-done | bytes 262176 | tf_op jit(solution)/shard_map/ppermute | solution.py:333
  116.7 1.3 divide_convert_fusion
  118.2 1.5 collective-permute-done.8
  119.8 1.5 gather_fusion.1
  121.3 6.0 %all-to-all-start.3 = ((bf16[8,32,128]{2,1,0:T(8,128)(2,1)}), bf16[8,32,128]{2,1,0:T(8,128)(2,1)S(1)}, u32[]{:S(2)}, u32[]{:S(2)}) async-start(bf16[8,32,128]{2,1,0:T(8,128)(2,1)} %bitcast.26), calls=%async_computation.3 | async-start | bytes 131072 | tf_op jit(solution)/shard_map/all_to_all | solution.py:339
  127.3 2.7 %edge_gather.3.refs_2_ = f32[1024,128]{1,0:T(8,128)S(1)} custom-call(s32[1024]{0:T(1024)S(1)} %copy-done.25, s32[1024]{0:T(1024)S(1)} %copy-done.26, bf16[2048,128]{1,0:T(8,128)(2,1)S(1)} %pad_maximum_fusion.refs_2_, bf16[2,384,128]{2,1,0:T(8,128)(2,1)S(1)} %copy-done.4), custom_call_target="tpu_custom_call" | custom-call | tf_op jit(solution)/shard_map/edge_gather/pallas_call | solution.py:52
  130.0 4.2 %all-to-all-done.3 = bf16[8,32,128]{2,1,0:T(8,128)(2,1)S(1)} async-done(((bf16[8,32,128]{2,1,0:T(8,128)(2,1)}), bf16[8,32,128]{2,1,0:T(8,128)(2,1)S(1)}, u32[]{:S(2)}, u32[]{:S(2)}) %all-to-all-start.3) | async-done | bytes 65568 | tf_op jit(solution)/shard_map/all_to_all | solution.py:339
  134.2 4.6 %edge_message.3 = (f32[512,128]{1,0:T(8,128)S(1)}, f32[512,128]{1,0:T(8,128)S(1)}, bf16[512,128]{1,0:T(8,128)(2,1)}, bf16[512,128]{1,0:T(8,128)(2,1)S(1)}) custom-call(s32[1024]{0:T(1024)S(1)} %fusion.22.refs_0_, s32[8,128]{1,0:T(8,128)S(1)} %bitcast.25, f32[1024,128]{1,0:T(8,128)S(1)} %edge_gather.3.refs_2_, bf16[1024,128]{1,0:T(8,128)(2,1)S(1)} %copy-done.16, ...), custom_call_target="tpu_custom_call" | custom-call | tf_op jit(solution)/shard_map/edge_message/pallas_call | solution.py:52
  138.8 0.5 collective-permute-start.9
  139.3 0.8 collective-permute-done.10
  140.2 0.6 collective-permute-start.11
  140.8 1.0 fusion.6.refs_0_
  141.8 4.0 %collective-permute-done.11.refs_3_ = bf16[512,128]{1,0:T(8,128)(2,1)S(1)} collective-permute-done((bf16[512,128]{1,0:T(8,128)(2,1)S(1)}, bf16[512,128]{1,0:T(8,128)(2,1)S(1)}, u32[]{:S(2)}, u32[]{:S(2)}) %collective-permute-start.11) | collective-permute-done | bytes 131104 | tf_op jit(solution)/shard_map/ppermute | solution.py:333
  145.8 0.7 copy-done.30
  146.5 0.8 node_update.3
  147.3 0.9 broadcast_in_dim.2
  148.2 3.5 %all-to-all-start.4 = ((bf16[4,512,128]{2,1,0:T(8,128)(2,1)}), bf16[4,512,128]{2,1,0:T(8,128)(2,1)S(1)}, u32[]{:S(2)}, u32[]{:S(2)}) async-start(bf16[4,512,128]{2,1,0:T(8,128)(2,1)} %broadcast_in_dim.2), calls=%async_computation.4 | async-start | bytes 1048576 | tf_op jit(solution)/shard_map/all_to_all | solution.py:461
  151.7 1.1 copy-done.9
  152.8 10.5 %take_rows.3.refs_2_ = bf16[8192,128]{1,0:T(8,128)(2,1)S(1)} custom-call(s32[8192]{0:T(1024)S(1)} %fusion.17.refs_1_.refs_0_, bf16[3072,128]{1,0:T(8,128)(2,1)} %node_update.2.refs_1_, bf16[3072,128]{1,0:T(8,128)(2,1)S(1)} %collective-permute-done.3.refs_2_, bf16[3072,128]{1,0:T(8,128)(2,1)S(1)} %copy-done.9, bf16[3072,128]{1,0:T(8,128)(2,1)} %collective-permute-done.7.refs_4_), custom_call_target="tpu_custom_call" | custom-call | tf_op jit(solution)/shard_map/take_rows/pallas_call | solution.py:52
  163.3 2.6 %all-to-all-done.4 = bf16[4,512,128]{2,1,0:T(8,128)(2,1)S(1)} async-done(((bf16[4,512,128]{2,1,0:T(8,128)(2,1)}), bf16[4,512,128]{2,1,0:T(8,128)(2,1)S(1)}, u32[]{:S(2)}, u32[]{:S(2)}) %all-to-all-start.4) | async-done | bytes 524320 | tf_op jit(solution)/shard_map/all_to_all | solution.py:461
  165.8 0.5 collective-permute-start.13
  166.8 12.0 %collective-permute-done.13.refs_5_ = bf16[2048,128]{1,0:T(8,128)(2,1)S(1)} collective-permute-done((bf16[2048,128]{1,0:T(8,128)(2,1)S(1)}, bf16[2048,128]{1,0:T(8,128)(2,1)S(1)}, u32[]{:S(2)}, u32[]{:S(2)}) %collective-permute-start.13) | collective-permute-done | bytes 524320 | tf_op jit(solution)/shard_map/ppermute | solution.py:333
  178.8 0.5 collective-permute-start.15
  179.3 1.0 slice.12
  180.2 0.6 collective-permute-start.17
  180.8 1.1 collective-permute-start.14
  181.9 3.5 %collective-permute-done.15.refs_7_ = bf16[1024,128]{1,0:T(8,128)(2,1)S(1)} collective-permute-done((bf16[1024,128]{1,0:T(8,128)(2,1)S(1)}, bf16[1024,128]{1,0:T(8,128)(2,1)S(1)}, u32[]{:S(2)}, u32[]{:S(2)}) %collective-permute-start.15) | collective-permute-done | bytes 262176 | tf_op jit(solution)/shard_map/ppermute | solution.py:458
  185.5 3.8 %collective-permute-done.14.refs_6_ = bf16[1024,128]{1,0:T(8,128)(2,1)} collective-permute-done((bf16[1024,128]{1,0:T(8,128)(2,1)S(1)}, bf16[1024,128]{1,0:T(8,128)(2,1)}, u32[]{:S(2)}, u32[]{:S(2)}) %collective-permute-start.14) | collective-permute-done | bytes 262176 | tf_op jit(solution)/shard_map/ppermute | solution.py:333
  189.3 1.8 collective-permute-done.19.refs_11_
  191.1 12.4 %unpool.1 = (bf16[8192,128]{1,0:T(8,128)(2,1)}, bf16[2048,128]{1,0:T(8,128)(2,1)}) custom-call(s32[8192]{0:T(1024)S(1)} %copy-done.18, s32[4]{0:T(128)S(1)} %multiply_add_fusion.refs_1_, bf16[8192,128]{1,0:T(8,128)(2,1)S(1)} %take_rows.3.refs_2_, bf16[2048,128]{1,0:T(8,128)(2,1)S(1)} %bitcast.20, bf16[2048,128]{1,0:T(8,128)(2,1)} %collective-permute-done.12.refs_4_, ...), custom_call_target="tpu_custom_call" | custom-call | tf_op jit(solution)/shard_map/unpool/pallas_call | solution.py:52
  (111 shorter events, 1.5 us)
Async XLA Ops:
  0.6 48.6 %copy-start = (s32[1,8,1536]{2,1,0:T(8,128)S(1)}, s32[1,8,1536]{2,1,0:T(8,128)}, u32[]{:S(2)}) copy-start(s32[1,8,1536]{2,1,0:T(8,128)} %param.27) | copy-start | bytes 147460
  5.0 21.1 %all-to-all-start = ((bf16[8,64,128]{2,1,0:T(8,128)(2,1)}), bf16[8,64,128]{2,1,0:T(8,128)(2,1)S(1)}, u32[]{:S(2)}, u32[]{:S(2)}) async-start(bf16[8,64,128]{2,1,0:T(8,128)(2,1)} %bitcast.3), calls=%async_computation | async-start | bytes 262144 | tf_op jit(solution)/shard_map/all_to_all | solution.py:339
  12.3 1.6 copy-start.1
  13.9 0.9 copy-start.3
  14.8 0.7 copy-start.21
  15.5 0.7 copy-start.23
  16.2 9.7 %copy-start.19 = (s32[8192]{0:T(1024)S(1)}, s32[8192]{0:T(1024)}, u32[]{:S(2)}) copy-start(s32[8192]{0:T(1024)} %refs_1_.5) | copy-start | bytes 98308
  16.2 9.8 %copy-start.4 = (bf16[2,384,128]{2,1,0:T(8,128)(2,1)S(1)}, bf16[2,384,128]{2,1,0:T(8,128)(2,1)}, u32[]{:S(2)}) copy-start(bf16[2,384,128]{2,1,0:T(8,128)(2,1)} %refs_5_.4) | copy-start | bytes 589828
  16.2 9.8 %copy-start.7 = (bf16[4096,128]{1,0:T(8,128)(2,1)S(1)}, bf16[4096,128]{1,0:T(8,128)(2,1)}, u32[]{:S(2)}) copy-start(bf16[4096,128]{1,0:T(8,128)(2,1)} %refs_4_.3) | copy-start | bytes 3145732
  26.1 0.8 copy-start.12
  26.9 0.7 copy-start.22
  27.6 0.7 copy-start.24
  28.3 0.7 copy-start.27
  44.2 3.4 %copy-start.5 = (f32[3072,128]{1,0:T(8,128)}, f32[3072,128]{1,0:T(8,128)S(1)}, u32[]{:S(2)}) copy-start(f32[3072,128]{1,0:T(8,128)S(1)} %get-tuple-element.29.refs_1_) | copy-start | bytes 4718596
  44.2 5.0 %copy-start.33 = (s32[1,8,1536]{2,1,0:T(8,128)S(1)}, s32[1,8,1536]{2,1,0:T(8,128)}, u32[]{:S(2)}) copy-start(s32[1,8,1536]{2,1,0:T(8,128)} %param.28) | copy-start | bytes 147460
  44.2 11.6 %copy-start.2 = (bf16[8192,128]{1,0:T(8,128)(2,1)S(1)}, bf16[8192,128]{1,0:T(8,128)(2,1)}, u32[]{:S(2)}) copy-start(bf16[8192,128]{1,0:T(8,128)(2,1)} %refs_1_.4) | copy-start | bytes 6291460
  44.2 2.4 %collective-permute-start.1 = (bf16[3072,128]{1,0:T(8,128)(2,1)S(1)}, bf16[3072,128]{1,0:T(8,128)(2,1)S(1)}, u32[]{:S(2)}, u32[]{:S(2)}) collective-permute-start(bf16[3072,128]{1,0:T(8,128)(2,1)S(1)} %get-tuple-element.32), channel_id=1, source_target_pairs={{0,1},{1,0},{2,3},{3,2},{4,5},{5,4},{6,7},{7,6},{8,9},{9,8},{10,11... | collective-permute-start | bytes 2359304 | tf_op jit(solution)/shard_map/ppermute | solution.py:333
  44.3 15.3 %collective-permute-start = (bf16[3072,128]{1,0:T(8,128)(2,1)}, bf16[3072,128]{1,0:T(8,128)(2,1)S(1)}, u32[]{:S(2)}, u32[]{:S(2)}) collective-permute-start(bf16[3072,128]{1,0:T(8,128)(2,1)} %get-tuple-element.30), channel_id=1, source_target_pairs={{0,1},{1,0},{2,3},{3,2},{4,5},{5,4},{6,7},{7,6},{8,9},{9,8},{10,11... | collective-permute-start | bytes 2359304 | tf_op jit(solution)/shard_map/ppermute | solution.py:333
  47.6 20.0 %copy-start.10 = (bf16[2,256,128]{2,1,0:T(8,128)(2,1)S(1)}, bf16[2,256,128]{2,1,0:T(8,128)(2,1)}, u32[]{:S(2)}) copy-start(bf16[2,256,128]{2,1,0:T(8,128)(2,1)} %refs_4_.5) | copy-start | bytes 393220
  47.6 20.0 %copy-start.14 = (bf16[2,128,128]{2,1,0:T(8,128)(2,1)S(1)}, bf16[2,128,128]{2,1,0:T(8,128)(2,1)}, u32[]{:S(2)}) copy-start(bf16[2,128,128]{2,1,0:T(8,128)(2,1)} %refs_5_.5) | copy-start | bytes 196612
  47.6 20.0 %copy-start.29 = (f32[2,128]{1,0:T(2,128)S(1)}, f32[2,128]{1,0:T(2,128)}, u32[]{:S(2)}) copy-start(f32[2,128]{1,0:T(2,128)} %refs_6_.7) | copy-start | bytes 3076
  47.6 20.0 %collective-permute-start.2 = (bf16[3072,128]{1,0:T(8,128)(2,1)}, bf16[3072,128]{1,0:T(8,128)(2,1)}, u32[]{:S(2)}, u32[]{:S(2)}) collective-permute-start(bf16[3072,128]{1,0:T(8,128)(2,1)} %add_convert_fusion), channel_id=1, source_target_pairs={{0,2},{1,3},{2,0},{3,1},{4,6},{5,7},{6,4},{7,5},{8,10},{9,11},{10,... | collective-permute-start | bytes 2359304 | tf_op jit(solution)/shard_map/ppermute | solution.py:333
  49.9 23.4 %all-to-all-start.1 = ((s32[8,1,1536]{2,1,0:T(1,128)}), s32[8,1,1536]{2,1,0:T(1,128)S(1)}, u32[]{:S(2)}, u32[]{:S(2)}) async-start(s32[8,1,1536]{2,1,0:T(1,128)} %all_to_all.21), calls=%async_computation.1 | async-start | bytes 98304 | tf_op jit(solution)/shard_map/all_to_all | solution.py:399
  55.9 11.7 %copy-start.6 = (f32[3072,128]{1,0:T(8,128)S(1)}, f32[3072,128]{1,0:T(8,128)}, u32[]{:S(2)}) copy-start(f32[3072,128]{1,0:T(8,128)} %copy-done.5) | copy-start | bytes 4718596
  73.2 8.7 %copy-start.20 = (s32[8192]{0:T(1024)S(1)}, s32[8192]{0:T(1024)}, u32[]{:S(2)}) copy-start(s32[8192]{0:T(1024)} %refs_1_.5) | copy-start | bytes 98308
  73.3 6.0 %copy-start.35 = (s32[8,1,1536]{2,1,0:T(1,128)}, s32[8,1,1536]{2,1,0:T(1,128)S(1)}, u32[]{:S(2)}) copy-start(s32[8,1,1536]{2,1,0:T(1,128)S(1)} %all-to-all-done.1) | copy-start | bytes 147460
  73.3 26.0 %all-to-all-start.2 = ((bf16[8,384,128]{2,1,0:T(8,128)(2,1)}), bf16[8,384,128]{2,1,0:T(8,128)(2,1)S(1)}, u32[]{:S(2)}, u32[]{:S(2)}) async-start(bf16[8,384,128]{2,1,0:T(8,128)(2,1)} %bitcast.6), calls=%async_computation.2 | async-start | bytes 1572864 | tf_op jit(solution)/shard_map/all_to_all | solution.py:404
  79.3 25.5 %copy-start.34 = (s32[1,8,1536]{2,1,0:T(8,128)S(1)}, s32[1,8,1536]{2,1,0:T(8,128)}, u32[]{:S(2)}) copy-start(s32[1,8,1536]{2,1,0:T(8,128)} %param.28) | copy-start | bytes 147460
  79.3 20.0 %collective-permute-start.3 = (bf16[3072,128]{1,0:T(8,128)(2,1)}, bf16[3072,128]{1,0:T(8,128)(2,1)S(1)}, u32[]{:S(2)}, u32[]{:S(2)}) collective-permute-start(bf16[3072,128]{1,0:T(8,128)(2,1)} %node_update.2.refs_1_), channel_id=1, source_target_pairs={{0,2},{1,3},{2,0},{3,1},{4,6},{5,7},{6,4},{7,5},{8,10},{9,11},{10,... | collective-permute-start | bytes 2359304 | tf_op jit(solution)/shard_map/ppermute | solution.py:333
  98.7 0.6 copy-start.17
  99.3 10.1 %copy-start.36 = (s32[1,8,32]{2,1,0:T(8,128)S(1)}, s32[1,8,32]{2,1,0:T(8,128)}, u32[]{:S(2)}) copy-start(s32[1,8,32]{2,1,0:T(8,128)} %param.26) | copy-start | bytes 3076
  104.8 2.3 %collective-permute-start.4 = (f32[1024,128]{1,0:T(8,128)}, f32[1024,128]{1,0:T(8,128)}, u32[]{:S(2)}, u32[]{:S(2)}) collective-permute-start(f32[1024,128]{1,0:T(8,128)} %constant_dynamic-slice_fusion), channel_id=1, source_target_pairs={{0,1},{1,0},{2,3},{3,2},{4,5},{5,4},{6,7},{7,6},{8,9},{9,8},{10,11... | collective-permute-start | bytes 1572872 | tf_op jit(solution)/shard_map/ppermute | solution.py:333
  104.8 13.2 %collective-permute-start.6 = (bf16[3072,128]{1,0:T(8,128)(2,1)}, bf16[3072,128]{1,0:T(8,128)(2,1)S(1)}, u32[]{:S(2)}, u32[]{:S(2)}) collective-permute-start(bf16[3072,128]{1,0:T(8,128)(2,1)} %node_update.2.refs_1_), channel_id=1, source_target_pairs={{0,1},{1,0},{2,3},{3,2},{4,5},{5,4},{6,7},{7,6},{8,9},{9,8},{10,11... | collective-permute-start | bytes 2359304 | tf_op jit(solution)/shard_map/ppermute | solution.py:333
  105.3 12.7 %collective-permute-start.7 = (bf16[3072,128]{1,0:T(8,128)(2,1)S(1)}, bf16[3072,128]{1,0:T(8,128)(2,1)}, u32[]{:S(2)}, u32[]{:S(2)}) collective-permute-start(bf16[3072,128]{1,0:T(8,128)(2,1)S(1)} %collective-permute-done.3.refs_2_), channel_id=1, source_target_pairs={{0,1},{1,0},{2,3},{3,2},{4,5},{5,4},{6,7},{7,6},{8,9},{9,8},{10,11... | collective-permute-start | bytes 2359304 | tf_op jit(solution)/shard_map/ppermute | solution.py:333
  108.1 8.5 %collective-permute-start.5 = (bf16[1024,128]{1,0:T(8,128)(2,1)S(1)}, bf16[1024,128]{1,0:T(8,128)(2,1)}, u32[]{:S(2)}, u32[]{:S(2)}) collective-permute-start(bf16[1024,128]{1,0:T(8,128)(2,1)S(1)} %fusion.5), channel_id=1, source_target_pairs={{0,2},{1,3},{2,0},{3,1},{4,6},{5,7},{6,4},{7,5},{8,10},{9,11},{10,... | collective-permute-start | bytes 786440 | tf_op jit(solution)/shard_map/ppermute | solution.py:333
  111.3 16.0 %copy-start.26 = (s32[1024]{0:T(1024)S(1)}, s32[1024]{0:T(1024)}, u32[]{:S(2)}) copy-start(s32[1024]{0:T(1024)} %refs_1_.6) | copy-start | bytes 12292
  111.3 16.0 %copy-start.25 = (s32[1024]{0:T(1024)S(1)}, s32[1024]{0:T(1024)}, u32[]{:S(2)}) copy-start(s32[1024]{0:T(1024)} %refs_0_.5) | copy-start | bytes 12292
  118.0 16.1 %copy-start.13 = (bf16[2,128,128]{2,1,0:T(8,128)(2,1)S(1)}, bf16[2,128,128]{2,1,0:T(8,128)(2,1)}, u32[]{:S(2)}) copy-start(bf16[2,128,128]{2,1,0:T(8,128)(2,1)} %refs_6_.6) | copy-start | bytes 196612
  118.0 16.1 %copy-start.16 = (bf16[1024,128]{1,0:T(8,128)(2,1)S(1)}, bf16[1024,128]{1,0:T(8,128)(2,1)}, u32[]{:S(2)}) copy-start(bf16[1024,128]{1,0:T(8,128)(2,1)} %refs_3_.5) | copy-start | bytes 786436
  118.0 16.1 %copy-start.28 = (f32[2,128]{1,0:T(2,128)S(1)}, f32[2,128]{1,0:T(2,128)}, u32[]{:S(2)}) copy-start(f32[2,128]{1,0:T(2,128)} %refs_7_.3) | copy-start | bytes 3076
  118.0 20.7 %copy-start.8 = (bf16[3072,128]{1,0:T(8,128)(2,1)}, bf16[3072,128]{1,0:T(8,128)(2,1)S(1)}, u32[]{:S(2)}) copy-start(bf16[3072,128]{1,0:T(8,128)(2,1)S(1)} %collective-permute-done.6.refs_3_) | copy-start | bytes 2359300
  118.1 1.6 collective-permute-start.8
  119.7 7.5 %copy-start.31 = (bf16[1024,128]{1,0:T(8,128)(2,1)}, bf16[1024,128]{1,0:T(8,128)(2,1)S(1)}, u32[]{:S(2)}) copy-start(bf16[1024,128]{1,0:T(8,128)(2,1)S(1)} %get-tuple-element.50) | copy-start | bytes 786436
  119.7 7.5 %copy-start.32 = (bf16[1024,128]{1,0:T(8,128)(2,1)}, bf16[1024,128]{1,0:T(8,128)(2,1)S(1)}, u32[]{:S(2)}) copy-start(bf16[1024,128]{1,0:T(8,128)(2,1)S(1)} %get-tuple-element.51) | copy-start | bytes 786436
  119.8 26.0 %copy-start.11 = (bf16[2,256,128]{2,1,0:T(8,128)(2,1)S(1)}, bf16[2,256,128]{2,1,0:T(8,128)(2,1)}, u32[]{:S(2)}) copy-start(bf16[2,256,128]{2,1,0:T(8,128)(2,1)} %refs_4_.5) | copy-start | bytes 393220
  119.8 26.0 %copy-start.15 = (bf16[2,128,128]{2,1,0:T(8,128)(2,1)S(1)}, bf16[2,128,128]{2,1,0:T(8,128)(2,1)}, u32[]{:S(2)}) copy-start(bf16[2,128,128]{2,1,0:T(8,128)(2,1)} %refs_5_.5) | copy-start | bytes 196612
  121.3 12.9 %all-to-all-start.3 = ((bf16[8,32,128]{2,1,0:T(8,128)(2,1)}), bf16[8,32,128]{2,1,0:T(8,128)(2,1)S(1)}, u32[]{:S(2)}, u32[]{:S(2)}) async-start(bf16[8,32,128]{2,1,0:T(8,128)(2,1)} %bitcast.26), calls=%async_computation.3 | async-start | bytes 131072 | tf_op jit(solution)/shard_map/all_to_all | solution.py:339
  138.8 1.4 collective-permute-start.10
  138.8 3.0 %collective-permute-start.9 = (bf16[512,128]{1,0:T(8,128)(2,1)}, bf16[512,128]{1,0:T(8,128)(2,1)S(1)}, u32[]{:S(2)}, u32[]{:S(2)}) collective-permute-start(bf16[512,128]{1,0:T(8,128)(2,1)} %get-tuple-element.41), channel_id=1, source_target_pairs={{0,1},{1,0},{2,3},{3,2},{4,5},{5,4},{6,7},{7,6},{8,9},{9,8},{10,11... | collective-permute-start | bytes 393224 | tf_op jit(solution)/shard_map/ppermute | solution.py:333
  140.2 5.6 %collective-permute-start.11 = (bf16[512,128]{1,0:T(8,128)(2,1)S(1)}, bf16[512,128]{1,0:T(8,128)(2,1)S(1)}, u32[]{:S(2)}, u32[]{:S(2)}) collective-permute-start(bf16[512,128]{1,0:T(8,128)(2,1)S(1)} %add_convert_fusion.1), channel_id=1, source_target_pairs={{0,2},{1,3},{2,0},{3,1},{4,6},{5,7},{6,4},{7,5},{8,10},{9,11},{10,... | collective-permute-start | bytes 393224 | tf_op jit(solution)/shard_map/ppermute | solution.py:333
  145.8 0.7 copy-start.30
  148.2 17.7 %all-to-all-start.4 = ((bf16[4,512,128]{2,1,0:T(8,128)(2,1)}), bf16[4,512,128]{2,1,0:T(8,128)(2,1)S(1)}, u32[]{:S(2)}, u32[]{:S(2)}) async-start(bf16[4,512,128]{2,1,0:T(8,128)(2,1)} %broadcast_in_dim.2), calls=%async_computation.4 | async-start | bytes 1048576 | tf_op jit(solution)/shard_map/all_to_all | solution.py:461
  151.7 1.1 copy-start.9
  152.8 38.3 %copy-start.18 = (s32[8192]{0:T(1024)S(1)}, s32[8192]{0:T(1024)}, u32[]{:S(2)}) copy-start(s32[8192]{0:T(1024)} %copy-done.17) | copy-start | bytes 98308
  165.8 12.9 %collective-permute-start.13 = (bf16[2048,128]{1,0:T(8,128)(2,1)S(1)}, bf16[2048,128]{1,0:T(8,128)(2,1)S(1)}, u32[]{:S(2)}, u32[]{:S(2)}) collective-permute-start(bf16[2048,128]{1,0:T(8,128)(2,1)S(1)} %bitcast.17), channel_id=1, source_target_pairs={{0,2},{1,3},{2,0},{3,1},{4,6},{5,7},{6,4},{7,5},{8,10},{9,11},{10,... | collective-permute-start | bytes 1572872 | tf_op jit(solution)/shard_map/ppermute | solution.py:333
  166.4 12.9 %collective-permute-start.12 = (bf16[2048,128]{1,0:T(8,128)(2,1)S(1)}, bf16[2048,128]{1,0:T(8,128)(2,1)}, u32[]{:S(2)}, u32[]{:S(2)}) collective-permute-start(bf16[2048,128]{1,0:T(8,128)(2,1)S(1)} %bitcast.18), channel_id=1, source_target_pairs={{0,4},{4,0},{8,12},{12,8},{16,20},{20,16},{24,28},{28,24},{1,5},{5... | collective-permute-start | bytes 1572872 | tf_op jit(solution)/shard_map/ppermute | solution.py:458
  166.8 22.5 %collective-permute-start.16 = (bf16[2048,128]{1,0:T(8,128)(2,1)S(1)}, bf16[2048,128]{1,0:T(8,128)(2,1)}, u32[]{:S(2)}, u32[]{:S(2)}) collective-permute-start(bf16[2048,128]{1,0:T(8,128)(2,1)S(1)} %bitcast.19), channel_id=1, source_target_pairs={{0,1},{1,0},{2,3},{3,2},{4,5},{5,4},{6,7},{7,6},{8,9},{9,8},{10,11... | collective-permute-start | bytes 1572872 | tf_op jit(solution)/shard_map/ppermute | solution.py:333
  178.8 6.6 %collective-permute-start.15 = (bf16[1024,128]{1,0:T(8,128)(2,1)S(1)}, bf16[1024,128]{1,0:T(8,128)(2,1)S(1)}, u32[]{:S(2)}, u32[]{:S(2)}) collective-permute-start(bf16[1024,128]{1,0:T(8,128)(2,1)S(1)} %slice.13), channel_id=1, source_target_pairs={{0,4},{4,0},{8,12},{12,8},{16,20},{20,16},{24,28},{28,24},{1,5},{5... | collective-permute-start | bytes 786440 | tf_op jit(solution)/shard_map/ppermute | solution.py:458
  179.3 10.0 %collective-permute-start.18 = (bf16[2048,128]{1,0:T(8,128)(2,1)S(1)}, bf16[2048,128]{1,0:T(8,128)(2,1)}, u32[]{:S(2)}, u32[]{:S(2)}) collective-permute-start(bf16[2048,128]{1,0:T(8,128)(2,1)S(1)} %collective-permute-done.13.refs_5_), channel_id=1, source_target_pairs={{0,1},{1,0},{2,3},{3,2},{4,5},{5,4},{6,7},{7,6},{8,9},{9,8},{10,11... | collective-permute-start | bytes 1572872 | tf_op jit(solution)/shard_map/ppermute | solution.py:333
  180.2 9.0 %collective-permute-start.17 = (bf16[2048,128]{1,0:T(8,128)(2,1)}, bf16[2048,128]{1,0:T(8,128)(2,1)}, u32[]{:S(2)}, u32[]{:S(2)}) collective-permute-start(bf16[2048,128]{1,0:T(8,128)(2,1)} %collective-permute-done.12.refs_4_), channel_id=1, source_target_pairs={{0,1},{1,0},{2,3},{3,2},{4,5},{5,4},{6,7},{7,6},{8,9},{9,8},{10,11... | collective-permute-start | bytes 1572872 | tf_op jit(solution)/shard_map/ppermute | solution.py:333
  180.8 8.4 %collective-permute-start.14 = (bf16[1024,128]{1,0:T(8,128)(2,1)S(1)}, bf16[1024,128]{1,0:T(8,128)(2,1)}, u32[]{:S(2)}, u32[]{:S(2)}) collective-permute-start(bf16[1024,128]{1,0:T(8,128)(2,1)S(1)} %slice.12), channel_id=1, source_target_pairs={{0,2},{1,3},{2,0},{3,1},{4,6},{5,7},{6,4},{7,5},{8,10},{9,11},{10,... | collective-permute-start | bytes 786440 | tf_op jit(solution)/shard_map/ppermute | solution.py:333
  185.4 3.8 %collective-permute-start.20 = (bf16[1024,128]{1,0:T(8,128)(2,1)S(1)}, bf16[1024,128]{1,0:T(8,128)(2,1)}, u32[]{:S(2)}, u32[]{:S(2)}) collective-permute-start(bf16[1024,128]{1,0:T(8,128)(2,1)S(1)} %collective-permute-done.15.refs_7_), channel_id=1, source_target_pairs={{0,1},{1,0},{2,3},{3,2},{4,5},{5,4},{6,7},{7,6},{8,9},{9,8},{10,11... | collective-permute-start | bytes 786440 | tf_op jit(solution)/shard_map/ppermute | solution.py:333
  189.2 1.9 collective-permute-start.19

commit v3 on v2

v3 whole, which is shorter than its diff:
```python
import jax
import jax.numpy as jnp
from jax import lax
from jax.experimental import pallas as pl
from jax.experimental.pallas import tpu as pltpu
from jax.sharding import PartitionSpec as P


BF = jnp.bfloat16
F32 = jnp.float32
VMEM = pl.BlockSpec(memory_space=pltpu.VMEM)
SMEM = pl.BlockSpec(memory_space=pltpu.SMEM)
HBM = pl.BlockSpec(memory_space=pltpu.HBM)
INDEX = "index"
WEIGHT = "weight"
LOAD = "load"
LATE = (INDEX, WEIGHT, LOAD)
FULL = 60 * 1024 * 1024
COARSE = 2048
UNROLL = 32
ACCS = 4
CHUNKS = 1


def nbytes(x):
    width = -(-x.shape[-1] // 128) * 128
    return x.size // x.shape[-1] * width * x.dtype.itemsize


class Late:
    def __init__(self, source, ref, sems):
        self.ref = ref
        self.pieces = sems.shape[0]
        self.size = source.shape[0] // self.pieces
        self.copies = []
        for k in range(self.pieces):
            at = pl.ds(k * self.size, self.size)
            self.copies.append(pltpu.make_async_copy(source.at[at], ref.at[at], sems.at[k]))
            self.copies[-1].start()

    def wait(self):
        for copy in self.copies:
            copy.wait()

    def loop(self, body, unroll, after=None):
        for k, copy in enumerate(self.copies):
            copy.wait()

            def step(i, carry, start=k * self.size):
                for j in range(unroll):
                    body(start + i * unroll + j)
                return carry

            lax.fori_loop(0, self.size // unroll, step, 0)
            if after is not None:
                after(k, self.size)


def pieces_of(x, spec):
    return x.shape[0] // 2048 if spec in (INDEX, LOAD) and x.shape[0] % 2048 == 0 else 1


def call(kernel, out_shape, in_specs, scratch=(), out_specs=None, full=False):
    def run(*args):
        late = [k for k, spec in enumerate(in_specs) if spec in LATE]
        homes = [(pltpu.SMEM if in_specs[k] is INDEX else pltpu.VMEM)(args[k].shape, args[k].dtype) for k in late]
        sems = [pltpu.SemaphoreType.DMA((pieces_of(args[k], in_specs[k]),)) for k in late]
        used = sum(nbytes(x) for x, spec in zip(args, in_specs) if spec is not INDEX)
        used += sum(nbytes(x) for x in jax.tree.leaves(out_shape))
        used += sum(nbytes(x) for x in scratch if hasattr(x, "size"))
        n_out = len(jax.tree.leaves(out_shape))

        def body(*refs):
            ins, outs = list(refs[: len(args)]), refs[len(args) : len(args) + n_out]
            mine = refs[len(args) + n_out : len(args) + n_out + len(scratch)]
            rest = refs[len(args) + n_out + len(scratch) :]
            for at, k in enumerate(late):
                ins[k] = Late(ins[k], rest[at], rest[len(late) + at])
            kernel(*ins, *outs, *mine)

        return pl.pallas_call(
            body,
            out_shape=out_shape,
            in_specs=[HBM if spec in LATE else spec for spec in in_specs],
            out_specs=out_specs or jax.tree.map(lambda x: VMEM, out_shape),
            scratch_shapes=[pltpu.VMEM(x.shape, x.dtype) if hasattr(x, "size") else x for x in scratch]
            + homes
            + sems,
            compiler_params=pltpu.CompilerParams(vmem_limit_bytes=FULL if full else used + 2 * 1024 * 1024),
        )(*args)

    return run


def shaped(rows, dtype, width=128):
    return jax.ShapeDtypeStruct((rows, width), dtype)


def dot(a, b):
    return jnp.dot(a, b, preferred_element_type=F32)


def silu(v):
    return v / (1.0 + jnp.exp(-v))


def norm(values, gain):
    center = values - jnp.mean(values, axis=-1, keepdims=True)
    spread = jnp.mean(center * center, axis=-1, keepdims=True)
    return center * lax.rsqrt(spread + 1e-05) * gain


def chunk(total, size):
    return max(k for k in range(16, min(size, total) + 1, 16) if total % k == 0)


def blocks(total, size, body):
    size = min(size, total)

    def step(i, carry):
        body(pl.multiple_of(i * size, size))
        return carry

    lax.fori_loop(0, total // size, step, 0)


def edge_gather(nodes, senders, receivers, table, w_in, level, ghost_rows):
    rows, width = nodes.shape
    count = senders.shape[0]
    mapped = table is not None
    n = 128

    def kernel(send_idx, recv_idx, w_late, nodes_late, *refs):
        if mapped:
            table_late, lines_late, refs = refs[0], refs[1], refs[2:]
            out_ref, place_ref, send_tab, recv_tab, stage, places, sems = refs
        else:
            out_ref, send_tab, recv_tab, stage, sems = refs
        send_tab[pl.ds(rows, ghost_rows), :] = jnp.zeros((ghost_rows, width), F32)
        w_late.wait()
        w_s = w_late.ref[level, 0:width, :]
        w_r = w_late.ref[level, width : 2 * width, :]
        for k, copy in enumerate(nodes_late.copies):
            copy.wait()

            def project(at, start=k * nodes_late.size):
                block = nodes_late.ref[pl.ds(start + at, 512), :]
                send_tab[pl.ds(start + at, 512), :] = dot(block, w_s)
                recv_tab[pl.ds(start + at, 512), :] = dot(block, w_r)

            blocks(nodes_late.size, 512, project)
        if mapped:
            table_late.wait()
            lines_late.wait()
            high, low = digits(table_late.ref[...])
        send_idx.wait()
        copies = []
        for k, copy in enumerate(recv_idx.copies):
            copy.wait()
            start = k * recv_idx.size

            def gather(i, carry, start=start):
                base = start + i * n
                for j in range(n):
                    s = send_idx.ref[base + j]
                    r = recv_idx.ref[base + j]
                    stage[pl.ds(base + j, 1), :] = send_tab[pl.ds(s, 1), :] + recv_tab[pl.ds(r, 1), :]
                if mapped:
                    line = pl.ds(start // n + i, 1)
                    places[line, :] = look_up(high, low, lines_late.ref[line, :])
                return carry

            lax.fori_loop(0, recv_idx.size // n, gather, 0)
            spot = pl.ds(start, recv_idx.size)
            copies.append(pltpu.make_async_copy(stage.at[spot], out_ref.at[spot], sems.at[k]))
            copies[-1].start()
        if mapped:
            copies.append(pltpu.make_async_copy(places, place_ref, sems.at[recv_idx.pieces]))
            copies[-1].start()
        for copy in copies:
            copy.wait()

    any_space = pl.BlockSpec(memory_space=pl.ANY)
    sems = pltpu.SemaphoreType.DMA((pieces_of(receivers, INDEX) + 1,))
    scratch = [shaped(rows + ghost_rows, F32), shaped(rows, F32), shaped(count, F32)]
    args = (senders, receivers, w_in, nodes)
    specs = [INDEX, INDEX, WEIGHT, LOAD]
    if not mapped:
        return call(kernel, shaped(count, F32), specs, scratch + [sems], any_space, level == 0)(*args), None
    places = shaped(count // n, jnp.int32)
    pre, place = call(
        kernel,
        (shaped(count, F32), places),
        specs + [WEIGHT, WEIGHT],
        scratch + [places, sems],
        (any_space, any_space),
        True,
    )(*args, table.reshape(-1, 128), receivers.reshape(-1, 128))
    return pre, place.reshape(-1)


def edge_message(pre, edges, ghosts, senders, places, w_in, w_out, gain, level, rows, slots):
    count, width = pre.shape
    ghost_rows = ghosts.shape[0]
    fourth = slots // 4
    n = 256
    total = count // n

    def kernel(recv_idx, *refs):
        (send_late, w_late, wo_late, gain_late, pre_late, edge_late, ghost_late,
         k0_ref, k2_ref, s1_ref, s3_ref, even, odd, k0_st, k2_st, s1_st, s3_st) = refs[:17]
        accs, sems = refs[17:-1], refs[-1]

        room = chunk(slots, 512)

        def clear(at):
            for acc in accs:
                acc[pl.ds(at, room), :] = jnp.zeros((room, width), F32)

        blocks(slots, room, clear)
        send_late.wait()
        w_late.wait()
        wo_late.wait()
        gain_late.wait()
        pre_late.wait()
        edge_late.wait()
        ghost_late.wait()
        w_s = w_late.ref[level, 0:width, :]
        w_e = w_late.ref[level, 2 * width : 3 * width, :]
        w_o = wo_late.ref[level]
        scale = gain_late.ref[level : level + 1, :]

        def message(b, msg):
            at = pl.multiple_of(b * n, n)
            columns = []
            for k in range(n // 128):
                far = (send_late.ref[pl.ds(b * (n // 128) + k, 1), :] - rows).astype(F32)
                columns.append(jnp.broadcast_to(far, (8, 128)).T[:, 0:1])
            column = jnp.concatenate(columns, axis=0)
            lane = lax.broadcasted_iota(jnp.int32, (n, ghost_rows), 1).astype(F32)
            pick = (column == lane).astype(BF)
            picked = dot(pick, ghost_late.ref[...]).astype(BF)
            first = pre_late.ref[pl.ds(at, n), :] + (dot(picked, w_s) + dot(edge_late.ref[pl.ds(at, n), :], w_e))
            msg[...] = norm(dot(silu(first).astype(BF), w_o), scale)

        def scatter(b, msg):
            base = b * n
            for j in range(n):
                acc = accs[j % ACCS]
                r = recv_idx.ref[base + j]
                acc[pl.ds(r, 1), :] = acc[pl.ds(r, 1), :] + msg[pl.ds(j, 1), :]

        message(0, even)
        recv_idx.wait()

        def step(i, carry):
            b = 2 * i
            message(b + 1, odd)
            scatter(b, even)
            message(jnp.minimum(b + 2, total - 1), even)
            scatter(b + 1, odd)
            return carry

        lax.fori_loop(0, total // 2, step, 0)
        copies = []
        outs = ((3, s3_st, s3_ref), (1, k2_st, k2_ref), (2, s1_st, s1_ref), (0, k0_st, k0_ref))
        for k, (place, stage, out_ref) in enumerate(outs):
            m = chunk(fourth, 400)

            def body(at, stage=stage, start=place * fourth, m=m):
                value = accs[0][pl.ds(at + start, m), :]
                for acc in accs[1:]:
                    value = value + acc[pl.ds(at + start, m), :]
                stage[pl.ds(at, m), :] = value.astype(stage.dtype)

            blocks(fourth, m, body)
            copies.append(pltpu.make_async_copy(stage, out_ref, sems.at[k]))
            copies[-1].start()
        for copy in copies:
            copy.wait()

    outs = (shaped(fourth, F32), shaped(fourth, F32), shaped(fourth, BF), shaped(fourth, BF))
    return call(
        kernel,
        outs,
        [INDEX] + [WEIGHT] * 4 + [LOAD] * 3,
        [shaped(n, F32), shaped(n, F32), *outs]
        + [shaped(slots, F32)] * ACCS
        + [pltpu.SemaphoreType.DMA((4,))],
        (pl.BlockSpec(memory_space=pl.ANY),) * 4,
        level == 0,
    )(places, senders.reshape(-1, 128), w_in, w_out, gain, pre, edges, ghosts)


def node_update(rows, kept, first, second, w_in, w_out, gain, level):
    count, width = rows.shape
    n = chunk(count, 704)

    def kernel(rows_ref, kept_ref, first_ref, second_ref, w_ref, wo_ref, gain_ref, out_ref):
        own = rows_ref[...]
        total = (kept_ref[...] + first_ref[...].astype(F32) + second_ref[...].astype(F32)).astype(BF)
        hidden = silu(dot(own, w_ref[level, 0:width, :]) + dot(total, w_ref[level, width : 2 * width, :])).astype(BF)
        result = norm(dot(hidden, wo_ref[level]), gain_ref[level : level + 1, :])
        out_ref[...] = (own.astype(F32) + result).astype(BF)

    block = pl.BlockSpec((n, width), lambda i: (i, 0))
    return pl.pallas_call(
        kernel,
        grid=(count // n,),
        out_shape=shaped(count, BF),
        in_specs=[block] * 4
        + [pl.BlockSpec(x.shape, lambda i, d=x.ndim: (0,) * d) for x in (w_in, w_out, gain)],
        out_specs=block,
        name="node_update",
        compiler_params=pltpu.CompilerParams(vmem_limit_bytes=FULL if level == 0 else 8 * 1024 * 1024),
    )(rows, kept, first, second, w_in, w_out, gain)


def take_rows(tables, index):
    rows = sum(x.shape[0] for x in tables)
    count = index.shape[0]

    def kernel(index_late, *refs):
        refs, (out_ref, wide, picked) = refs[:-3], refs[-3:]
        start = 0
        for ref in refs:

            m = chunk(ref.shape[0], 400)

            def widen(at, ref=ref, start=start, m=m):
                wide[pl.ds(start + at, m), :] = ref[pl.ds(at, m), :].astype(F32)

            blocks(ref.shape[0], m, widen)
            start += ref.shape[0]

        def gather(j):
            picked[pl.ds(j, 1), :] = wide[pl.ds(index_late.ref[j], 1), :]

        index_late.loop(gather, UNROLL)

        def narrow(at):
            out_ref[pl.ds(at, 256), :] = picked[pl.ds(at, 256), :].astype(BF)

        blocks(count, 256, narrow)

    return call(
        kernel, shaped(count, BF), [INDEX] + [VMEM] * len(tables), [shaped(rows, F32), shaped(count, F32)]
    )(index, *tables)


def packed_rows(nodes, index, base, room):
    rows, width = nodes.shape
    n_dom, part = index.shape
    unroll = chunk(part, 32)

    def kernel(base_late, index_late, nodes_ref, out_ref, wide, picked):
        m = chunk(room + part, 512)

        def clear(at):
            picked[pl.ds(at, m), :] = jnp.zeros((m, width), F32)

        blocks(room + part, m, clear)

        def widen(at):
            wide[pl.ds(at, 256), :] = nodes_ref[pl.ds(at, 256), :].astype(F32)

        blocks(rows, 256, widen)
        base_late.wait()
        index_late.wait()

        def group(p, carry):
            start = base_late.ref[p]

            def gather(i, c):
                at = i * unroll
                for j in range(unroll):
                    picked[pl.ds(start + at + j, 1), :] = wide[pl.ds(index_late.ref[p * part + at + j], 1), :]
                return c

            return lax.fori_loop(0, part // unroll, gather, carry)

        lax.fori_loop(0, n_dom, group, 0)
        m = chunk(room, 400)

        def narrow(at, m=m):
            out_ref[pl.ds(at, m), :] = picked[pl.ds(at, m), :].astype(BF)

        blocks(room, m, narrow)

    return call(
        kernel, shaped(room, BF), [INDEX, INDEX, VMEM], [shaped(rows, F32), shaped(room + part, F32)]
    )(base, index.reshape(-1), nodes)


def expand(packed, base, part):
    room, width = packed.shape
    n_dom = base.shape[0]

    def kernel(base_late, packed_ref, out_ref, wide):
        wide[pl.ds(room, part), :] = jnp.zeros((part, width), F32)
        m = chunk(room, 400)

        def widen(at):
            wide[pl.ds(at, m), :] = packed_ref[pl.ds(at, m), :].astype(F32)

        blocks(room, m, widen)
        base_late.wait()

        def copy(p, carry):
            rows = wide[pl.ds(base_late.ref[p], part), :]
            out_ref[pl.ds(pl.multiple_of(p * part, 16), part), :] = rows.astype(BF)
            return carry

        lax.fori_loop(0, n_dom, copy, 0)

    return call(kernel, shaped(n_dom * part, BF), [INDEX, VMEM], [shaped(room + part, F32)])(base, packed)


def layout(unpool_slot, me, n_dom, span, room):
    lines = unpool_slot.shape[0] // 128

    def kernel(me_ref, slot_ref, place_ref, base_ref):
        here = me_ref[0]
        slot = slot_ref[...]
        owner = jnp.zeros_like(slot)
        for k in range(1, n_dom):
            owner = owner + (slot >= k * span).astype(jnp.int32)
        within = slot - owner * span
        quarter = within & 3
        place = jnp.zeros_like(slot)
        starts = [jnp.int32(0)] * 4
        for k in range(n_dom):
            mine = owner == k
            count = jnp.sum(mine.astype(F32)).astype(jnp.int32)
            base = jnp.int32(0)
            for e in range(4):
                place = jnp.where(mine & (quarter == e), starts[e], place)
                base = base + jnp.where(here == e, starts[e], 0)
                starts[e] = starts[e] + ((count - e + 3) >> 2)
            base_ref[k] = base
        rel = quarter ^ here
        place_ref[...] = ((rel & 1) * 2 + (rel >> 1)) * room + place + (within >> 2)

    place, base = pl.pallas_call(
        kernel,
        out_shape=(jax.ShapeDtypeStruct((lines, 128), jnp.int32), jax.ShapeDtypeStruct((n_dom,), jnp.int32)),
        in_specs=[SMEM, VMEM],
        out_specs=(VMEM, SMEM),
        name="layout",
        compiler_params=pltpu.CompilerParams(vmem_limit_bytes=8 * 1024 * 1024),
    )(me.reshape(1), unpool_slot.reshape(lines, 128))
    return place.reshape(-1), base


def digits(table):
    return (table >> 7).astype(F32).T.astype(BF), (table & 127).astype(F32).T.astype(BF)


def look_up(high, low, at):
    pick = (lax.broadcasted_iota(jnp.int32, (high.shape[1], 128), 0) == (at >> 7)).astype(BF)
    value = dot(high, pick) * 128.0 + dot(low, pick)
    lane = lax.broadcasted_iota(jnp.int32, (128, 128), 0) == (at & 127)
    return jnp.sum(jnp.where(lane, value, 0.0), axis=0, keepdims=True).astype(jnp.int32)


def resolve(table, index):
    lines = index.shape[0] // 128
    tall = table.shape[0] // 128

    def kernel(table_ref, index_ref, out_ref):
        high, low = digits(table_ref[...])

        def step(i, carry):
            for k in range(8):
                out_ref[pl.ds(i * 8 + k, 1), :] = look_up(high, low, index_ref[pl.ds(i * 8 + k, 1), :])
            return carry

        lax.fori_loop(0, lines // 8, step, 0)

    out = jax.ShapeDtypeStruct((lines, 128), jnp.int32)
    return call(kernel, out, [VMEM, VMEM], ())(table.reshape(tall, 128), index.reshape(lines, 128)).reshape(-1)


def pool_sum(arrived, places, bit):
    count, _ = arrived.shape
    n = 256
    half = COARSE // 2

    def kernel(bit_late, arrived_ref, places_late, mine_ref, theirs_ref):
        places_late.wait()
        bit_late.wait()
        rows = arrived_ref[...]
        for out_ref, start in ((theirs_ref, (1 - bit_late.ref[0]) * half), (mine_ref, bit_late.ref[0] * half)):

            def step(at, out_ref=out_ref, start=start):
                near = jnp.clip(places_late.ref[...] - (start + at), -1, n).astype(F32).astype(BF)
                row = lax.broadcasted_iota(jnp.int32, (n, count), 0).astype(F32).astype(BF)
                pick = jnp.where(near == row, jnp.ones((), BF), jnp.zeros((), BF))
                out_ref[pl.ds(at, n), :] = dot(pick, rows)

            blocks(half, n, step)

    return call(kernel, (shaped(half, F32), shaped(half, F32)), [INDEX, VMEM, WEIGHT], ())(
        bit.reshape(1), arrived, places.reshape(1, count)
    )


def child_count(places):
    high = (places // 128)[None, :] == jnp.arange(COARSE // 128, dtype=jnp.int32)[:, None]
    low = (places % 128)[:, None] == jnp.arange(128, dtype=jnp.int32)[None, :]
    return dot(high.astype(BF), low.astype(BF)).reshape(COARSE)


def swap(x, bit):
    size = lax.axis_size("edge")
    return lax.ppermute(x, "edge", [(i, i ^ bit) for i in range(size)])


def layer_sums(nodes, edges, senders, receivers, border, level, w, slots, table):
    rows, width = nodes.shape
    outgoing = nodes[border[0].reshape(-1)].reshape(border.shape[1], border.shape[2], width)
    arrived = lax.all_to_all(outgoing, "dom", split_axis=0, concat_axis=0, tiled=True)
    ghosts = arrived.reshape(-1, width)
    pre, places = edge_gather(nodes, senders, receivers, table, w[0], level, ghosts.shape[0])
    if table is None:
        me = lax.axis_index("edge")
        quarter = rows // 4
        places = order_of((receivers // quarter) ^ me) * quarter + receivers % quarter
    k0, k2, s1, s3 = edge_message(pre, edges, ghosts, senders, places, w[0], w[1], w[4], level, rows, slots)
    second = swap((k2 + swap(s3, 1).astype(F32)).astype(BF), 2)
    return k0, swap(s1, 1), second


def order_of(rel):
    return (rel & 1) * 2 + (rel >> 1)


def shards(
    fine_nodes,
    fine_edges,
    fine_senders,
    fine_receivers,
    fine_halo,
    coarse_edges,
    coarse_senders,
    coarse_receivers,
    coarse_halo,
    pool_send,
    pool_dest,
    unpool_slot,
    edge_in_weight,
    edge_out_weight,
    node_in_weight,
    node_out_weight,
    edge_gain,
    node_gain,
):
    w = (edge_in_weight, edge_out_weight, node_in_weight, node_out_weight, edge_gain, node_gain)
    width = fine_nodes.shape[-1]
    n_dom = pool_send.shape[1]
    span = pool_send.shape[2]
    part = span // 4
    me = lax.axis_index("edge")
    direct = n_dom == 8
    room = -(-(fine_nodes.shape[0] // 4 + n_dom) // 64) * 64
    slot_place, base = layout(unpool_slot, me, n_dom, span, room)

    def own_quarter(lists):
        return lax.dynamic_index_in_dim(lists[0].reshape(n_dom, part, 4), me, 2, keepdims=False)

    my_dest = own_quarter(pool_dest).reshape(-1)
    counts = child_count(pool_dest[0].reshape(-1))
    scale = jnp.maximum(counts, 1.0)[:, None]

    kept, first, second = layer_sums(
        fine_nodes, fine_edges, fine_senders, fine_receivers, fine_halo, 0, w, 4 * room, slot_place
    )
    sends, kept = lax.optimization_barrier((pool_send, kept))
    own = packed_rows(fine_nodes, own_quarter(sends), base, room)
    mid = node_update(own, kept, first, second, w[2], w[3], w[5], 0)
    if direct:
        mid_x = swap(mid, 2)
    spread = expand(mid, base, part)
    arrived = lax.all_to_all(spread.reshape(n_dom, part, width), "dom", split_axis=0, concat_axis=0, tiled=True)
    bit = me & 1
    half = COARSE // 2
    mine, theirs = pool_sum(arrived.reshape(-1, width), my_dest, bit)
    mine = mine + swap(theirs, 1)
    half_sum = mine.astype(BF)
    if direct:
        lists, half_sum = lax.optimization_barrier((pool_dest[0], half_sum))
    other = swap(half_sum, 2)
    if direct:
        known = lax.all_to_all(lists, "dom", 0, 0, tiled=True)
    mine = mine + other.astype(F32)
    mine = (mine / lax.dynamic_slice_in_dim(scale, bit * half, half, 0)).astype(BF)
    if direct:
        mine, mid, mid_1, mid_3, known = lax.optimization_barrier((mine, mid, swap(mid, 1), swap(mid_x, 1), known))
    theirs = swap(mine, 1)
    coarse_in = jnp.concatenate([jnp.where(bit == 0, mine, theirs), jnp.where(bit == 0, theirs, mine)], axis=0)

    kept, first, second = layer_sums(
        coarse_in, coarse_edges, coarse_senders, coarse_receivers, coarse_halo, 1, w, COARSE, None
    )
    fourth = COARSE // 4
    own = lax.dynamic_slice_in_dim(coarse_in, me * fourth, fourth, 0)
    top = node_update(own, kept, first, second, w[2], w[3], w[5], 1)
    if direct:
        return spread_out(top, [mid, mid_x, mid_1, mid_3], slot_place, known, unpool_slot)

    coarse_out = lax.all_gather(top, "edge", axis=0, tiled=True)
    parents = take_rows([coarse_out], jnp.minimum(my_dest, COARSE - 1))
    back = lax.all_to_all(parents.reshape(n_dom, part, width), "dom", split_axis=0, concat_axis=0, tiled=True)
    final = (spread.astype(F32) + back.reshape(-1, width).astype(F32)).astype(BF)
    final_x = swap(final, 2)
    within = unpool_slot % span
    place = order_of((within % 4) ^ me) * (n_dom * part) + (unpool_slot // span) * part + within // 4
    fine_out = take_rows([final, final_x, swap(final, 1), swap(final_x, 1)], place)
    return (fine_out, coarse_out)


def spot_of(rel, dy, z, row):
    fourth = COARSE // 4
    size = fourth // CHUNKS
    return (rel & 1) * (16 * fourth) + (row // size) * (16 * size) + ((rel >> 1) * 2 + dy) * (4 * size) + z * size + row % size


def place_of(known):
    me = lax.axis_index("edge")
    here = lax.axis_index("dom")
    fourth = COARSE // 4
    owner = jnp.arange(known.shape[0], dtype=jnp.int32).reshape((-1,) + (1,) * (known.ndim - 1))
    return spot_of((known // fourth) ^ me, (owner ^ here) & 1, owner >> 1, known % fourth).reshape(-1)


def spread_out(top, mids, slot_place, known, unpool_slot):
    fourth, width = top.shape
    size = fourth // CHUNKS
    me = lax.axis_index("edge")
    here = lax.axis_index("dom")
    groups = [[0, 2, 4, 6], [1, 3, 5, 7]]

    def cross(x):
        return lax.ppermute(x, "dom", [(i, i ^ 1) for i in range(8)])

    slot_place, known, _ = lax.optimization_barrier((slot_place, known, top))
    parent = resolve(place_of(known), unpool_slot)
    mid_rows = take_rows(mids, slot_place)
    lines = []
    for h in range(CHUNKS):
        copies = jnp.broadcast_to(top[None, h * size : (h + 1) * size], (4, size, width))
        line = lax.all_to_all(copies, "dom", 0, 0, tiled=True, axis_index_groups=groups)
        lines.append(line.reshape(4 * size, width))
    lines[-1], mid_rows, parent = lax.optimization_barrier((lines[-1], mid_rows, parent))
    pieces = []
    for line in lines:
        low, high = line[: 2 * size], line[2 * size :]
        low_y = cross(low)
        high_x = swap(high, 2)
        high_y = cross(high)
        low_x = swap(low, 2)
        pieces += [line, low_y, high_y, low_x, high_x, swap(low_y, 2), cross(high_x)]
    pieces = pieces + [swap(x, 1) for x in pieces]
    row = jnp.arange(CHUNKS, dtype=jnp.int32)[None, :] * size
    rel = jnp.arange(4, dtype=jnp.int32)[:, None] ^ me
    starts = spot_of(rel, 0, here >> 1, row).reshape(-1)
    return unpool(pieces, mid_rows, parent, starts, size)


def unpool(pieces, mid_rows, parent, starts, size):
    count, _ = mid_rows.shape
    total = sum(x.shape[0] for x in pieces)

    def kernel(parent_late, starts_late, mid_ref, *refs):
        refs, (out_ref, coarse_ref, wide, picked, stage, stage_c, sems) = refs[:-7], refs[-7:]
        start = 0
        for ref in refs:

            def widen(at, ref=ref, start=start):
                wide[pl.ds(start + at, 256), :] = ref[pl.ds(at, 256), :].astype(F32)

            blocks(ref.shape[0], 256, widen)
            start += ref.shape[0]
        starts_late.wait()
        for k in range(COARSE // size):
            rows = wide[pl.ds(pl.multiple_of(starts_late.ref[k], size), size), :]
            stage_c[k * size : (k + 1) * size, :] = rows.astype(BF)
        copies = [pltpu.make_async_copy(stage_c, coarse_ref, sems.at[parent_late.pieces])]
        copies[0].start()

        def gather(j):
            picked[pl.ds(j, 1), :] = wide[pl.ds(parent_late.ref[j], 1), :]

        def flush(k, rows):
            def narrow(at):
                spot = pl.ds(k * rows + at, 256)
                stage[spot, :] = (picked[spot, :] + mid_ref[spot, :].astype(F32)).astype(BF)

            blocks(rows, 256, narrow)
            spot = pl.ds(k * rows, rows)
            copies.append(pltpu.make_async_copy(stage.at[spot], out_ref.at[spot], sems.at[k]))
            copies[-1].start()

        parent_late.loop(gather, UNROLL, flush)
        for copy in copies:
            copy.wait()

    return call(
        kernel,
        (shaped(count, BF), shaped(COARSE, BF)),
        [INDEX, INDEX, VMEM] + [VMEM] * len(pieces),
        [
            shaped(total, F32),
            shaped(count, F32),
            shaped(count, BF),
            shaped(COARSE, BF),
            pltpu.SemaphoreType.DMA((pieces_of(parent, INDEX) + 1,)),
        ],
        (pl.BlockSpec(memory_space=pl.ANY), pl.BlockSpec(memory_space=pl.ANY)),
    )(parent, starts, mid_rows, *pieces)


def solution(mesh):
    placed = (
        P("dom", None),
        P(("dom", "edge"), None),
        P(("dom", "edge")),
        P(("dom", "edge")),
        P("dom", None, None),
        P(("dom", "edge"), None),
        P(("dom", "edge")),
        P(("dom", "edge")),
        P("dom", None, None),
        P("dom", None, None),
        P("dom", None, None),
        P("dom"),
        P(),
        P(),
        P(),
        P(),
        P(),
        P(),
    )

    return jax.shard_map(
        shards,
        mesh=mesh,
        in_specs=placed,
        out_specs=(P("dom", None), P("dom", None)),
        check_vma=False,
    )
```

time: 205 us -> 202 us (0.985)
  Pallas kernels: 86.5 us -> 73.7 us
  waiting for transfers between devices: 51 us -> 58.2 us
  local copies, waits for them, and re-layouts: 18.8 us -> 21.6 us
    ppermute x19 -> x22, waiting for transfers between devices: 40.7 us -> 23.5 us  [swap(): return lax.ppermute(x, 'edge', [(i, i ^ bit) for i in range(size)])]
    all_to_all x2, waiting for transfers between devices: 2.59 us -> 18 us  [the longest x1 18 us: shards(): lax.all_to_all(spread.reshape(n_dom, part, width), 'dom', split_axis=0, c...]
    pallas_call x11 -> x13, Pallas kernels: 86.5 us -> 73.7 us  [the longest x10 67.9 us: run(): pl.pallas_call(body, out_shape=out_shape, in_specs=[HBM if spec in LATE e...]
    all_to_all x1, waiting for transfers between devices: 0.01 us -> 4.93 us  [shards(): known = lax.all_to_all(lists, 'dom', 0, 0, tiled=True)]
    ppermute x2 -> x3, waiting for transfers between devices: 3.52 us -> 7.82 us  [cross(): return lax.ppermute(x, 'dom', [(i, i ^ 1) for i in range(8)])]
    all_to_all x1, starting transfers between devices: 6 us -> 3.5 us  [shards(): known = lax.all_to_all(lists, 'dom', 0, 0, tiled=True)]
    all_to_all x2, starting transfers between devices: 13.3 us -> 10.8 us  [layer_sums(): lax.all_to_all(outgoing, 'dom', split_axis=0, concat_axis=0, tiled=True)]
    ppermute x19 -> x22, starting transfers between devices: 8.93 us -> 11.2 us  [swap(): return lax.ppermute(x, 'edge', [(i, i ^ bit) for i in range(size)])]
  transfers between devices with their start and end apart: 26 -> 30, of which waited for: 13 -> 15; matrix products, arithmetic and copies ran while one was open for 4% -> 6% of each run, Pallas kernels for 24% -> 18%
where the time goes in v3:
time: 202 us; the launch traced here: 201 us
  Pallas kernels  73.7 us (36%)
  waiting for transfers between devices  58.2 us (29%)
  starting transfers between devices  37.4 us (19%)
  local copies, waits for them, and re-layouts  21.6 us (11%)
  other arithmetic  6.75 us (3%)
    pallas_call x10, Pallas kernels, run(): pl.pallas_call(body, out_shape=out_shape, in_specs=[HBM if spec in LATE e...  67.9 us
    ppermute x22, waiting for transfers between devices, swap(): return lax.ppermute(x, 'edge', [(i, i ^ bit) for i in range(size)])  23.5 us
    all_to_all x1, waiting for transfers between devices, shards(): lax.all_to_all(spread.reshape(n_dom, part, width), 'dom', split_axis=0, c...  18 us
    ppermute x22, starting transfers between devices, swap(): return lax.ppermute(x, 'edge', [(i, i ^ bit) for i in range(size)])  11.2 us
    all_to_all x2, starting transfers between devices, layer_sums(): lax.all_to_all(outgoing, 'dom', split_axis=0, concat_axis=0, tiled=True)  10.8 us
    unnamed x71, local copies, waits for them, and re-layouts  10.7 us
    ppermute x3, waiting for transfers between devices, cross(): return lax.ppermute(x, 'dom', [(i, i ^ 1) for i in range(8)])  7.82 us
    all_to_all x1, starting transfers between devices, shards(): lax.all_to_all(spread.reshape(n_dom, part, width), 'dom', split_axis=0, c...  6.01 us
  transfers between devices with their start and end apart: 30, of which 15 were waited for; matrix products, arithmetic and copies ran while one was open for 6% of the time, Pallas kernels for 18%

profile of v3, /device:TPU:0, one launch (start us, length us, event | category | flops | bytes accessed | tf_op | source)
XLA Modules:
  0.0 200.9 jit_solution(732144479080292059)
XLA Ops:
  0.6 0.8 reshape_squeeze.15
  1.4 3.5 %gather_fusion = bf16[512,128]{1,0:T(8,128)(2,1)} fusion(bf16[8192,128]{1,0:T(8,128)(2,1)} %refs_2_.7, s32[1024]{0:T(1024)S(1)} %pad_clamp_fusion.1), kind=kCustom, calls=%fused_computation | custom fusion | bytes 264192 | tf_op jit(solution)/shard_map/gather | solution.py:521
  4.9 7.3 %all-to-all-start = ((bf16[8,64,128]{2,1,0:T(8,128)(2,1)}), bf16[8,64,128]{2,1,0:T(8,128)(2,1)S(1)}, u32[]{:S(2)}, u32[]{:S(2)}) async-start(bf16[8,64,128]{2,1,0:T(8,128)(2,1)} %bitcast.7), calls=%async_computation | async-start | bytes 262144 | tf_op jit(solution)/shard_map/all_to_all | solution.py:522
  12.3 0.8 copy-done.20
  13.0 0.8 layout.1
  13.8 0.6 copy-done.18
  14.4 12.0 %shard_map.185 = (f32[4096,128]{1,0:T(8,128)}, s32[32,128]{1,0:T(8,128)}) custom-call(s32[4096]{0:T(1024)} %refs_0_.2, s32[4096]{0:T(1024)} %refs_1_.2, bf16[2,384,128]{2,1,0:T(8,128)(2,1)} %refs_2_.9, bf16[8192,128]{1,0:T(8,128)(2,1)} %refs_2_.7, s32[64,128]{1,0:T(8,128)} %copy-done.18, s32[32,128]{1,0:T(8,128)} %bitcast.48), custom_call_target="tpu_custom_call" | custom-call | tf_op jit(solution)/shard_map/pallas_call | solution.py:81
  26.4 0.6 copy-done.30
  27.1 14.7 %shard_map.186 = (f32[2112,128]{1,0:T(8,128)}, f32[2112,128]{1,0:T(8,128)}, bf16[2112,128]{1,0:T(8,128)(2,1)}, bf16[2112,128]{1,0:T(8,128)(2,1)}) custom-call(s32[4096]{0:T(1024)} %bitcast.51, s32[32,128]{1,0:T(8,128)} %bitcast.49, bf16[2,384,128]{2,1,0:T(8,128)(2,1)} %refs_2_.9, bf16[2,128,128]{2,1,0:T(8,128)(2,1)} %refs_3_.5, f32[2,128]{1,0:T(2,128)} %refs_4_.3, ...), custom_call_target="tpu_custom_call" | custom-call | tf_op jit(solution)/shard_map/pallas_call | solution.py:81
  42.4 1.6 collective-permute-done.1
  44.0 2.3 %add_convert_fusion = bf16[2112,128]{1,0:T(8,128)(2,1)} fusion(f32[2112,128]{1,0:T(8,128)} %get-tuple-element.38, bf16[2112,128]{1,0:T(8,128)(2,1)S(1)} %collective-permute-done.1), kind=kLoop, calls=%fused_computation.7 | loop fusion | flops 811008 | bytes 2162688 | tf_op jit(solution)/shard_map/convert_element_type | solution.py:530
  46.3 1.5 collective-permute-start.2
  48.1 1.2 copy.25
  49.2 2.2 %constant_dynamic-slice_fusion = (s32[8,384,1]{0,2,1:T(1,128)}, s32[8,384,1]{0,2,1:T(1,128)S(1)}) fusion(s32[8,384,4]{0,2,1:T(4,128)S(1)} %bitcast.42, s32[]{:T(128)S(6)} %select_n.101, s32[8,384,4]{0,2,1:T(4,128)} %bitcast.43), kind=kLoop, calls=%fused_computation.67 | loop fusion | bytes 49156 | tf_op jit(solution)/shard_map/jit(dynamic_index_in_dim)/dynamic_slice | solution.py:569
  51.5 3.8 %shard_map.187.rows_ref = bf16[2112,128]{1,0:T(8,128)(2,1)S(1)} custom-call(s32[8]{0:T(128)S(1)} %get-tuple-element.30.refs_0_, s32[3072]{0:T(1024)S(1)} %reshape.210.refs_1_, bf16[8192,128]{1,0:T(8,128)(2,1)S(1)} %copy-done), custom_call_target="tpu_custom_call" | custom-call | tf_op jit(solution)/shard_map/pallas_call | solution.py:81
  55.3 0.8 copy-done.4
  56.1 4.8 %collective-permute-done.2.second_ref = bf16[2112,128]{1,0:T(8,128)(2,1)} collective-permute-done((bf16[2112,128]{1,0:T(8,128)(2,1)}, bf16[2112,128]{1,0:T(8,128)(2,1)}, u32[]{:S(2)}, u32[]{:S(2)}) %collective-permute-start.2) | collective-permute-done | bytes 540704 | tf_op jit(solution)/shard_map/ppermute | solution.py:516
  61.0 4.5 %node_update.2.refs_1_ = bf16[2112,128]{1,0:T(8,128)(2,1)} custom-call(bf16[2112,128]{1,0:T(8,128)(2,1)} %copy-done.4, f32[2112,128]{1,0:T(8,128)} %get-tuple-element.36.kept_ref, bf16[2112,128]{1,0:T(8,128)(2,1)} %collective-permute-done.first_ref, bf16[2112,128]{1,0:T(8,128)(2,1)} %collective-permute-done.2.second_ref, bf16[2,256,128]{2,1,0:T(8,128)(2,1)} %w_ref.3, ...), custom_call_target="tpu_custom_call" | custom-call | tf_op jit(solution)/shard_map/node_update/pallas_call | solution.py:307
  65.4 1.0 copy-done.1
  66.5 1.5 shard_map.188
  68.0 6.0 %all-to-all-start.1 = ((bf16[8,384,128]{2,1,0:T(8,128)(2,1)}), bf16[8,384,128]{2,1,0:T(8,128)(2,1)S(1)}, u32[]{:S(2)}, u32[]{:S(2)}) async-start(bf16[8,384,128]{2,1,0:T(8,128)(2,1)} %bitcast.10), calls=%async_computation.1 | async-start | bytes 1572864 | tf_op jit(solution)/shard_map/all_to_all | solution.py:584
  74.1 1.6 collective-permute-start.6
  75.8 18.0 %all-to-all-done.1 = bf16[8,384,128]{2,1,0:T(8,128)(2,1)S(1)} async-done(((bf16[8,384,128]{2,1,0:T(8,128)(2,1)}), bf16[8,384,128]{2,1,0:T(8,128)(2,1)S(1)}, u32[]{:S(2)}, u32[]{:S(2)}) %all-to-all-start.1) | async-done | bytes 786464 | tf_op jit(solution)/shard_map/all_to_all | solution.py:584
  93.7 5.4 %shard_map.189 = (f32[1024,128]{1,0:T(8,128)S(1)}, f32[1024,128]{1,0:T(8,128)}) custom-call(s32[1]{0:T(128)} %bitcast.refs_0_, bf16[3072,128]{1,0:T(8,128)(2,1)S(1)} %bitcast.34, s32[1,3072]{1,0:T(1,128)S(1)} %bitcast.40), custom_call_target="tpu_custom_call" | custom-call | tf_op jit(solution)/shard_map/pallas_call | solution.py:81
  99.2 0.8 copy-done.11
  100.6 1.5 collective-permute-done.3
  102.1 0.8 copy-done.29
  102.9 2.0 fusion.26
  104.9 1.5 collective-permute-start.4
  106.5 0.7 all_to_all.22
  107.2 3.5 %all-to-all-start.2 = ((s32[8,1,1536]{2,1,0:T(1,128)}), s32[8,1,1536]{2,1,0:T(1,128)S(1)}, u32[]{:S(2)}, u32[]{:S(2)}) async-start(s32[8,1,1536]{2,1,0:T(1,128)} %all_to_all.22), calls=%async_computation.2 | async-start | bytes 98304 | tf_op jit(solution)/shard_map/all_to_all | solution.py:594
  110.7 1.8 fusion.3
  112.5 4.9 %all-to-all-done.2 = s32[8,1,1536]{2,1,0:T(1,128)S(1)} async-done(((s32[8,1,1536]{2,1,0:T(1,128)}), s32[8,1,1536]{2,1,0:T(1,128)S(1)}, u32[]{:S(2)}, u32[]{:S(2)}) %all-to-all-start.2) | async-done | bytes 49184 | tf_op jit(solution)/shard_map/all_to_all | solution.py:594
  117.5 1.2 divide_convert_fusion
  118.8 1.5 collective-permute-done.8
  120.5 1.5 gather_fusion.1
  121.9 3.5 %all-to-all-start.3 = ((bf16[8,32,128]{2,1,0:T(8,128)(2,1)}), bf16[8,32,128]{2,1,0:T(8,128)(2,1)S(1)}, u32[]{:S(2)}, u32[]{:S(2)}) async-start(bf16[8,32,128]{2,1,0:T(8,128)(2,1)} %bitcast.46), calls=%async_computation.3 | async-start | bytes 131072 | tf_op jit(solution)/shard_map/all_to_all | solution.py:522
  125.5 2.7 %shard_map.190.refs_5_ = f32[1024,128]{1,0:T(8,128)S(1)} custom-call(s32[1024]{0:T(1024)S(1)} %copy-done.22, s32[1024]{0:T(1024)S(1)} %copy-done.23, bf16[2,384,128]{2,1,0:T(8,128)(2,1)S(1)} %copy-done.3, bf16[2048,128]{1,0:T(8,128)(2,1)S(1)} %pad_maximum_fusion.refs_3_), custom_call_target="tpu_custom_call" | custom-call | tf_op jit(solution)/shard_map/pallas_call | solution.py:81
  128.2 3.9 %all-to-all-done.3 = bf16[8,32,128]{2,1,0:T(8,128)(2,1)S(1)} async-done(((bf16[8,32,128]{2,1,0:T(8,128)(2,1)}), bf16[8,32,128]{2,1,0:T(8,128)(2,1)S(1)}, u32[]{:S(2)}, u32[]{:S(2)}) %all-to-all-start.3) | async-done | bytes 65568 | tf_op jit(solution)/shard_map/all_to_all | solution.py:522
  132.1 4.9 %shard_map.191 = (f32[512,128]{1,0:T(8,128)S(1)}, f32[512,128]{1,0:T(8,128)S(1)}, bf16[512,128]{1,0:T(8,128)(2,1)}, bf16[512,128]{1,0:T(8,128)(2,1)S(1)}) custom-call(s32[1024]{0:T(1024)S(1)} %fusion.21.refs_0_, s32[8,128]{1,0:T(8,128)S(1)} %bitcast.41, bf16[2,384,128]{2,1,0:T(8,128)(2,1)S(1)} %copy-done.3, bf16[2,128,128]{2,1,0:T(8,128)(2,1)S(1)} %copy-done.17, ...), custom_call_target="tpu_custom_call" | custom-call | tf_op jit(solution)/shard_map/pallas_call | solution.py:81
  137.7 0.8 collective-permute-done.10
  138.5 0.6 collective-permute-start.11
  139.1 1.0 fusion.5.rows_ref
  140.1 4.0 %collective-permute-done.11.second_ref = bf16[512,128]{1,0:T(8,128)(2,1)S(1)} collective-permute-done((bf16[512,128]{1,0:T(8,128)(2,1)S(1)}, bf16[512,128]{1,0:T(8,128)(2,1)S(1)}, u32[]{:S(2)}, u32[]{:S(2)}) %collective-permute-start.11) | collective-permute-done | bytes 131104 | tf_op jit(solution)/shard_map/ppermute | solution.py:516
  144.7 0.9 broadcast_in_dim.2
  145.6 3.5 %all-to-all-start.4 = ((bf16[4,512,128]{2,1,0:T(8,128)(2,1)}), bf16[4,512,128]{2,1,0:T(8,128)(2,1)S(1)}, u32[]{:S(2)}, u32[]{:S(2)}) async-start(bf16[4,512,128]{2,1,0:T(8,128)(2,1)} %broadcast_in_dim.2), calls=%async_computation.4 | async-start | bytes 1048576 | tf_op jit(solution)/shard_map/all_to_all | solution.py:652
  149.2 2.5 %shard_map.193 = s32[64,128]{1,0:T(8,128)S(1)} custom-call(s32[96,128]{1,0:T(8,128)S(1)} %reshape_reshape.7.refs_0_, s32[64,128]{1,0:T(8,128)S(1)} %bitcast.39), custom_call_target="tpu_custom_call" | custom-call | tf_op jit(solution)/shard_map/pallas_call | solution.py:81
  151.7 1.0 copy-done.6
  152.8 1.0 copy-done.8
  153.8 1.0 copy-done.10
  154.9 8.6 %shard_map.192.refs_2_ = bf16[8192,128]{1,0:T(8,128)(2,1)S(1)} custom-call(s32[8192]{0:T(1024)S(1)} %bitcast.36, bf16[2112,128]{1,0:T(8,128)(2,1)S(1)} %copy-done.2, bf16[2112,128]{1,0:T(8,128)(2,1)S(1)} %copy-done.6, bf16[2112,128]{1,0:T(8,128)(2,1)S(1)} %copy-done.8, bf16[2112,128]{1,0:T(8,128)(2,1)S(1)} %copy-done.10), custom_call_target="tpu_custom_call" | custom-call | tf_op jit(solution)/shard_map/pallas_call | solution.py:81
  163.6 0.6 collective-permute-start.15
  164.6 1.6 collective-permute-start.12
  166.2 1.5 collective-permute-start.14
  167.7 5.1 %collective-permute-done.15.refs_7_ = bf16[1024,128]{1,0:T(8,128)(2,1)S(1)} collective-permute-done((bf16[1024,128]{1,0:T(8,128)(2,1)S(1)}, bf16[1024,128]{1,0:T(8,128)(2,1)S(1)}, u32[]{:S(2)}, u32[]{:S(2)}) %collective-permute-start.15) | collective-permute-done | bytes 262176 | tf_op jit(solution)/shard_map/ppermute | solution.py:516
  172.9 0.6 collective-permute-done.13.refs_5_
  173.9 5.2 %collective-permute-done.12.refs_4_ = bf16[1024,128]{1,0:T(8,128)(2,1)} collective-permute-done((bf16[1024,128]{1,0:T(8,128)(2,1)S(1)}, bf16[1024,128]{1,0:T(8,128)(2,1)}, u32[]{:S(2)}, u32[]{:S(2)}) %collective-permute-start.12) | collective-permute-done | bytes 262176 | tf_op jit(solution)/shard_map/ppermute | solution.py:644
  179.1 1.5 collective-permute-start.16
  181.1 0.7 copy-done.14
  181.9 2.0 collective-permute-done.17.refs_9_
  183.9 2.2 %collective-permute-done.16.refs_8_ = bf16[1024,128]{1,0:T(8,128)(2,1)} collective-permute-done((bf16[1024,128]{1,0:T(8,128)(2,1)}, bf16[1024,128]{1,0:T(8,128)(2,1)}, u32[]{:S(2)}, u32[]{:S(2)}) %collective-permute-start.16) | collective-permute-done | bytes 262176 | tf_op jit(solution)/shard_map/ppermute | solution.py:516
  186.2 1.8 collective-permute-done.23.refs_15_
  188.0 0.9 copy-done.15
  188.9 11.9 %shard_map.194 = (bf16[8192,128]{1,0:T(8,128)(2,1)}, bf16[2048,128]{1,0:T(8,128)(2,1)}) custom-call(s32[8192]{0:T(1024)S(1)} %bitcast.37, s32[4]{0:T(128)S(1)} %add_add_fusion.refs_1_, bf16[8192,128]{1,0:T(8,128)(2,1)S(1)} %shard_map.192.refs_2_, bf16[2048,128]{1,0:T(8,128)(2,1)S(1)} %bitcast.33, bf16[1024,128]{1,0:T(8,128)(2,1)} %collective-permute-done.12.refs_4_, ...), custom_call_target="tpu_custom_call" | custom-call | tf_op jit(solution)/shard_map/pallas_call | solution.py:81
  (112 shorter events, 4.9 us)
Async XLA Ops:
  4.9 21.5 %all-to-all-start = ((bf16[8,64,128]{2,1,0:T(8,128)(2,1)}), bf16[8,64,128]{2,1,0:T(8,128)(2,1)S(1)}, u32[]{:S(2)}, u32[]{:S(2)}) async-start(bf16[8,64,128]{2,1,0:T(8,128)(2,1)} %bitcast.7), calls=%async_computation | async-start | bytes 262144 | tf_op jit(solution)/shard_map/all_to_all | solution.py:522
  12.2 0.8 copy-start.20
  13.8 0.6 copy-start.18
  26.4 0.7 copy-start.30
  27.1 20.7 %copy-start.31 = (s32[1,8,1536]{2,1,0:T(8,128)S(1)}, s32[1,8,1536]{2,1,0:T(8,128)}, u32[]{:S(2)}) copy-start(s32[1,8,1536]{2,1,0:T(8,128)} %param.28) | copy-start | bytes 147460
  41.8 6.3 %copy-start.32 = (s32[1,8,1536]{2,1,0:T(8,128)S(1)}, s32[1,8,1536]{2,1,0:T(8,128)}, u32[]{:S(2)}) copy-start(s32[1,8,1536]{2,1,0:T(8,128)} %param.27) | copy-start | bytes 147460
  41.8 2.2 %collective-permute-start.1 = (bf16[2112,128]{1,0:T(8,128)(2,1)}, bf16[2112,128]{1,0:T(8,128)(2,1)S(1)}, u32[]{:S(2)}, u32[]{:S(2)}) collective-permute-start(bf16[2112,128]{1,0:T(8,128)(2,1)} %get-tuple-element.39), channel_id=1, source_target_pairs={{0,1},{1,0},{2,3},{3,2},{4,5},{5,4},{6,7},{7,6},{8,9},{9,8},{10,11... | collective-permute-start | bytes 1622024 | tf_op jit(solution)/shard_map/ppermute | solution.py:516
  41.9 14.2 %collective-permute-start = (bf16[2112,128]{1,0:T(8,128)(2,1)}, bf16[2112,128]{1,0:T(8,128)(2,1)}, u32[]{:S(2)}, u32[]{:S(2)}) collective-permute-start(bf16[2112,128]{1,0:T(8,128)(2,1)} %get-tuple-element.37), channel_id=1, source_target_pairs={{0,1},{1,0},{2,3},{3,2},{4,5},{5,4},{6,7},{7,6},{8,9},{9,8},{10,11... | collective-permute-start | bytes 1622024 | tf_op jit(solution)/shard_map/ppermute | solution.py:516
  44.0 7.5 %copy-start = (bf16[8192,128]{1,0:T(8,128)(2,1)S(1)}, bf16[8192,128]{1,0:T(8,128)(2,1)}, u32[]{:S(2)}) copy-start(bf16[8192,128]{1,0:T(8,128)(2,1)} %refs_2_.7) | copy-start | bytes 6291460
  46.3 14.6 %collective-permute-start.2 = (bf16[2112,128]{1,0:T(8,128)(2,1)}, bf16[2112,128]{1,0:T(8,128)(2,1)}, u32[]{:S(2)}, u32[]{:S(2)}) collective-permute-start(bf16[2112,128]{1,0:T(8,128)(2,1)} %add_convert_fusion), channel_id=1, source_target_pairs={{0,2},{1,3},{2,0},{3,1},{4,6},{5,7},{6,4},{7,5},{8,10},{9,11},{10,... | collective-permute-start | bytes 1622024 | tf_op jit(solution)/shard_map/ppermute | solution.py:516
  55.3 0.8 copy-start.4
  65.4 1.0 copy-start.1
  66.5 7.6 %copy-start.2 = (bf16[2112,128]{1,0:T(8,128)(2,1)S(1)}, bf16[2112,128]{1,0:T(8,128)(2,1)}, u32[]{:S(2)}) copy-start(bf16[2112,128]{1,0:T(8,128)(2,1)} %node_update.2.refs_1_) | copy-start | bytes 1622020
  66.5 9.2 %copy-start.28 = (s32[8,384,1]{0,2,1:T(1,128)S(1)}, s32[8,384,1]{0,2,1:T(1,128)}, u32[]{:S(2)}) copy-start(s32[8,384,1]{0,2,1:T(1,128)} %get-tuple-element.66) | copy-start | bytes 36868
  68.0 38.4 %copy-start.33 = (s32[1,8,32]{2,1,0:T(8,128)S(1)}, s32[1,8,32]{2,1,0:T(8,128)}, u32[]{:S(2)}) copy-start(s32[1,8,32]{2,1,0:T(8,128)} %param.26) | copy-start | bytes 3076
  68.0 25.7 %all-to-all-start.1 = ((bf16[8,384,128]{2,1,0:T(8,128)(2,1)}), bf16[8,384,128]{2,1,0:T(8,128)(2,1)S(1)}, u32[]{:S(2)}, u32[]{:S(2)}) async-start(bf16[8,384,128]{2,1,0:T(8,128)(2,1)} %bitcast.10), calls=%async_computation.1 | async-start | bytes 1572864 | tf_op jit(solution)/shard_map/all_to_all | solution.py:584
  74.1 26.4 %collective-permute-start.6 = (bf16[2112,128]{1,0:T(8,128)(2,1)S(1)}, bf16[2112,128]{1,0:T(8,128)(2,1)S(1)}, u32[]{:S(2)}, u32[]{:S(2)}) collective-permute-start(bf16[2112,128]{1,0:T(8,128)(2,1)S(1)} %copy-done.2), channel_id=1, source_target_pairs={{0,2},{1,3},{2,0},{3,1},{4,6},{5,7},{6,4},{7,5},{8,10},{9,11},{10,... | collective-permute-start | bytes 1622024 | tf_op jit(solution)/shard_map/ppermute | solution.py:516
  99.2 0.8 copy-start.11
  100.0 2.1 %collective-permute-start.3 = (f32[1024,128]{1,0:T(8,128)}, f32[1024,128]{1,0:T(8,128)S(1)}, u32[]{:S(2)}, u32[]{:S(2)}) collective-permute-start(f32[1024,128]{1,0:T(8,128)} %get-tuple-element.41), channel_id=1, source_target_pairs={{0,1},{1,0},{2,3},{3,2},{4,5},{5,4},{6,7},{7,6},{8,9},{9,8},{10,11... | collective-permute-start | bytes 1572872 | tf_op jit(solution)/shard_map/ppermute | solution.py:516
  100.0 18.7 %collective-permute-start.5 = (bf16[2112,128]{1,0:T(8,128)(2,1)S(1)}, bf16[2112,128]{1,0:T(8,128)(2,1)S(1)}, u32[]{:S(2)}, u32[]{:S(2)}) collective-permute-start(bf16[2112,128]{1,0:T(8,128)(2,1)S(1)} %copy-done.2), channel_id=1, source_target_pairs={{0,1},{1,0},{2,3},{3,2},{4,5},{5,4},{6,7},{7,6},{8,9},{9,8},{10,11... | collective-permute-start | bytes 1622024 | tf_op jit(solution)/shard_map/ppermute | solution.py:516
  100.5 12.0 %copy-start.5 = (bf16[2112,128]{1,0:T(8,128)(2,1)}, bf16[2112,128]{1,0:T(8,128)(2,1)S(1)}, u32[]{:S(2)}) copy-start(bf16[2112,128]{1,0:T(8,128)(2,1)S(1)} %collective-permute-done.6.refs_2_) | copy-start | bytes 1622020
  100.5 18.2 %collective-permute-start.7 = (bf16[2112,128]{1,0:T(8,128)(2,1)S(1)}, bf16[2112,128]{1,0:T(8,128)(2,1)S(1)}, u32[]{:S(2)}, u32[]{:S(2)}) collective-permute-start(bf16[2112,128]{1,0:T(8,128)(2,1)S(1)} %collective-permute-done.6.refs_2_), channel_id=1, source_target_pairs={{0,1},{1,0},{2,3},{3,2},{4,5},{5,4},{6,7},{7,6},{8,9},{9,8},{10,11... | collective-permute-start | bytes 1622024 | tf_op jit(solution)/shard_map/ppermute | solution.py:516
  102.1 0.8 copy-start.29
  104.9 12.6 %collective-permute-start.4 = (bf16[1024,128]{1,0:T(8,128)(2,1)}, bf16[1024,128]{1,0:T(8,128)(2,1)}, u32[]{:S(2)}, u32[]{:S(2)}) collective-permute-start(bf16[1024,128]{1,0:T(8,128)(2,1)} %get-tuple-element.42), channel_id=1, source_target_pairs={{0,2},{1,3},{2,0},{3,1},{4,6},{5,7},{6,4},{7,5},{8,10},{9,11},{10,... | collective-permute-start | bytes 786440 | tf_op jit(solution)/shard_map/ppermute | solution.py:516
  107.2 10.3 %all-to-all-start.2 = ((s32[8,1,1536]{2,1,0:T(1,128)}), s32[8,1,1536]{2,1,0:T(1,128)S(1)}, u32[]{:S(2)}, u32[]{:S(2)}) async-start(s32[8,1,1536]{2,1,0:T(1,128)} %all_to_all.22), calls=%async_computation.2 | async-start | bytes 98304 | tf_op jit(solution)/shard_map/all_to_all | solution.py:594
  112.5 13.0 %copy-start.23 = (s32[1024]{0:T(1024)S(1)}, s32[1024]{0:T(1024)}, u32[]{:S(2)}) copy-start(s32[1024]{0:T(1024)} %refs_1_.3) | copy-start | bytes 12292
  112.5 13.0 %copy-start.3 = (bf16[2,384,128]{2,1,0:T(8,128)(2,1)S(1)}, bf16[2,384,128]{2,1,0:T(8,128)(2,1)}, u32[]{:S(2)}) copy-start(bf16[2,384,128]{2,1,0:T(8,128)(2,1)} %refs_2_.9) | copy-start | bytes 589828
  112.5 13.0 %copy-start.22 = (s32[1024]{0:T(1024)S(1)}, s32[1024]{0:T(1024)}, u32[]{:S(2)}) copy-start(s32[1024]{0:T(1024)} %refs_0_.3) | copy-start | bytes 12292
  118.6 13.5 %copy-start.13 = (bf16[1024,128]{1,0:T(8,128)(2,1)S(1)}, bf16[1024,128]{1,0:T(8,128)(2,1)}, u32[]{:S(2)}) copy-start(bf16[1024,128]{1,0:T(8,128)(2,1)} %refs_6_.3) | copy-start | bytes 786436
  118.7 13.5 %copy-start.17 = (bf16[2,128,128]{2,1,0:T(8,128)(2,1)S(1)}, bf16[2,128,128]{2,1,0:T(8,128)(2,1)}, u32[]{:S(2)}) copy-start(bf16[2,128,128]{2,1,0:T(8,128)(2,1)} %refs_3_.5) | copy-start | bytes 196612
  118.7 13.5 %copy-start.25 = (f32[2,128]{1,0:T(2,128)S(1)}, f32[2,128]{1,0:T(2,128)}, u32[]{:S(2)}) copy-start(f32[2,128]{1,0:T(2,128)} %refs_4_.3) | copy-start | bytes 3076
  118.7 18.4 %copy-start.7 = (bf16[2112,128]{1,0:T(8,128)(2,1)}, bf16[2112,128]{1,0:T(8,128)(2,1)S(1)}, u32[]{:S(2)}) copy-start(bf16[2112,128]{1,0:T(8,128)(2,1)S(1)} %collective-permute-done.5.refs_3_) | copy-start | bytes 1622020
  118.7 18.4 %copy-start.9 = (bf16[2112,128]{1,0:T(8,128)(2,1)}, bf16[2112,128]{1,0:T(8,128)(2,1)S(1)}, u32[]{:S(2)}) copy-start(bf16[2112,128]{1,0:T(8,128)(2,1)S(1)} %collective-permute-done.7.refs_4_) | copy-start | bytes 1622020
  118.7 1.6 collective-permute-start.8
  120.4 5.1 %copy-start.26 = (bf16[1024,128]{1,0:T(8,128)(2,1)}, bf16[1024,128]{1,0:T(8,128)(2,1)S(1)}, u32[]{:S(2)}) copy-start(bf16[1024,128]{1,0:T(8,128)(2,1)S(1)} %get-tuple-element.62) | copy-start | bytes 786436
  120.4 5.1 %copy-start.27 = (bf16[1024,128]{1,0:T(8,128)(2,1)}, bf16[1024,128]{1,0:T(8,128)(2,1)S(1)}, u32[]{:S(2)}) copy-start(bf16[1024,128]{1,0:T(8,128)(2,1)S(1)} %get-tuple-element.63) | copy-start | bytes 786436
  120.4 23.7 %copy-start.12 = (bf16[2,256,128]{2,1,0:T(8,128)(2,1)S(1)}, bf16[2,256,128]{2,1,0:T(8,128)(2,1)}, u32[]{:S(2)}) copy-start(bf16[2,256,128]{2,1,0:T(8,128)(2,1)} %w_ref.3) | copy-start | bytes 393220
  120.4 23.7 %copy-start.16 = (bf16[2,128,128]{2,1,0:T(8,128)(2,1)S(1)}, bf16[2,128,128]{2,1,0:T(8,128)(2,1)}, u32[]{:S(2)}) copy-start(bf16[2,128,128]{2,1,0:T(8,128)(2,1)} %wo_ref.3) | copy-start | bytes 196612
  120.5 23.7 %copy-start.24 = (f32[2,128]{1,0:T(2,128)S(1)}, f32[2,128]{1,0:T(2,128)}, u32[]{:S(2)}) copy-start(f32[2,128]{1,0:T(2,128)} %gain_ref.3) | copy-start | bytes 3076
  121.9 10.2 %all-to-all-start.3 = ((bf16[8,32,128]{2,1,0:T(8,128)(2,1)}), bf16[8,32,128]{2,1,0:T(8,128)(2,1)S(1)}, u32[]{:S(2)}, u32[]{:S(2)}) async-start(bf16[8,32,128]{2,1,0:T(8,128)(2,1)} %bitcast.46), calls=%async_computation.3 | async-start | bytes 131072 | tf_op jit(solution)/shard_map/all_to_all | solution.py:522
  137.1 12.1 %copy-start.21 = (s32[8192]{0:T(1024)S(1)}, s32[8192]{0:T(1024)}, u32[]{:S(2)}) copy-start(s32[8192]{0:T(1024)} %param.29) | copy-start | bytes 98308
  137.1 1.4 collective-permute-start.10
  137.2 3.0 %collective-permute-start.9 = (bf16[512,128]{1,0:T(8,128)(2,1)}, bf16[512,128]{1,0:T(8,128)(2,1)S(1)}, u32[]{:S(2)}, u32[]{:S(2)}) collective-permute-start(bf16[512,128]{1,0:T(8,128)(2,1)} %get-tuple-element.46), channel_id=1, source_target_pairs={{0,1},{1,0},{2,3},{3,2},{4,5},{5,4},{6,7},{7,6},{8,9},{9,8},{10,11... | collective-permute-start | bytes 393224 | tf_op jit(solution)/shard_map/ppermute | solution.py:516
  138.5 13.2 %copy-start.19 = (s32[64,128]{1,0:T(8,128)S(1)}, s32[64,128]{1,0:T(8,128)}, u32[]{:S(2)}) copy-start(s32[64,128]{1,0:T(8,128)} %copy-done.18) | copy-start | bytes 98308
  138.5 5.6 %collective-permute-start.11 = (bf16[512,128]{1,0:T(8,128)(2,1)S(1)}, bf16[512,128]{1,0:T(8,128)(2,1)S(1)}, u32[]{:S(2)}, u32[]{:S(2)}) collective-permute-start(bf16[512,128]{1,0:T(8,128)(2,1)S(1)} %add_convert_fusion.1), channel_id=1, source_target_pairs={{0,2},{1,3},{2,0},{3,1},{4,6},{5,7},{6,4},{7,5},{8,10},{9,11},{10,... | collective-permute-start | bytes 393224 | tf_op jit(solution)/shard_map/ppermute | solution.py:516
  145.6 17.9 %all-to-all-start.4 = ((bf16[4,512,128]{2,1,0:T(8,128)(2,1)}), bf16[4,512,128]{2,1,0:T(8,128)(2,1)S(1)}, u32[]{:S(2)}, u32[]{:S(2)}) async-start(bf16[4,512,128]{2,1,0:T(8,128)(2,1)} %broadcast_in_dim.2), calls=%async_computation.4 | async-start | bytes 1048576 | tf_op jit(solution)/shard_map/all_to_all | solution.py:652
  151.7 1.1 copy-start.6
  152.8 1.0 copy-start.8
  153.8 1.0 copy-start.10
  163.5 17.1 %collective-permute-start.18 = (bf16[2048,128]{1,0:T(8,128)(2,1)S(1)}, bf16[2048,128]{1,0:T(8,128)(2,1)S(1)}, u32[]{:S(2)}, u32[]{:S(2)}) collective-permute-start(bf16[2048,128]{1,0:T(8,128)(2,1)S(1)} %bitcast.32), channel_id=1, source_target_pairs={{0,1},{1,0},{2,3},{3,2},{4,5},{5,4},{6,7},{7,6},{8,9},{9,8},{10,11... | collective-permute-start | bytes 1572872 | tf_op jit(solution)/shard_map/ppermute | solution.py:516
  163.6 9.2 %collective-permute-start.15 = (bf16[1024,128]{1,0:T(8,128)(2,1)S(1)}, bf16[1024,128]{1,0:T(8,128)(2,1)S(1)}, u32[]{:S(2)}, u32[]{:S(2)}) collective-permute-start(bf16[1024,128]{1,0:T(8,128)(2,1)S(1)} %get-tuple-element.60), channel_id=1, source_target_pairs={{0,2},{1,3},{2,0},{3,1},{4,6},{5,7},{6,4},{7,5},{8,10},{9,11},{10,... | collective-permute-start | bytes 786440 | tf_op jit(solution)/shard_map/ppermute | solution.py:516
  164.2 9.3 %collective-permute-start.13 = (bf16[1024,128]{1,0:T(8,128)(2,1)S(1)}, bf16[1024,128]{1,0:T(8,128)(2,1)}, u32[]{:S(2)}, u32[]{:S(2)}) collective-permute-start(bf16[1024,128]{1,0:T(8,128)(2,1)S(1)} %get-tuple-element.60), channel_id=1, source_target_pairs={{0,4},{4,0},{8,12},{12,8},{16,20},{20,16},{24,28},{28,24},{1,5},{5... | collective-permute-start | bytes 786440 | tf_op jit(solution)/shard_map/ppermute | solution.py:644
  164.6 14.5 %collective-permute-start.12 = (bf16[1024,128]{1,0:T(8,128)(2,1)S(1)}, bf16[1024,128]{1,0:T(8,128)(2,1)}, u32[]{:S(2)}, u32[]{:S(2)}) collective-permute-start(bf16[1024,128]{1,0:T(8,128)(2,1)S(1)} %get-tuple-element.61), channel_id=1, source_target_pairs={{0,4},{4,0},{8,12},{12,8},{16,20},{20,16},{24,28},{28,24},{1,5},{5... | collective-permute-start | bytes 786440 | tf_op jit(solution)/shard_map/ppermute | solution.py:644
  166.2 14.4 %collective-permute-start.14 = (bf16[1024,128]{1,0:T(8,128)(2,1)S(1)}, bf16[1024,128]{1,0:T(8,128)(2,1)}, u32[]{:S(2)}, u32[]{:S(2)}) collective-permute-start(bf16[1024,128]{1,0:T(8,128)(2,1)S(1)} %get-tuple-element.61), channel_id=1, source_target_pairs={{0,2},{1,3},{2,0},{3,1},{4,6},{5,7},{6,4},{7,5},{8,10},{9,11},{10,... | collective-permute-start | bytes 786440 | tf_op jit(solution)/shard_map/ppermute | solution.py:516
  172.9 8.3 %collective-permute-start.22 = (bf16[1024,128]{1,0:T(8,128)(2,1)S(1)}, bf16[1024,128]{1,0:T(8,128)(2,1)S(1)}, u32[]{:S(2)}, u32[]{:S(2)}) collective-permute-start(bf16[1024,128]{1,0:T(8,128)(2,1)S(1)} %collective-permute-done.15.refs_7_), channel_id=1, source_target_pairs={{0,1},{1,0},{2,3},{3,2},{4,5},{5,4},{6,7},{7,6},{8,9},{9,8},{10,11... | collective-permute-start | bytes 786440 | tf_op jit(solution)/shard_map/ppermute | solution.py:516
  173.5 10.4 %collective-permute-start.17 = (bf16[1024,128]{1,0:T(8,128)(2,1)S(1)}, bf16[1024,128]{1,0:T(8,128)(2,1)}, u32[]{:S(2)}, u32[]{:S(2)}) collective-permute-start(bf16[1024,128]{1,0:T(8,128)(2,1)S(1)} %collective-permute-done.15.refs_7_), channel_id=1, source_target_pairs={{0,4},{4,0},{8,12},{12,8},{16,20},{20,16},{24,28},{28,24},{1,5},{5... | collective-permute-start | bytes 786440 | tf_op jit(solution)/shard_map/ppermute | solution.py:644
  179.1 7.0 %collective-permute-start.16 = (bf16[1024,128]{1,0:T(8,128)(2,1)}, bf16[1024,128]{1,0:T(8,128)(2,1)}, u32[]{:S(2)}, u32[]{:S(2)}) collective-permute-start(bf16[1024,128]{1,0:T(8,128)(2,1)} %collective-permute-done.12.refs_4_), channel_id=1, source_target_pairs={{0,2},{1,3},{2,0},{3,1},{4,6},{5,7},{6,4},{7,5},{8,10},{9,11},{10,... | collective-permute-start | bytes 786440 | tf_op jit(solution)/shard_map/ppermute | solution.py:516
  180.6 5.5 %collective-permute-start.19 = (bf16[1024,128]{1,0:T(8,128)(2,1)}, bf16[1024,128]{1,0:T(8,128)(2,1)}, u32[]{:S(2)}, u32[]{:S(2)}) collective-permute-start(bf16[1024,128]{1,0:T(8,128)(2,1)} %collective-permute-done.12.refs_4_), channel_id=1, source_target_pairs={{0,1},{1,0},{2,3},{3,2},{4,5},{5,4},{6,7},{7,6},{8,9},{9,8},{10,11... | collective-permute-start | bytes 786440 | tf_op jit(solution)/shard_map/ppermute | solution.py:516
  180.6 5.5 %collective-permute-start.20 = (bf16[1024,128]{1,0:T(8,128)(2,1)}, bf16[1024,128]{1,0:T(8,128)(2,1)}, u32[]{:S(2)}, u32[]{:S(2)}) collective-permute-start(bf16[1024,128]{1,0:T(8,128)(2,1)} %collective-permute-done.13.refs_5_), channel_id=1, source_target_pairs={{0,1},{1,0},{2,3},{3,2},{4,5},{5,4},{6,7},{7,6},{8,9},{9,8},{10,11... | collective-permute-start | bytes 786440 | tf_op jit(solution)/shard_map/ppermute | solution.py:516
  181.1 0.7 copy-start.14
  181.8 4.3 %collective-permute-start.21 = (bf16[1024,128]{1,0:T(8,128)(2,1)}, bf16[1024,128]{1,0:T(8,128)(2,1)}, u32[]{:S(2)}, u32[]{:S(2)}) collective-permute-start(bf16[1024,128]{1,0:T(8,128)(2,1)} %collective-permute-done.14.refs_6_), channel_id=1, source_target_pairs={{0,1},{1,0},{2,3},{3,2},{4,5},{5,4},{6,7},{7,6},{8,9},{9,8},{10,11... | collective-permute-start | bytes 786440 | tf_op jit(solution)/shard_map/ppermute | solution.py:516
  183.9 2.2 %collective-permute-start.24 = (bf16[1024,128]{1,0:T(8,128)(2,1)}, bf16[1024,128]{1,0:T(8,128)(2,1)}, u32[]{:S(2)}, u32[]{:S(2)}) collective-permute-start(bf16[1024,128]{1,0:T(8,128)(2,1)} %collective-permute-done.17.refs_9_), channel_id=1, source_target_pairs={{0,1},{1,0},{2,3},{3,2},{4,5},{5,4},{6,7},{7,6},{8,9},{9,8},{10,11... | collective-permute-start | bytes 786440 | tf_op jit(solution)/shard_map/ppermute | solution.py:516
  186.1 1.9 collective-permute-start.23
  188.0 1.0 copy-start.15

commit v4 on v3

--- a/solution.py
+++ b/solution.py
@@ -19,7 +19,7 @@
 COARSE = 2048
 UNROLL = 32
 ACCS = 4
-CHUNKS = 1
+EARLY = 128
 
 
 def nbytes(x):
@@ -199,9 +199,9 @@
     return pre, place.reshape(-1)
 
 
-def edge_message(pre, edges, ghosts, senders, places, w_in, w_out, gain, level, rows, slots):
+def edge_message(pre, edges, ghosts, halo, senders, places, w_in, w_out, gain, level, rows, slots):
     count, width = pre.shape
-    ghost_rows = ghosts.shape[0]
+    ghost_rows = ghosts.shape[0] * halo
     fourth = slots // 4
     n = 256
     total = count // n
@@ -239,7 +239,8 @@
             column = jnp.concatenate(columns, axis=0)
             lane = lax.broadcasted_iota(jnp.int32, (n, ghost_rows), 1).astype(F32)
             pick = (column == lane).astype(BF)
-            picked = dot(pick, ghost_late.ref[...]).astype(BF)
+            border = ghost_late.ref[:, 0:halo, :].reshape(ghost_rows, width)
+            picked = dot(pick, border).astype(BF)
             first = pre_late.ref[pl.ds(at, n), :] + (dot(picked, w_s) + dot(edge_late.ref[pl.ds(at, n), :], w_e))
             msg[...] = norm(dot(silu(first).astype(BF), w_o), scale)
 
@@ -288,29 +289,37 @@
         + [shaped(slots, F32)] * ACCS
         + [pltpu.SemaphoreType.DMA((4,))],
         (pl.BlockSpec(memory_space=pl.ANY),) * 4,
-        level == 0,
+        True,
     )(places, senders.reshape(-1, 128), w_in, w_out, gain, pre, edges, ghosts)
 
 
-def node_update(rows, kept, first, second, w_in, w_out, gain, level):
+def node_update(rows, kept, first, second, w_in, w_out, gain, level, copies=1):
     count, width = rows.shape
     n = chunk(count, 704)
-
-    def kernel(rows_ref, kept_ref, first_ref, second_ref, w_ref, wo_ref, gain_ref, out_ref):
+    assert copies == 1 or n == count
+    head = 0 if copies == 1 else EARLY
+    tail = n - head
+
+    def kernel(rows_ref, kept_ref, first_ref, second_ref, w_ref, wo_ref, gain_ref, out_ref, *head_ref):
         own = rows_ref[...]
         total = (kept_ref[...] + first_ref[...].astype(F32) + second_ref[...].astype(F32)).astype(BF)
         hidden = silu(dot(own, w_ref[level, 0:width, :]) + dot(total, w_ref[level, width : 2 * width, :])).astype(BF)
         result = norm(dot(hidden, wo_ref[level]), gain_ref[level : level + 1, :])
-        out_ref[...] = (own.astype(F32) + result).astype(BF)
+        value = (own.astype(F32) + result).astype(BF)
+        for ref in head_ref:
+            ref[...] = value[:head]
+        for k in range(copies):
+            out_ref[k * tail : (k + 1) * tail, :] = value[head:]
 
     block = pl.BlockSpec((n, width), lambda i: (i, 0))
     return pl.pallas_call(
         kernel,
         grid=(count // n,),
-        out_shape=shaped(count, BF),
+        out_shape=[shaped(copies * (count - head), BF)] + [shaped(head, BF)] * (head > 0),
         in_specs=[block] * 4
         + [pl.BlockSpec(x.shape, lambda i, d=x.ndim: (0,) * d) for x in (w_in, w_out, gain)],
-        out_specs=block,
+        out_specs=[pl.BlockSpec((copies * tail, width), lambda i: (i, 0))]
+        + [pl.BlockSpec((head, width), lambda i: (i, 0))] * (head > 0),
         name="node_update",
         compiler_params=pltpu.CompilerParams(vmem_limit_bytes=FULL if level == 0 else 8 * 1024 * 1024),
     )(rows, kept, first, second, w_in, w_out, gain)
@@ -516,19 +525,21 @@
     return lax.ppermute(x, "edge", [(i, i ^ bit) for i in range(size)])
 
 
-def layer_sums(nodes, edges, senders, receivers, border, level, w, slots, table):
+def layer_sums(nodes, edges, senders, receivers, border, level, w, slots, table, extra=None):
     rows, width = nodes.shape
-    outgoing = nodes[border[0].reshape(-1)].reshape(border.shape[1], border.shape[2], width)
+    n_dom, halo = border.shape[1:]
+    outgoing = nodes[border[0].reshape(-1)].reshape(n_dom, halo, width)
+    if extra is not None:
+        outgoing = jnp.concatenate([outgoing, extra], axis=1)
     arrived = lax.all_to_all(outgoing, "dom", split_axis=0, concat_axis=0, tiled=True)
-    ghosts = arrived.reshape(-1, width)
-    pre, places = edge_gather(nodes, senders, receivers, table, w[0], level, ghosts.shape[0])
+    pre, places = edge_gather(nodes, senders, receivers, table, w[0], level, n_dom * halo)
     if table is None:
         me = lax.axis_index("edge")
         quarter = rows // 4
         places = order_of((receivers // quarter) ^ me) * quarter + receivers % quarter
-    k0, k2, s1, s3 = edge_message(pre, edges, ghosts, senders, places, w[0], w[1], w[4], level, rows, slots)
+    k0, k2, s1, s3 = edge_message(pre, edges, arrived, halo, senders, places, w[0], w[1], w[4], level, rows, slots)
     second = swap((k2 + swap(s3, 1).astype(F32)).astype(BF), 2)
-    return k0, swap(s1, 1), second
+    return k0, swap(s1, 1), second, arrived
 
 
 def order_of(rel):
@@ -561,7 +572,7 @@
     span = pool_send.shape[2]
     part = span // 4
     me = lax.axis_index("edge")
-    direct = n_dom == 8
+    direct = n_dom == 8 and span % 128 == 0 and fine_halo.shape[2] % 16 == 0
     room = -(-(fine_nodes.shape[0] // 4 + n_dom) // 64) * 64
     slot_place, base = layout(unpool_slot, me, n_dom, span, room)
 
@@ -572,43 +583,49 @@
     counts = child_count(pool_dest[0].reshape(-1))
     scale = jnp.maximum(counts, 1.0)[:, None]
 
-    kept, first, second = layer_sums(
-        fine_nodes, fine_edges, fine_senders, fine_receivers, fine_halo, 0, w, 4 * room, slot_place
+    extra = None
+    if direct:
+        lists = pool_dest[0].reshape(n_dom, span // 128, 128)
+        digit = [(lists >> 7).astype(BF), (lists & 127).astype(BF)]
+        extra = jnp.concatenate(digit + [jnp.zeros((n_dom, -2 * (span // 128) % 16, 128), BF)], axis=1)
+    kept, first, second, arrived_lists = layer_sums(
+        fine_nodes, fine_edges, fine_senders, fine_receivers, fine_halo, 0, w, 4 * room, slot_place, extra
     )
     sends, kept = lax.optimization_barrier((pool_send, kept))
     own = packed_rows(fine_nodes, own_quarter(sends), base, room)
-    mid = node_update(own, kept, first, second, w[2], w[3], w[5], 0)
+    (mid,) = node_update(own, kept, first, second, w[2], w[3], w[5], 0)
     if direct:
         mid_x = swap(mid, 2)
     spread = expand(mid, base, part)
     arrived = lax.all_to_all(spread.reshape(n_dom, part, width), "dom", split_axis=0, concat_axis=0, tiled=True)
+    if direct:
+        lists, _ = lax.optimization_barrier((arrived_lists, spread))
+        n = span // 128
+        digit = lists[:, fine_halo.shape[2] : fine_halo.shape[2] + 2 * n].astype(jnp.int32)
+        known = (digit[:, :n] * 128 + digit[:, n:]).reshape(-1, span)
+        parent = resolve(place_of(known), unpool_slot)
+        my_dest, parent = lax.optimization_barrier((my_dest, parent))
     bit = me & 1
     half = COARSE // 2
     mine, theirs = pool_sum(arrived.reshape(-1, width), my_dest, bit)
     mine = mine + swap(theirs, 1)
-    half_sum = mine.astype(BF)
-    if direct:
-        lists, half_sum = lax.optimization_barrier((pool_dest[0], half_sum))
-    other = swap(half_sum, 2)
-    if direct:
-        known = lax.all_to_all(lists, "dom", 0, 0, tiled=True)
-    mine = mine + other.astype(F32)
+    mine = mine + swap(mine.astype(BF), 2).astype(F32)
     mine = (mine / lax.dynamic_slice_in_dim(scale, bit * half, half, 0)).astype(BF)
     if direct:
-        mine, mid, mid_1, mid_3, known = lax.optimization_barrier((mine, mid, swap(mid, 1), swap(mid_x, 1), known))
+        mine, mid, mid_1, mid_3 = lax.optimization_barrier((mine, mid, swap(mid, 1), swap(mid_x, 1)))
     theirs = swap(mine, 1)
     coarse_in = jnp.concatenate([jnp.where(bit == 0, mine, theirs), jnp.where(bit == 0, theirs, mine)], axis=0)
 
-    kept, first, second = layer_sums(
+    kept, first, second, _ = layer_sums(
         coarse_in, coarse_edges, coarse_senders, coarse_receivers, coarse_halo, 1, w, COARSE, None
     )
     fourth = COARSE // 4
     own = lax.dynamic_slice_in_dim(coarse_in, me * fourth, fourth, 0)
-    top = node_update(own, kept, first, second, w[2], w[3], w[5], 1)
+    top = node_update(own, kept, first, second, w[2], w[3], w[5], 1, 4 if direct else 1)
     if direct:
-        return spread_out(top, [mid, mid_x, mid_1, mid_3], slot_place, known, unpool_slot)
-
-    coarse_out = lax.all_gather(top, "edge", axis=0, tiled=True)
+        return spread_out(top, [mid, mid_x, mid_1, mid_3], slot_place, parent)
+
+    coarse_out = lax.all_gather(top[0], "edge", axis=0, tiled=True)
     parents = take_rows([coarse_out], jnp.minimum(my_dest, COARSE - 1))
     back = lax.all_to_all(parents.reshape(n_dom, part, width), "dom", split_axis=0, concat_axis=0, tiled=True)
     final = (spread.astype(F32) + back.reshape(-1, width).astype(F32)).astype(BF)
@@ -619,23 +636,30 @@
     return (fine_out, coarse_out)
 
 
-def spot_of(rel, dy, z, row):
-    fourth = COARSE // 4
-    size = fourth // CHUNKS
-    return (rel & 1) * (16 * fourth) + (row // size) * (16 * size) + ((rel >> 1) * 2 + dy) * (4 * size) + z * size + row % size
+def late_spot(rel, dy, z, row):
+    size = COARSE // 4 - EARLY
+    return (rel & 1) * (4 * COARSE) + ((rel >> 1) * 2 + dy) * (4 * size) + z * size + row - EARLY
+
+
+def early_spot(rel, dy, z, row):
+    here = lax.axis_index("dom") >> 1
+    size = COARSE // 4 - EARLY
+    return (rel & 1) * (4 * COARSE) + 16 * size + ((here - z) & 3) * (4 * EARLY) + ((rel >> 1) * 2 + dy) * EARLY + row
 
 
 def place_of(known):
     me = lax.axis_index("edge")
     here = lax.axis_index("dom")
     fourth = COARSE // 4
-    owner = jnp.arange(known.shape[0], dtype=jnp.int32).reshape((-1,) + (1,) * (known.ndim - 1))
-    return spot_of((known // fourth) ^ me, (owner ^ here) & 1, owner >> 1, known % fourth).reshape(-1)
-
-
-def spread_out(top, mids, slot_place, known, unpool_slot):
-    fourth, width = top.shape
-    size = fourth // CHUNKS
+    owner = jnp.arange(known.shape[0], dtype=jnp.int32)[:, None]
+    at = ((known // fourth) ^ me, (owner ^ here) & 1, owner >> 1, known % fourth)
+    return jnp.where(at[3] < EARLY, early_spot(*at), late_spot(*at)).reshape(-1)
+
+
+def spread_out(top, mids, slot_place, parent):
+    late, early = top
+    width = early.shape[1]
+    size = late.shape[0] // 4
     me = lax.axis_index("edge")
     here = lax.axis_index("dom")
     groups = [[0, 2, 4, 6], [1, 3, 5, 7]]
@@ -643,58 +667,74 @@
     def cross(x):
         return lax.ppermute(x, "dom", [(i, i ^ 1) for i in range(8)])
 
-    slot_place, known, _ = lax.optimization_barrier((slot_place, known, top))
-    parent = resolve(place_of(known), unpool_slot)
+    def over_x(x):
+        return swap(x, 2)
+
+    early_y = cross(early)
+    early_x = over_x(early)
+    line = lax.all_to_all(
+        late.reshape(4, size, width), "dom", 0, 0, tiled=True, axis_index_groups=groups
+    ).reshape(4 * size, width)
+    square = jnp.concatenate([early, early_y, early_x, over_x(early_y)], axis=0)
+    slot_place, _ = lax.optimization_barrier((slot_place, late))
     mid_rows = take_rows(mids, slot_place)
-    lines = []
-    for h in range(CHUNKS):
-        copies = jnp.broadcast_to(top[None, h * size : (h + 1) * size], (4, size, width))
-        line = lax.all_to_all(copies, "dom", 0, 0, tiled=True, axis_index_groups=groups)
-        lines.append(line.reshape(4 * size, width))
-    lines[-1], mid_rows, parent = lax.optimization_barrier((lines[-1], mid_rows, parent))
-    pieces = []
-    for line in lines:
-        low, high = line[: 2 * size], line[2 * size :]
-        low_y = cross(low)
-        high_x = swap(high, 2)
-        high_y = cross(high)
-        low_x = swap(low, 2)
-        pieces += [line, low_y, high_y, low_x, high_x, swap(low_y, 2), cross(high_x)]
-    pieces = pieces + [swap(x, 1) for x in pieces]
-    row = jnp.arange(CHUNKS, dtype=jnp.int32)[None, :] * size
-    rel = jnp.arange(4, dtype=jnp.int32)[:, None] ^ me
-    starts = spot_of(rel, 0, here >> 1, row).reshape(-1)
-    return unpool(pieces, mid_rows, parent, starts, size)
-
-
-def unpool(pieces, mid_rows, parent, starts, size):
+    line, square, mid_rows = lax.optimization_barrier((line, square, mid_rows))
+    low, high = line[: 2 * size], line[2 * size :]
+    low_y, high_x = cross(low), over_x(high)
+    squares = [square]
+    for k in range(1, 4):
+        squares.append(lax.ppermute(square, "dom", [(i, (i + 2 * k) % 8) for i in range(8)]))
+    high_y, low_x = cross(high), over_x(low)
+    corner_x, corner_y = over_x(low_y), cross(high_x)
+    partner_x = swap(corner_x, 1)
+    partner_y = swap(corner_y, 1)
+    first = [line, low_y, high_y, low_x, high_x]
+    pieces = first + [corner_x, corner_y] + squares
+    pieces += [swap(x, 1) for x in first] + [partner_x, partner_y, swap(square, 1)]
+    for x in squares[1:]:
+        pieces.append(swap(x, 1))
+    rel = jnp.arange(4, dtype=jnp.int32) ^ me
+    starts = jnp.concatenate([early_spot(rel, 0, here >> 1, 0), late_spot(rel, 0, here >> 1, EARLY)])
+    return unpool(pieces, mid_rows, parent, starts)
+
+
+def unpool(pieces, mid_rows, parent, starts):
     count, _ = mid_rows.shape
     total = sum(x.shape[0] for x in pieces)
 
-    def kernel(parent_late, starts_late, mid_ref, *refs):
+    def kernel(parent_late, starts_late, *refs):
+        mid_late, refs = refs[-8], refs[:-8] + refs[-7:]
         refs, (out_ref, coarse_ref, wide, picked, stage, stage_c, sems) = refs[:-7], refs[-7:]
         start = 0
         for ref in refs:
 
-            def widen(at, ref=ref, start=start):
+            ref.wait()
+
+            def widen(at, ref=ref.ref, start=start):
                 wide[pl.ds(start + at, 256), :] = ref[pl.ds(at, 256), :].astype(F32)
 
-            blocks(ref.shape[0], 256, widen)
-            start += ref.shape[0]
+            blocks(ref.ref.shape[0], 256, widen)
+            start += ref.ref.shape[0]
         starts_late.wait()
-        for k in range(COARSE // size):
-            rows = wide[pl.ds(pl.multiple_of(starts_late.ref[k], size), size), :]
-            stage_c[k * size : (k + 1) * size, :] = rows.astype(BF)
+        fourth = COARSE // 4
+        for k in range(8):
+            first, rows = ((k & 3) * fourth, EARLY) if k < 4 else ((k & 3) * fourth + EARLY, fourth - EARLY)
+            found = wide[pl.ds(pl.multiple_of(starts_late.ref[k], 128), rows), :]
+            stage_c[first : first + rows, :] = found.astype(BF)
         copies = [pltpu.make_async_copy(stage_c, coarse_ref, sems.at[parent_late.pieces])]
         copies[0].start()
 
         def gather(j):
             picked[pl.ds(j, 1), :] = wide[pl.ds(parent_late.ref[j], 1), :]
 
+        assert mid_late.pieces == parent_late.pieces
+
         def flush(k, rows):
+            mid_late.copies[k].wait()
+
             def narrow(at):
                 spot = pl.ds(k * rows + at, 256)
-                stage[spot, :] = (picked[spot, :] + mid_ref[spot, :].astype(F32)).astype(BF)
+                stage[spot, :] = (picked[spot, :] + mid_late.ref[spot, :].astype(F32)).astype(BF)
 
             blocks(rows, 256, narrow)
             spot = pl.ds(k * rows, rows)
@@ -708,7 +748,7 @@
     return call(
         kernel,
         (shaped(count, BF), shaped(COARSE, BF)),
-        [INDEX, INDEX, VMEM] + [VMEM] * len(pieces),
+        [INDEX, INDEX] + [LOAD] * len(pieces) + [LOAD],
         [
             shaped(total, F32),
             shaped(count, F32),
@@ -717,7 +757,8 @@
             pltpu.SemaphoreType.DMA((pieces_of(parent, INDEX) + 1,)),
         ],
         (pl.BlockSpec(memory_space=pl.ANY), pl.BlockSpec(memory_space=pl.ANY)),
-    )(parent, starts, mid_rows, *pieces)
+        True,
+    )(parent, starts, *pieces, mid_rows)
 
 
 def solution(mesh):

time: 202 us -> 208 us (1.030)
  starting transfers between devices: 37.4 us -> 41.6 us
  other arithmetic: 6.75 us -> 10.4 us
  local copies, waits for them, and re-layouts: 21.6 us -> 19.4 us
    ppermute x0 -> x3, waiting for transfers between devices: none -> 9.47 us  [spread_out(): lax.ppermute(square, 'dom', [(i, (i + 2 * k) % 8) for i in range(8)])]
    all_to_all x2 -> x1, waiting for transfers between devices: 4.94 us -> 0.01 us  [spread_out(): lax.all_to_all(late.reshape(4, size, width), 'dom', 0, 0, tiled=True, axi...]
    ppermute x0 -> x3, starting transfers between devices: none -> 4.9 us  [spread_out(): lax.ppermute(square, 'dom', [(i, (i + 2 * k) % 8) for i in range(8)])]
    all_to_all x1, waiting for transfers between devices: 18 us -> 13.4 us  [shards(): lax.all_to_all(spread.reshape(n_dom, part, width), 'dom', split_axis=0, c...]
    ppermute x22 -> x28, starting transfers between devices: 11.2 us -> 14.8 us  [swap(): return lax.ppermute(x, 'edge', [(i, i ^ bit) for i in range(size)])]
    all_to_all x2 -> x1, starting transfers between devices: 6.97 us -> 3.46 us  [spread_out(): lax.all_to_all(late.reshape(4, size, width), 'dom', 0, 0, tiled=True, axi...]
    ppermute x3 -> x4, waiting for transfers between devices: 7.82 us -> 11.2 us  [cross(): return lax.ppermute(x, 'dom', [(i, i ^ 1) for i in range(8)])]
    ppermute x22 -> x28, waiting for transfers between devices: 23.5 us -> 20.6 us  [swap(): return lax.ppermute(x, 'edge', [(i, i ^ bit) for i in range(size)])]
  transfers between devices with their start and end apart: 30 -> 39, of which waited for: 15 -> 16; matrix products, arithmetic and copies ran while one was open for 6% -> 7% of each run, Pallas kernels for 18% -> 17%
where the time goes in v4:
time: 208 us; the launch traced here: 207 us
  Pallas kernels  75 us (36%)
  waiting for transfers between devices  57.5 us (28%)
  starting transfers between devices  41.6 us (20%)
  local copies, waits for them, and re-layouts  19.4 us (9%)
  other arithmetic  10.4 us (5%)
    pallas_call x10, Pallas kernels, run(): pl.pallas_call(body, out_shape=out_shape, in_specs=[HBM if spec in LATE e...  68.4 us
    ppermute x28, waiting for transfers between devices, swap(): return lax.ppermute(x, 'edge', [(i, i ^ bit) for i in range(size)])  20.6 us
    ppermute x28, starting transfers between devices, swap(): return lax.ppermute(x, 'edge', [(i, i ^ bit) for i in range(size)])  14.8 us
    all_to_all x1, waiting for transfers between devices, shards(): lax.all_to_all(spread.reshape(n_dom, part, width), 'dom', split_axis=0, c...  13.4 us
    ppermute x4, waiting for transfers between devices, cross(): return lax.ppermute(x, 'dom', [(i, i ^ 1) for i in range(8)])  11.2 us
    all_to_all x2, starting transfers between devices, layer_sums(): lax.all_to_all(outgoing, 'dom', split_axis=0, concat_axis=0, tiled=True)  10.8 us
    unnamed x95, local copies, waits for them, and re-layouts  9.99 us
    ppermute x3, waiting for transfers between devices, spread_out(): lax.ppermute(square, 'dom', [(i, (i + 2 * k) % 8) for i in range(8)])  9.47 us
  transfers between devices with their start and end apart: 39, of which 16 were waited for; matrix products, arithmetic and copies ran while one was open for 7% of the time, Pallas kernels for 17%

profile of v4, /device:TPU:0, one launch (start us, length us, event | category | flops | bytes accessed | tf_op | source)
XLA Modules:
  0.0 207.3 jit_solution(2122775252383803033)
XLA Ops:
  0.6 0.8 reshape_squeeze.17
  1.4 0.8 fusion.11
  2.4 2.9 %gather_fusion = bf16[512,128]{1,0:T(8,128)(2,1)S(1)} fusion(bf16[8192,128]{1,0:T(8,128)(2,1)} %refs_2_.7, s32[1024]{0:T(1024)S(1)} %pad_clamp_fusion.1), kind=kCustom, calls=%fused_computation | custom fusion | bytes 264192 | tf_op jit(solution)/shard_map/gather | solution.py:531
  5.3 0.8 maximum_maximum_fusion
  6.1 7.3 %all-to-all-start = ((bf16[8,96,128]{2,1,0:T(8,128)(2,1)}), bf16[8,96,128]{2,1,0:T(8,128)(2,1)S(1)}, u32[]{:S(2)}, u32[]{:S(2)}) async-start(bf16[8,96,128]{2,1,0:T(8,128)(2,1)} %maximum_maximum_fusion), calls=%async_computation | async-start | bytes 393216 | tf_op jit(solution)/shard_map/all_to_all | solution.py:534
  13.4 0.8 layout.1
  14.8 12.0 %shard_map.185 = (f32[4096,128]{1,0:T(8,128)}, s32[32,128]{1,0:T(8,128)}) custom-call(s32[4096]{0:T(1024)} %refs_0_.2, s32[4096]{0:T(1024)} %refs_1_.2, bf16[2,384,128]{2,1,0:T(8,128)(2,1)} %refs_2_.9, bf16[8192,128]{1,0:T(8,128)(2,1)} %refs_2_.7, s32[64,128]{1,0:T(8,128)} %copy-done.10, s32[32,128]{1,0:T(8,128)} %bitcast.43), custom_call_target="tpu_custom_call" | custom-call | tf_op jit(solution)/shard_map/pallas_call | solution.py:81
  26.8 0.7 copy-done.19
  27.5 14.7 %shard_map.186 = (f32[2112,128]{1,0:T(8,128)}, f32[2112,128]{1,0:T(8,128)}, bf16[2112,128]{1,0:T(8,128)(2,1)}, bf16[2112,128]{1,0:T(8,128)(2,1)}) custom-call(s32[4096]{0:T(1024)} %bitcast.45, s32[32,128]{1,0:T(8,128)} %bitcast.44, bf16[2,384,128]{2,1,0:T(8,128)(2,1)} %refs_2_.9, bf16[2,128,128]{2,1,0:T(8,128)(2,1)} %refs_3_.5, f32[2,128]{1,0:T(2,128)} %refs_4_.3, ...), custom_call_target="tpu_custom_call" | custom-call | tf_op jit(solution)/shard_map/pallas_call | solution.py:81
  42.8 1.6 collective-permute-done.1
  44.4 2.3 %add_convert_fusion = bf16[2112,128]{1,0:T(8,128)(2,1)} fusion(f32[2112,128]{1,0:T(8,128)} %get-tuple-element.39, bf16[2112,128]{1,0:T(8,128)(2,1)S(1)} %collective-permute-done.1), kind=kLoop, calls=%fused_computation.7 | loop fusion | flops 811008 | bytes 2162688 | tf_op jit(solution)/shard_map/convert_element_type | solution.py:541
  46.7 1.5 collective-permute-start.2
  48.5 1.2 copy.24
  49.6 2.2 %constant_dynamic-slice_fusion = (s32[8,384,1]{0,2,1:T(1,128)S(1)}, s32[8,384,1]{0,2,1:T(1,128)}) fusion(s32[8,384,4]{0,2,1:T(4,128)} %bitcast.41, s32[]{:T(128)S(6)} %select_n.91, s32[8,384,4]{0,2,1:T(4,128)S(1)} %bitcast.40), kind=kLoop, calls=%fused_computation.61 | loop fusion | bytes 49156 | tf_op jit(solution)/shard_map/jit(dynamic_index_in_dim)/dynamic_slice | solution.py:580
  51.9 3.8 %shard_map.187.rows_ref = bf16[2112,128]{1,0:T(8,128)(2,1)S(1)} custom-call(s32[8]{0:T(128)S(1)} %get-tuple-element.31.refs_0_, s32[3072]{0:T(1024)S(1)} %reshape.212.refs_1_, bf16[8192,128]{1,0:T(8,128)(2,1)S(1)} %copy-done), custom_call_target="tpu_custom_call" | custom-call | tf_op jit(solution)/shard_map/pallas_call | solution.py:81
  55.7 0.8 copy-done.5
  56.5 4.8 %collective-permute-done.2.second_ref = bf16[2112,128]{1,0:T(8,128)(2,1)} collective-permute-done((bf16[2112,128]{1,0:T(8,128)(2,1)}, bf16[2112,128]{1,0:T(8,128)(2,1)}, u32[]{:S(2)}, u32[]{:S(2)}) %collective-permute-start.2) | collective-permute-done | bytes 540704 | tf_op jit(solution)/shard_map/ppermute | solution.py:525
  61.3 4.5 %node_update.2.refs_1_ = bf16[2112,128]{1,0:T(8,128)(2,1)} custom-call(bf16[2112,128]{1,0:T(8,128)(2,1)} %copy-done.5, f32[2112,128]{1,0:T(8,128)} %get-tuple-element.37.kept_ref, bf16[2112,128]{1,0:T(8,128)(2,1)} %collective-permute-done.first_ref, bf16[2112,128]{1,0:T(8,128)(2,1)} %collective-permute-done.2.second_ref, bf16[2,256,128]{2,1,0:T(8,128)(2,1)} %w_ref.3, ...), custom_call_target="tpu_custom_call" | custom-call | tf_op jit(solution)/shard_map/node_update/pallas_call | solution.py:315
  65.8 1.0 copy-done.2
  66.9 1.5 shard_map.188
  68.4 6.0 %all-to-all-start.1 = ((bf16[8,384,128]{2,1,0:T(8,128)(2,1)}), bf16[8,384,128]{2,1,0:T(8,128)(2,1)S(1)}, u32[]{:S(2)}, u32[]{:S(2)}) async-start(bf16[8,384,128]{2,1,0:T(8,128)(2,1)} %bitcast.13), calls=%async_computation.1 | async-start | bytes 1572864 | tf_op jit(solution)/shard_map/all_to_all | solution.py:600
  75.0 1.6 collective-permute-start.6
  76.6 0.8 slice_convert_fusion
  77.5 2.5 %shard_map.189 = s32[64,128]{1,0:T(8,128)S(1)} custom-call(s32[96,128]{1,0:T(8,128)S(1)} %add_select_fusion.4.refs_0_, s32[64,128]{1,0:T(8,128)S(1)} %bitcast.34), custom_call_target="tpu_custom_call" | custom-call | tf_op jit(solution)/shard_map/pallas_call | solution.py:81
  80.7 13.4 %all-to-all-done.1 = bf16[8,384,128]{2,1,0:T(8,128)(2,1)S(1)} async-done(((bf16[8,384,128]{2,1,0:T(8,128)(2,1)}), bf16[8,384,128]{2,1,0:T(8,128)(2,1)S(1)}, u32[]{:S(2)}, u32[]{:S(2)}) %all-to-all-start.1) | async-done | bytes 786464 | tf_op jit(solution)/shard_map/all_to_all | solution.py:600
  94.1 5.4 %shard_map.190 = (f32[1024,128]{1,0:T(8,128)S(1)}, f32[1024,128]{1,0:T(8,128)}) custom-call(s32[1]{0:T(128)} %bitcast.12.refs_0_, bf16[3072,128]{1,0:T(8,128)(2,1)S(1)} %bitcast.30, s32[1,3072]{1,0:T(1,128)S(1)} %bitcast.35), custom_call_target="tpu_custom_call" | custom-call | tf_op jit(solution)/shard_map/pallas_call | solution.py:81
  100.2 1.5 collective-permute-done.3
  101.7 0.8 copy-done.21
  102.5 1.8 fusion.21
  104.3 1.5 collective-permute-start.4
  105.9 1.8 fusion.3
  107.8 5.1 %collective-permute-done.4 = bf16[1024,128]{1,0:T(8,128)(2,1)S(1)} collective-permute-done((bf16[1024,128]{1,0:T(8,128)(2,1)}, bf16[1024,128]{1,0:T(8,128)(2,1)S(1)}, u32[]{:S(2)}, u32[]{:S(2)}) %collective-permute-start.4) | collective-permute-done | bytes 262176 | tf_op jit(solution)/shard_map/ppermute | solution.py:525
  113.2 1.5 collective-permute-done.8
  114.7 0.7 copy-done.18
  115.5 1.5 gather_fusion.1
  117.0 3.5 %all-to-all-start.2 = ((bf16[8,32,128]{2,1,0:T(8,128)(2,1)}), bf16[8,32,128]{2,1,0:T(8,128)(2,1)S(1)}, u32[]{:S(2)}, u32[]{:S(2)}) async-start(bf16[8,32,128]{2,1,0:T(8,128)(2,1)} %bitcast.19), calls=%async_computation.2 | async-start | bytes 131072 | tf_op jit(solution)/shard_map/all_to_all | solution.py:534
  121.1 2.6 %shard_map.191.refs_5_ = f32[1024,128]{1,0:T(8,128)S(1)} custom-call(s32[1024]{0:T(1024)S(1)} %copy-done.14, s32[1024]{0:T(1024)S(1)} %copy-done.15, bf16[2,384,128]{2,1,0:T(8,128)(2,1)S(1)} %copy-done.4, bf16[2048,128]{1,0:T(8,128)(2,1)S(1)} %pad_maximum_fusion.refs_3_), custom_call_target="tpu_custom_call" | custom-call | tf_op jit(solution)/shard_map/pallas_call | solution.py:81
  123.8 0.8 copy-done.6
  124.6 2.8 %all-to-all-done.2.refs_7_ = bf16[8,32,128]{2,1,0:T(8,128)(2,1)S(1)} async-done(((bf16[8,32,128]{2,1,0:T(8,128)(2,1)}), bf16[8,32,128]{2,1,0:T(8,128)(2,1)S(1)}, u32[]{:S(2)}, u32[]{:S(2)}) %all-to-all-start.2) | async-done | bytes 65568 | tf_op jit(solution)/shard_map/all_to_all | solution.py:534
  128.0 5.4 %shard_map.192 = (f32[512,128]{1,0:T(8,128)}, f32[512,128]{1,0:T(8,128)}, bf16[512,128]{1,0:T(8,128)(2,1)}, bf16[512,128]{1,0:T(8,128)(2,1)}) custom-call(s32[1024]{0:T(1024)} %fusion.14.refs_0_, s32[8,128]{1,0:T(8,128)} %bitcast.36, bf16[2,384,128]{2,1,0:T(8,128)(2,1)} %refs_2_.9, bf16[2,128,128]{2,1,0:T(8,128)(2,1)} %refs_3_.5, f32[2,128]{1,0:T(2,128)} %refs_4_.3, ...), custom_call_target="tpu_custom_call" | custom-call | tf_op jit(solution)/shard_map/pallas_call | solution.py:81
  134.0 1.0 collective-permute-done.10
  135.0 1.0 add_convert_fusion.1
  136.0 1.6 collective-permute-start.11
  137.6 1.2 fusion.5.rows_ref
  138.7 2.9 %collective-permute-done.11.second_ref = bf16[512,128]{1,0:T(8,128)(2,1)S(1)} collective-permute-done((bf16[512,128]{1,0:T(8,128)(2,1)S(1)}, bf16[512,128]{1,0:T(8,128)(2,1)S(1)}, u32[]{:S(2)}, u32[]{:S(2)}) %collective-permute-start.11) | collective-permute-done | bytes 131104 | tf_op jit(solution)/shard_map/ppermute | solution.py:525
  141.6 0.9 copy-done.8
  142.6 1.3 node_update.3
  143.9 3.5 %all-to-all-start.3 = ((bf16[4,384,128]{2,1,0:T(8,128)(2,1)}), bf16[4,384,128]{2,1,0:T(8,128)(2,1)S(1)}, u32[]{:S(2)}, u32[]{:S(2)}) async-start(bf16[4,384,128]{2,1,0:T(8,128)(2,1)} %bitcast.20), calls=%async_computation.3 | async-start | bytes 786432 | tf_op jit(solution)/shard_map/all_to_all | solution.py:675
  147.8 1.5 collective-permute-start.13
  149.3 2.0 collective-permute-done.12
  151.3 1.5 collective-permute-start.14
  152.8 8.6 %shard_map.193.refs_24_ = bf16[8192,128]{1,0:T(8,128)(2,1)S(1)} custom-call(s32[8192]{0:T(1024)S(1)} %bitcast.31, bf16[2112,128]{1,0:T(8,128)(2,1)S(1)} %copy-done.3, bf16[2112,128]{1,0:T(8,128)(2,1)S(1)} %collective-permute-done.6.refs_2_, bf16[2112,128]{1,0:T(8,128)(2,1)S(1)} %collective-permute-done.5.refs_3_, ...), custom_call_target="tpu_custom_call" | custom-call | tf_op jit(solution)/shard_map/pallas_call | solution.py:81
  161.4 1.3 copy-done.1
  162.9 3.8 %collective-permute-start.23 = (bf16[512,128]{1,0:T(8,128)(2,1)S(1)}, bf16[512,128]{1,0:T(8,128)(2,1)S(1)}, u32[]{:S(2)}, u32[]{:S(2)}) collective-permute-start(bf16[512,128]{1,0:T(8,128)(2,1)S(1)} %pad_maximum_fusion.1.refs_9_), channel_id=1, source_target_pairs={{0,24},{4,28},{8,0},{12,4},{16,8},{20,12},{24,16},{28,20},{1,25},{... | collective-permute-start | bytes 393224 | tf_op jit(solution)/shard_map/ppermute | solution.py:686
  167.7 1.1 collective-permute-start.21
  168.8 1.8 collective-permute-done.23.refs_12_
  171.1 7.6 %collective-permute-done.22.refs_11_ = bf16[512,128]{1,0:T(8,128)(2,1)S(1)} collective-permute-done((bf16[512,128]{1,0:T(8,128)(2,1)S(1)}, bf16[512,128]{1,0:T(8,128)(2,1)S(1)}, u32[]{:S(2)}, u32[]{:S(2)}) %collective-permute-start.22) | collective-permute-done | bytes 131104 | tf_op jit(solution)/shard_map/ppermute | solution.py:686
  180.2 5.0 %collective-permute-done.15.refs_3_ = bf16[768,128]{1,0:T(8,128)(2,1)S(1)} collective-permute-done((bf16[768,128]{1,0:T(8,128)(2,1)S(1)}, bf16[768,128]{1,0:T(8,128)(2,1)S(1)}, u32[]{:S(2)}, u32[]{:S(2)}) %collective-permute-start.15) | collective-permute-done | bytes 196640 | tf_op jit(solution)/shard_map/ppermute | solution.py:668
  186.7 4.2 %collective-permute-done.20.refs_8_ = bf16[768,128]{1,0:T(8,128)(2,1)S(1)} collective-permute-done((bf16[768,128]{1,0:T(8,128)(2,1)S(1)}, bf16[768,128]{1,0:T(8,128)(2,1)S(1)}, u32[]{:S(2)}, u32[]{:S(2)}) %collective-permute-start.20) | collective-permute-done | bytes 196640 | tf_op jit(solution)/shard_map/ppermute | solution.py:668
  191.4 1.4 collective-permute-done.19.refs_7_
  192.9 0.7 pad_add_fusion.refs_1_
  193.6 0.7 collective-permute-done.29.refs_18_
  194.5 0.7 copy-done.37
  195.2 11.9 %shard_map.194 = (bf16[8192,128]{1,0:T(8,128)(2,1)}, bf16[2048,128]{1,0:T(8,128)(2,1)}) custom-call(s32[8192]{0:T(1024)} %bitcast.32, s32[8]{0:T(128)} %pad_add_fusion.refs_1_, bf16[1536,128]{1,0:T(8,128)(2,1)} %bitcast.39, bf16[768,128]{1,0:T(8,128)(2,1)} %copy-done.29, bf16[768,128]{1,0:T(8,128)(2,1)} %copy-done.27, bf16[768,128]{1,0:T(8,128)(2,1)} %copy-done.28, ...), custom_call_target="tpu_custom_call" | custom-call | tf_op jit(solution)/shard_map/pallas_call | solution.py:81
  (171 shorter events, 11.6 us)
Async XLA Ops:
  0.6 12.7 %copy-start.13 = (s32[8192]{0:T(1024)S(1)}, s32[8192]{0:T(1024)}, u32[]{:S(2)}) copy-start(s32[8192]{0:T(1024)} %param.29) | copy-start | bytes 98308
  6.1 20.7 %all-to-all-start = ((bf16[8,96,128]{2,1,0:T(8,128)(2,1)}), bf16[8,96,128]{2,1,0:T(8,128)(2,1)S(1)}, u32[]{:S(2)}, u32[]{:S(2)}) async-start(bf16[8,96,128]{2,1,0:T(8,128)(2,1)} %maximum_maximum_fusion), calls=%async_computation | async-start | bytes 393216 | tf_op jit(solution)/shard_map/all_to_all | solution.py:534
  27.5 20.7 %copy-start.23 = (s32[1,8,1536]{2,1,0:T(8,128)S(1)}, s32[1,8,1536]{2,1,0:T(8,128)}, u32[]{:S(2)}) copy-start(s32[1,8,1536]{2,1,0:T(8,128)} %param.28) | copy-start | bytes 147460
  42.2 6.3 %copy-start.45 = (s32[1,8,1536]{2,1,0:T(8,128)S(1)}, s32[1,8,1536]{2,1,0:T(8,128)}, u32[]{:S(2)}) copy-start(s32[1,8,1536]{2,1,0:T(8,128)} %param.27) | copy-start | bytes 147460
  42.2 2.2 %collective-permute-start.1 = (bf16[2112,128]{1,0:T(8,128)(2,1)}, bf16[2112,128]{1,0:T(8,128)(2,1)S(1)}, u32[]{:S(2)}, u32[]{:S(2)}) collective-permute-start(bf16[2112,128]{1,0:T(8,128)(2,1)} %get-tuple-element.40), channel_id=1, source_target_pairs={{0,1},{1,0},{2,3},{3,2},{4,5},{5,4},{6,7},{7,6},{8,9},{9,8},{10,11... | collective-permute-start | bytes 1622024 | tf_op jit(solution)/shard_map/ppermute | solution.py:525
  42.3 14.2 %collective-permute-start = (bf16[2112,128]{1,0:T(8,128)(2,1)}, bf16[2112,128]{1,0:T(8,128)(2,1)}, u32[]{:S(2)}, u32[]{:S(2)}) collective-permute-start(bf16[2112,128]{1,0:T(8,128)(2,1)} %get-tuple-element.38), channel_id=1, source_target_pairs={{0,1},{1,0},{2,3},{3,2},{4,5},{5,4},{6,7},{7,6},{8,9},{9,8},{10,11... | collective-permute-start | bytes 1622024 | tf_op jit(solution)/shard_map/ppermute | solution.py:525
  44.4 7.5 %copy-start = (bf16[8192,128]{1,0:T(8,128)(2,1)S(1)}, bf16[8192,128]{1,0:T(8,128)(2,1)}, u32[]{:S(2)}) copy-start(bf16[8192,128]{1,0:T(8,128)(2,1)} %refs_2_.7) | copy-start | bytes 6291460
  46.7 14.6 %collective-permute-start.2 = (bf16[2112,128]{1,0:T(8,128)(2,1)}, bf16[2112,128]{1,0:T(8,128)(2,1)}, u32[]{:S(2)}, u32[]{:S(2)}) collective-permute-start(bf16[2112,128]{1,0:T(8,128)(2,1)} %add_convert_fusion), channel_id=1, source_target_pairs={{0,2},{1,3},{2,0},{3,1},{4,6},{5,7},{6,4},{7,5},{8,10},{9,11},{10,... | collective-permute-start | bytes 1622024 | tf_op jit(solution)/shard_map/ppermute | solution.py:525
  66.9 8.1 %copy-start.20 = (s32[8,384,1]{0,2,1:T(1,128)S(1)}, s32[8,384,1]{0,2,1:T(1,128)}, u32[]{:S(2)}) copy-start(s32[8,384,1]{0,2,1:T(1,128)} %get-tuple-element.73) | copy-start | bytes 36868
  66.9 8.1 %copy-start.3 = (bf16[2112,128]{1,0:T(8,128)(2,1)S(1)}, bf16[2112,128]{1,0:T(8,128)(2,1)}, u32[]{:S(2)}) copy-start(bf16[2112,128]{1,0:T(8,128)(2,1)} %node_update.2.refs_1_) | copy-start | bytes 1622020
  68.4 25.7 %all-to-all-start.1 = ((bf16[8,384,128]{2,1,0:T(8,128)(2,1)}), bf16[8,384,128]{2,1,0:T(8,128)(2,1)S(1)}, u32[]{:S(2)}, u32[]{:S(2)}) async-start(bf16[8,384,128]{2,1,0:T(8,128)(2,1)} %bitcast.13), calls=%async_computation.1 | async-start | bytes 1572864 | tf_op jit(solution)/shard_map/all_to_all | solution.py:600
  74.4 31.5 %copy-start.46 = (s32[1,8,32]{2,1,0:T(8,128)S(1)}, s32[1,8,32]{2,1,0:T(8,128)}, u32[]{:S(2)}) copy-start(s32[1,8,32]{2,1,0:T(8,128)} %param.26) | copy-start | bytes 3076
  75.0 25.1 %collective-permute-start.6 = (bf16[2112,128]{1,0:T(8,128)(2,1)S(1)}, bf16[2112,128]{1,0:T(8,128)(2,1)S(1)}, u32[]{:S(2)}, u32[]{:S(2)}) collective-permute-start(bf16[2112,128]{1,0:T(8,128)(2,1)S(1)} %copy-done.3), channel_id=1, source_target_pairs={{0,2},{1,3},{2,0},{3,1},{4,6},{5,7},{6,4},{7,5},{8,10},{9,11},{10,... | collective-permute-start | bytes 1622024 | tf_op jit(solution)/shard_map/ppermute | solution.py:525
  99.5 2.2 %collective-permute-start.3 = (f32[1024,128]{1,0:T(8,128)}, f32[1024,128]{1,0:T(8,128)S(1)}, u32[]{:S(2)}, u32[]{:S(2)}) collective-permute-start(f32[1024,128]{1,0:T(8,128)} %get-tuple-element.45), channel_id=1, source_target_pairs={{0,1},{1,0},{2,3},{3,2},{4,5},{5,4},{6,7},{7,6},{8,9},{9,8},{10,11... | collective-permute-start | bytes 1572872 | tf_op jit(solution)/shard_map/ppermute | solution.py:525
  99.6 13.5 %collective-permute-start.5 = (bf16[2112,128]{1,0:T(8,128)(2,1)S(1)}, bf16[2112,128]{1,0:T(8,128)(2,1)S(1)}, u32[]{:S(2)}, u32[]{:S(2)}) collective-permute-start(bf16[2112,128]{1,0:T(8,128)(2,1)S(1)} %copy-done.3), channel_id=1, source_target_pairs={{0,1},{1,0},{2,3},{3,2},{4,5},{5,4},{6,7},{7,6},{8,9},{9,8},{10,11... | collective-permute-start | bytes 1622024 | tf_op jit(solution)/shard_map/ppermute | solution.py:525
  100.1 13.0 %collective-permute-start.7 = (bf16[2112,128]{1,0:T(8,128)(2,1)S(1)}, bf16[2112,128]{1,0:T(8,128)(2,1)S(1)}, u32[]{:S(2)}, u32[]{:S(2)}) collective-permute-start(bf16[2112,128]{1,0:T(8,128)(2,1)S(1)} %collective-permute-done.6.refs_2_), channel_id=1, source_target_pairs={{0,1},{1,0},{2,3},{3,2},{4,5},{5,4},{6,7},{7,6},{8,9},{9,8},{10,11... | collective-permute-start | bytes 1622024 | tf_op jit(solution)/shard_map/ppermute | solution.py:525
  104.3 8.6 %collective-permute-start.4 = (bf16[1024,128]{1,0:T(8,128)(2,1)}, bf16[1024,128]{1,0:T(8,128)(2,1)S(1)}, u32[]{:S(2)}, u32[]{:S(2)}) collective-permute-start(bf16[1024,128]{1,0:T(8,128)(2,1)} %get-tuple-element.60), channel_id=1, source_target_pairs={{0,2},{1,3},{2,0},{3,1},{4,6},{5,7},{6,4},{7,5},{8,10},{9,11},{10,... | collective-permute-start | bytes 786440 | tf_op jit(solution)/shard_map/ppermute | solution.py:525
  107.7 12.8 %copy-start.15 = (s32[1024]{0:T(1024)S(1)}, s32[1024]{0:T(1024)}, u32[]{:S(2)}) copy-start(s32[1024]{0:T(1024)} %refs_1_.3) | copy-start | bytes 12292
  107.8 13.4 %copy-start.4 = (bf16[2,384,128]{2,1,0:T(8,128)(2,1)S(1)}, bf16[2,384,128]{2,1,0:T(8,128)(2,1)}, u32[]{:S(2)}) copy-start(bf16[2,384,128]{2,1,0:T(8,128)(2,1)} %refs_2_.9) | copy-start | bytes 589828
  107.8 13.4 %copy-start.14 = (s32[1024]{0:T(1024)S(1)}, s32[1024]{0:T(1024)}, u32[]{:S(2)}) copy-start(s32[1024]{0:T(1024)} %refs_0_.3) | copy-start | bytes 12292
  113.1 1.6 collective-permute-start.8
  115.5 26.1 %copy-start.7 = (bf16[2,256,128]{2,1,0:T(8,128)(2,1)S(1)}, bf16[2,256,128]{2,1,0:T(8,128)(2,1)}, u32[]{:S(2)}) copy-start(bf16[2,256,128]{2,1,0:T(8,128)(2,1)} %w_ref.3) | copy-start | bytes 393220
  115.5 26.1 %copy-start.9 = (bf16[2,128,128]{2,1,0:T(8,128)(2,1)S(1)}, bf16[2,128,128]{2,1,0:T(8,128)(2,1)}, u32[]{:S(2)}) copy-start(bf16[2,128,128]{2,1,0:T(8,128)(2,1)} %wo_ref.3) | copy-start | bytes 196612
  115.5 26.1 %copy-start.16 = (f32[2,128]{1,0:T(2,128)S(1)}, f32[2,128]{1,0:T(2,128)}, u32[]{:S(2)}) copy-start(f32[2,128]{1,0:T(2,128)} %gain_ref.3) | copy-start | bytes 3076
  117.0 10.4 %all-to-all-start.2 = ((bf16[8,32,128]{2,1,0:T(8,128)(2,1)}), bf16[8,32,128]{2,1,0:T(8,128)(2,1)S(1)}, u32[]{:S(2)}, u32[]{:S(2)}) async-start(bf16[8,32,128]{2,1,0:T(8,128)(2,1)} %bitcast.19), calls=%async_computation.2 | async-start | bytes 131072 | tf_op jit(solution)/shard_map/all_to_all | solution.py:534
  124.6 28.3 %copy-start.11 = (s32[64,128]{1,0:T(8,128)S(1)}, s32[64,128]{1,0:T(8,128)}, u32[]{:S(2)}) copy-start(s32[64,128]{1,0:T(8,128)} %copy-done.10) | copy-start | bytes 98308
  133.4 1.6 collective-permute-start.10
  133.5 5.3 %collective-permute-start.9 = (bf16[512,128]{1,0:T(8,128)(2,1)}, bf16[512,128]{1,0:T(8,128)(2,1)S(1)}, u32[]{:S(2)}, u32[]{:S(2)}) collective-permute-start(bf16[512,128]{1,0:T(8,128)(2,1)} %get-tuple-element.48), channel_id=1, source_target_pairs={{0,1},{1,0},{2,3},{3,2},{4,5},{5,4},{6,7},{7,6},{8,9},{9,8},{10,11... | collective-permute-start | bytes 393224 | tf_op jit(solution)/shard_map/ppermute | solution.py:525
  136.0 5.6 %collective-permute-start.11 = (bf16[512,128]{1,0:T(8,128)(2,1)S(1)}, bf16[512,128]{1,0:T(8,128)(2,1)S(1)}, u32[]{:S(2)}, u32[]{:S(2)}) collective-permute-start(bf16[512,128]{1,0:T(8,128)(2,1)S(1)} %add_convert_fusion.1), channel_id=1, source_target_pairs={{0,2},{1,3},{2,0},{3,1},{4,6},{5,7},{6,4},{7,5},{8,10},{9,11},{10,... | collective-permute-start | bytes 393224 | tf_op jit(solution)/shard_map/ppermute | solution.py:525
  143.9 18.9 %all-to-all-start.3 = ((bf16[4,384,128]{2,1,0:T(8,128)(2,1)}), bf16[4,384,128]{2,1,0:T(8,128)(2,1)S(1)}, u32[]{:S(2)}, u32[]{:S(2)}) async-start(bf16[4,384,128]{2,1,0:T(8,128)(2,1)} %bitcast.20), calls=%async_computation.3 | async-start | bytes 786432 | tf_op jit(solution)/shard_map/all_to_all | solution.py:675
  147.3 4.0 %collective-permute-start.12 = (bf16[128,128]{1,0:T(8,128)(2,1)S(1)}, bf16[128,128]{1,0:T(8,128)(2,1)S(1)}, u32[]{:S(2)}, u32[]{:S(2)}) collective-permute-start(bf16[128,128]{1,0:T(8,128)(2,1)S(1)} %get-tuple-element.52), channel_id=1, source_target_pairs={{0,4},{4,0},{8,12},{12,8},{16,20},{20,16},{24,28},{28,24},{1,5},{5... | collective-permute-start | bytes 98312 | tf_op jit(solution)/shard_map/ppermute | solution.py:668
  147.8 15.0 %collective-permute-start.13 = (bf16[128,128]{1,0:T(8,128)(2,1)S(1)}, bf16[128,128]{1,0:T(8,128)(2,1)S(1)}, u32[]{:S(2)}, u32[]{:S(2)}) collective-permute-start(bf16[128,128]{1,0:T(8,128)(2,1)S(1)} %get-tuple-element.52), channel_id=1, source_target_pairs={{0,2},{1,3},{2,0},{3,1},{4,6},{5,7},{6,4},{7,5},{8,10},{9,11},{10,... | collective-permute-start | bytes 98312 | tf_op jit(solution)/shard_map/ppermute | solution.py:525
  151.3 11.4 %collective-permute-start.14 = (bf16[128,128]{1,0:T(8,128)(2,1)S(1)}, bf16[128,128]{1,0:T(8,128)(2,1)S(1)}, u32[]{:S(2)}, u32[]{:S(2)}) collective-permute-start(bf16[128,128]{1,0:T(8,128)(2,1)S(1)} %collective-permute-done.12), channel_id=1, source_target_pairs={{0,2},{1,3},{2,0},{3,1},{4,6},{5,7},{6,4},{7,5},{8,10},{9,11},{10,... | collective-permute-start | bytes 98312 | tf_op jit(solution)/shard_map/ppermute | solution.py:525
  162.8 31.6 %copy-start.22 = (bf16[512,128]{1,0:T(8,128)(2,1)}, bf16[512,128]{1,0:T(8,128)(2,1)S(1)}, u32[]{:S(2)}) copy-start(bf16[512,128]{1,0:T(8,128)(2,1)S(1)} %pad_maximum_fusion.1.refs_9_) | copy-start | bytes 393220
  162.8 31.5 %copy-start.17 = (bf16[4,384,128]{2,1,0:T(8,128)(2,1)}, bf16[4,384,128]{2,1,0:T(8,128)(2,1)S(1)}, u32[]{:S(2)}) copy-start(bf16[4,384,128]{2,1,0:T(8,128)(2,1)S(1)} %all-to-all-done.3) | copy-start | bytes 1179652
  162.8 4.9 %collective-permute-start.31 = (bf16[512,128]{1,0:T(8,128)(2,1)S(1)}, bf16[512,128]{1,0:T(8,128)(2,1)S(1)}, u32[]{:S(2)}, u32[]{:S(2)}) collective-permute-start(bf16[512,128]{1,0:T(8,128)(2,1)S(1)} %pad_maximum_fusion.1.refs_9_), channel_id=1, source_target_pairs={{0,1},{1,0},{2,3},{3,2},{4,5},{5,4},{6,7},{7,6},{8,9},{9,8},{10,11... | collective-permute-start | bytes 393224 | tf_op jit(solution)/shard_map/ppermute | solution.py:525
  162.9 7.7 %collective-permute-start.23 = (bf16[512,128]{1,0:T(8,128)(2,1)S(1)}, bf16[512,128]{1,0:T(8,128)(2,1)S(1)}, u32[]{:S(2)}, u32[]{:S(2)}) collective-permute-start(bf16[512,128]{1,0:T(8,128)(2,1)S(1)} %pad_maximum_fusion.1.refs_9_), channel_id=1, source_target_pairs={{0,24},{4,28},{8,0},{12,4},{16,8},{20,12},{24,16},{28,20},{1,25},{... | collective-permute-start | bytes 393224 | tf_op jit(solution)/shard_map/ppermute | solution.py:686
  166.7 12.1 %collective-permute-start.22 = (bf16[512,128]{1,0:T(8,128)(2,1)S(1)}, bf16[512,128]{1,0:T(8,128)(2,1)S(1)}, u32[]{:S(2)}, u32[]{:S(2)}) collective-permute-start(bf16[512,128]{1,0:T(8,128)(2,1)S(1)} %pad_maximum_fusion.1.refs_9_), channel_id=1, source_target_pairs={{0,16},{4,20},{8,24},{12,28},{16,0},{20,4},{24,8},{28,12},{1,17},{... | collective-permute-start | bytes 393224 | tf_op jit(solution)/shard_map/ppermute | solution.py:686
  166.7 12.5 %collective-permute-start.18 = (bf16[768,128]{1,0:T(8,128)(2,1)S(1)}, bf16[768,128]{1,0:T(8,128)(2,1)S(1)}, u32[]{:S(2)}, u32[]{:S(2)}) collective-permute-start(bf16[768,128]{1,0:T(8,128)(2,1)S(1)} %get-tuple-element.64), channel_id=1, source_target_pairs={{0,2},{1,3},{2,0},{3,1},{4,6},{5,7},{6,4},{7,5},{8,10},{9,11},{10,... | collective-permute-start | bytes 589832 | tf_op jit(solution)/shard_map/ppermute | solution.py:525
  167.3 12.4 %collective-permute-start.16 = (bf16[768,128]{1,0:T(8,128)(2,1)S(1)}, bf16[768,128]{1,0:T(8,128)(2,1)S(1)}, u32[]{:S(2)}, u32[]{:S(2)}) collective-permute-start(bf16[768,128]{1,0:T(8,128)(2,1)S(1)} %get-tuple-element.64), channel_id=1, source_target_pairs={{0,4},{4,0},{8,12},{12,8},{16,20},{20,16},{24,28},{28,24},{1,5},{5... | collective-permute-start | bytes 589832 | tf_op jit(solution)/shard_map/ppermute | solution.py:668
  167.7 26.7 %copy-start.38 = (bf16[512,128]{1,0:T(8,128)(2,1)}, bf16[512,128]{1,0:T(8,128)(2,1)S(1)}, u32[]{:S(2)}) copy-start(bf16[512,128]{1,0:T(8,128)(2,1)S(1)} %collective-permute-done.31.refs_20_) | copy-start | bytes 393220
  167.7 11.5 %collective-permute-start.21 = (bf16[512,128]{1,0:T(8,128)(2,1)S(1)}, bf16[512,128]{1,0:T(8,128)(2,1)S(1)}, u32[]{:S(2)}, u32[]{:S(2)}) collective-permute-start(bf16[512,128]{1,0:T(8,128)(2,1)S(1)} %pad_maximum_fusion.1.refs_9_), channel_id=1, source_target_pairs={{0,8},{4,12},{8,16},{12,20},{16,24},{20,28},{24,0},{28,4},{1,9},{5... | collective-permute-start | bytes 393224 | tf_op jit(solution)/shard_map/ppermute | solution.py:686
  170.6 23.7 %copy-start.39 = (bf16[512,128]{1,0:T(8,128)(2,1)}, bf16[512,128]{1,0:T(8,128)(2,1)S(1)}, u32[]{:S(2)}) copy-start(bf16[512,128]{1,0:T(8,128)(2,1)S(1)} %collective-permute-done.23.refs_12_) | copy-start | bytes 393220
  170.6 9.1 %collective-permute-start.17 = (bf16[768,128]{1,0:T(8,128)(2,1)S(1)}, bf16[768,128]{1,0:T(8,128)(2,1)S(1)}, u32[]{:S(2)}, u32[]{:S(2)}) collective-permute-start(bf16[768,128]{1,0:T(8,128)(2,1)S(1)} %get-tuple-element.65), channel_id=1, source_target_pairs={{0,2},{1,3},{2,0},{3,1},{4,6},{5,7},{6,4},{7,5},{8,10},{9,11},{10,... | collective-permute-start | bytes 589832 | tf_op jit(solution)/shard_map/ppermute | solution.py:525
  178.7 15.6 %copy-start.40 = (bf16[512,128]{1,0:T(8,128)(2,1)}, bf16[512,128]{1,0:T(8,128)(2,1)S(1)}, u32[]{:S(2)}) copy-start(bf16[512,128]{1,0:T(8,128)(2,1)S(1)} %collective-permute-done.22.refs_11_) | copy-start | bytes 393220
  178.7 6.4 %collective-permute-start.15 = (bf16[768,128]{1,0:T(8,128)(2,1)S(1)}, bf16[768,128]{1,0:T(8,128)(2,1)S(1)}, u32[]{:S(2)}, u32[]{:S(2)}) collective-permute-start(bf16[768,128]{1,0:T(8,128)(2,1)S(1)} %get-tuple-element.65), channel_id=1, source_target_pairs={{0,4},{4,0},{8,12},{12,8},{16,20},{20,16},{24,28},{28,24},{1,5},{5... | collective-permute-start | bytes 589832 | tf_op jit(solution)/shard_map/ppermute | solution.py:668
  179.1 15.2 %copy-start.41 = (bf16[512,128]{1,0:T(8,128)(2,1)}, bf16[512,128]{1,0:T(8,128)(2,1)S(1)}, u32[]{:S(2)}) copy-start(bf16[512,128]{1,0:T(8,128)(2,1)S(1)} %collective-permute-done.21.refs_10_) | copy-start | bytes 393220
  179.1 6.4 %collective-permute-start.34 = (bf16[512,128]{1,0:T(8,128)(2,1)S(1)}, bf16[512,128]{1,0:T(8,128)(2,1)S(1)}, u32[]{:S(2)}, u32[]{:S(2)}) collective-permute-start(bf16[512,128]{1,0:T(8,128)(2,1)S(1)} %collective-permute-done.23.refs_12_), channel_id=1, source_target_pairs={{0,1},{1,0},{2,3},{3,2},{4,5},{5,4},{6,7},{7,6},{8,9},{9,8},{10,11... | collective-permute-start | bytes 393224 | tf_op jit(solution)/shard_map/ppermute | solution.py:525
  179.1 15.2 %copy-start.26 = (bf16[768,128]{1,0:T(8,128)(2,1)}, bf16[768,128]{1,0:T(8,128)(2,1)S(1)}, u32[]{:S(2)}) copy-start(bf16[768,128]{1,0:T(8,128)(2,1)S(1)} %collective-permute-done.18.refs_6_) | copy-start | bytes 589828
  179.2 6.4 %collective-permute-start.33 = (bf16[512,128]{1,0:T(8,128)(2,1)S(1)}, bf16[512,128]{1,0:T(8,128)(2,1)S(1)}, u32[]{:S(2)}, u32[]{:S(2)}) collective-permute-start(bf16[512,128]{1,0:T(8,128)(2,1)S(1)} %collective-permute-done.22.refs_11_), channel_id=1, source_target_pairs={{0,1},{1,0},{2,3},{3,2},{4,5},{5,4},{6,7},{7,6},{8,9},{9,8},{10,11... | collective-permute-start | bytes 393224 | tf_op jit(solution)/shard_map/ppermute | solution.py:525
  179.7 14.7 %copy-start.27 = (bf16[768,128]{1,0:T(8,128)(2,1)}, bf16[768,128]{1,0:T(8,128)(2,1)S(1)}, u32[]{:S(2)}) copy-start(bf16[768,128]{1,0:T(8,128)(2,1)S(1)} %collective-permute-done.16.refs_4_) | copy-start | bytes 589828
  179.7 6.5 %collective-permute-start.32 = (bf16[512,128]{1,0:T(8,128)(2,1)S(1)}, bf16[512,128]{1,0:T(8,128)(2,1)S(1)}, u32[]{:S(2)}, u32[]{:S(2)}) collective-permute-start(bf16[512,128]{1,0:T(8,128)(2,1)S(1)} %collective-permute-done.21.refs_10_), channel_id=1, source_target_pairs={{0,1},{1,0},{2,3},{3,2},{4,5},{5,4},{6,7},{7,6},{8,9},{9,8},{10,11... | collective-permute-start | bytes 393224 | tf_op jit(solution)/shard_map/ppermute | solution.py:525
  179.7 14.6 %copy-start.28 = (bf16[768,128]{1,0:T(8,128)(2,1)}, bf16[768,128]{1,0:T(8,128)(2,1)S(1)}, u32[]{:S(2)}) copy-start(bf16[768,128]{1,0:T(8,128)(2,1)S(1)} %collective-permute-done.17.refs_5_) | copy-start | bytes 589828
  179.7 6.6 %collective-permute-start.28 = (bf16[768,128]{1,0:T(8,128)(2,1)S(1)}, bf16[768,128]{1,0:T(8,128)(2,1)S(1)}, u32[]{:S(2)}, u32[]{:S(2)}) collective-permute-start(bf16[768,128]{1,0:T(8,128)(2,1)S(1)} %collective-permute-done.18.refs_6_), channel_id=1, source_target_pairs={{0,1},{1,0},{2,3},{3,2},{4,5},{5,4},{6,7},{7,6},{8,9},{9,8},{10,11... | collective-permute-start | bytes 589832 | tf_op jit(solution)/shard_map/ppermute | solution.py:525
  185.2 9.2 %copy-start.29 = (bf16[768,128]{1,0:T(8,128)(2,1)}, bf16[768,128]{1,0:T(8,128)(2,1)S(1)}, u32[]{:S(2)}) copy-start(bf16[768,128]{1,0:T(8,128)(2,1)S(1)} %collective-permute-done.15.refs_3_) | copy-start | bytes 589828
  185.2 5.7 %collective-permute-start.20 = (bf16[768,128]{1,0:T(8,128)(2,1)S(1)}, bf16[768,128]{1,0:T(8,128)(2,1)S(1)}, u32[]{:S(2)}, u32[]{:S(2)}) collective-permute-start(bf16[768,128]{1,0:T(8,128)(2,1)S(1)} %collective-permute-done.18.refs_6_), channel_id=1, source_target_pairs={{0,4},{4,0},{8,12},{12,8},{16,20},{20,16},{24,28},{28,24},{1,5},{5... | collective-permute-start | bytes 589832 | tf_op jit(solution)/shard_map/ppermute | solution.py:668
  185.6 5.3 %collective-permute-start.26 = (bf16[768,128]{1,0:T(8,128)(2,1)S(1)}, bf16[768,128]{1,0:T(8,128)(2,1)S(1)}, u32[]{:S(2)}, u32[]{:S(2)}) collective-permute-start(bf16[768,128]{1,0:T(8,128)(2,1)S(1)} %collective-permute-done.16.refs_4_), channel_id=1, source_target_pairs={{0,1},{1,0},{2,3},{3,2},{4,5},{5,4},{6,7},{7,6},{8,9},{9,8},{10,11... | collective-permute-start | bytes 589832 | tf_op jit(solution)/shard_map/ppermute | solution.py:525
  185.6 7.3 %collective-permute-start.19 = (bf16[768,128]{1,0:T(8,128)(2,1)S(1)}, bf16[768,128]{1,0:T(8,128)(2,1)S(1)}, u32[]{:S(2)}, u32[]{:S(2)}) collective-permute-start(bf16[768,128]{1,0:T(8,128)(2,1)S(1)} %collective-permute-done.15.refs_3_), channel_id=1, source_target_pairs={{0,2},{1,3},{2,0},{3,1},{4,6},{5,7},{6,4},{7,5},{8,10},{9,11},{10,... | collective-permute-start | bytes 589832 | tf_op jit(solution)/shard_map/ppermute | solution.py:525
  186.2 7.4 %collective-permute-start.24 = (bf16[1536,128]{1,0:T(8,128)(2,1)S(1)}, bf16[1536,128]{1,0:T(8,128)(2,1)S(1)}, u32[]{:S(2)}, u32[]{:S(2)}) collective-permute-start(bf16[1536,128]{1,0:T(8,128)(2,1)S(1)} %bitcast.38), channel_id=1, source_target_pairs={{0,1},{1,0},{2,3},{3,2},{4,5},{5,4},{6,7},{7,6},{8,9},{9,8},{10,11... | collective-permute-start | bytes 1179656 | tf_op jit(solution)/shard_map/ppermute | solution.py:525
  186.3 8.1 %copy-start.30 = (bf16[768,128]{1,0:T(8,128)(2,1)}, bf16[768,128]{1,0:T(8,128)(2,1)S(1)}, u32[]{:S(2)}) copy-start(bf16[768,128]{1,0:T(8,128)(2,1)S(1)} %collective-permute-done.28.refs_17_) | copy-start | bytes 589828
  186.3 7.2 %collective-permute-start.25 = (bf16[768,128]{1,0:T(8,128)(2,1)S(1)}, bf16[768,128]{1,0:T(8,128)(2,1)S(1)}, u32[]{:S(2)}, u32[]{:S(2)}) collective-permute-start(bf16[768,128]{1,0:T(8,128)(2,1)S(1)} %collective-permute-done.15.refs_3_), channel_id=1, source_target_pairs={{0,1},{1,0},{2,3},{3,2},{4,5},{5,4},{6,7},{7,6},{8,9},{9,8},{10,11... | collective-permute-start | bytes 589832 | tf_op jit(solution)/shard_map/ppermute | solution.py:525
  190.8 2.7 %collective-permute-start.27 = (bf16[768,128]{1,0:T(8,128)(2,1)S(1)}, bf16[768,128]{1,0:T(8,128)(2,1)S(1)}, u32[]{:S(2)}, u32[]{:S(2)}) collective-permute-start(bf16[768,128]{1,0:T(8,128)(2,1)S(1)} %collective-permute-done.17.refs_5_), channel_id=1, source_target_pairs={{0,1},{1,0},{2,3},{3,2},{4,5},{5,4},{6,7},{7,6},{8,9},{9,8},{10,11... | collective-permute-start | bytes 589832 | tf_op jit(solution)/shard_map/ppermute | solution.py:525
  190.9 2.7 %collective-permute-start.30 = (bf16[768,128]{1,0:T(8,128)(2,1)S(1)}, bf16[768,128]{1,0:T(8,128)(2,1)S(1)}, u32[]{:S(2)}, u32[]{:S(2)}) collective-permute-start(bf16[768,128]{1,0:T(8,128)(2,1)S(1)} %collective-permute-done.20.refs_8_), channel_id=1, source_target_pairs={{0,1},{1,0},{2,3},{3,2},{4,5},{5,4},{6,7},{7,6},{8,9},{9,8},{10,11... | collective-permute-start | bytes 589832 | tf_op jit(solution)/shard_map/ppermute | solution.py:525
  192.9 1.4 collective-permute-start.29
  (22 other events, 37.7 us)
